TPU v7x, 512 devices: a whole 4x4x16 slice. The times are simulated.
512 devices in a mesh: sx: 32 (over z, core), sy: 16 (over x, y).
Axes of the slice: x: 4, y: 4, z: 16, core: 2. Of those that a mesh axis runs over, the one named last changes fastest.
Arguments:
- features: bfloat16 [64, 512, 2048], P(None, 'sx', 'sy'), may hold values from -6 to 6
- enc_weight: bfloat16 [3, 3, 3, 64, 64], replicated, may hold values from -0.15625 to 0.15625
- enc_bias: float32 [64], replicated, may hold values from -3 to 3
- proj_weight: bfloat16 [64, 512], replicated, may hold values from -0.25 to 0.25
- bottle_weight: bfloat16 [3, 3, 3, 512, 512], P(None, None, None, 'sy'), may hold values from -0.0546875 to 0.0546875
- bottle_bias: float32 [512], P('sy'), may hold values from -3 to 3
- out_weight: bfloat16 [512, 64], P('sy'), may hold values from -0.25 to 0.25
- dec_weight: bfloat16 [3, 3, 3, 64, 64], replicated, may hold values from -0.15625 to 0.15625
- dec_bias: float32 [64], replicated, may hold values from -3 to 3
Outputs:
- decoded: bfloat16 [64, 512, 2048], P(None, 'sx', 'sy')
All inputs are finite; a program needn't handle non-finite values.
Results may differ from a plain program's by a relative error of at most 0.009.
Values may be sent and summed in bfloat16 or wider, within the bound.
No kernel may reach another device: no remote copies, remote signals or barrier semaphores. Data moves between devices by JAX's collectives and lax.ppermute only.
A program may use at most 64 MiB of HBM per device.

v0:
```python
import jax
import jax.numpy as jnp
from jax import lax
from jax.sharding import PartitionSpec as P

POOL = 8
FZ = 16


layout = ("NCDHW", "DHWOI", "NCDHW")


def padded_2(shard, sides, width):
    for axis, dim in sides:
        size, length = (lax.axis_size(axis), shard.shape[dim])
        up = [(i, (i + 1) % size) for i in range(size - 1)]
        down = [(j, i) for i, j in up]
        last = lax.slice_in_dim(shard, length - width, length, axis=dim)
        first = lax.slice_in_dim(shard, 0, width, axis=dim)
        before = lax.ppermute(last, axis, up)
        after = lax.ppermute(first, axis, down)
        shard = jnp.concatenate([before, shard, after], axis=dim)
    return shard


def copy_for_each(shard, axis):
    copies = jnp.broadcast_to(shard, (lax.axis_size(axis), *shard.shape))
    return lax.all_to_all(copies, axis, split_axis=0, concat_axis=0, tiled=True)


def laid_out(pieces, dim):
    pieces = jnp.moveaxis(pieces, 0, dim)
    shape = pieces.shape
    return pieces.reshape(*shape[:dim], shape[dim] * shape[dim + 1], *shape[dim + 2 :])


def collect(shard, axis, dim):
    pieces = copy_for_each(shard, axis)
    return laid_out(pieces, dim)


def of_everyone(shard, axis):
    everything = copy_for_each(shard, axis)
    return jnp.sum(everything, axis=0)


def convolve(padded, kernel, pad_x, pad_y):
    result = lax.conv_general_dilated(
        padded[None],
        kernel,
        (1, 1, 1),
        ((pad_x, pad_x), (pad_y, pad_y), (1, 1)),
        dimension_numbers=layout,
        preferred_element_type=jnp.float32,
    )
    return result[0]


def interpolate(fine_count, fine_first, coarse_count, coarse_first, coarse_total):
    fine_index = fine_first + jnp.arange(fine_count, dtype=jnp.int32)
    coarse_index = coarse_first + jnp.arange(coarse_count, dtype=jnp.int32)
    numerator = 2 * fine_index + 1 - POOL
    low_cell = jnp.floor_divide(numerator, 2 * POOL)
    weight_high = (numerator - 2 * POOL * low_cell).astype(jnp.float32) / jnp.float32(2 * POOL)
    weight_high = jnp.where(low_cell < 0, jnp.float32(0.0), weight_high)
    low_cell = jnp.maximum(low_cell, 0)
    weight_high = jnp.where(low_cell >= coarse_total - 1, jnp.float32(0.0), weight_high)
    low_cell = jnp.minimum(low_cell, coarse_total - 1)
    low_hit = (coarse_index[None, :] == low_cell[:, None]).astype(jnp.float32)
    high_hit = (coarse_index[None, :] == low_cell[:, None] + 1).astype(jnp.float32)
    return (1.0 - weight_high)[:, None] * low_hit + weight_high[:, None] * high_hit


def project(proj_weight, pooled):
    return jnp.einsum(
        "ck,cxyz->kxyz", proj_weight, pooled, preferred_element_type=jnp.float32
    ).astype(jnp.bfloat16)


def per_device(
    features,
    enc_weight,
    enc_bias,
    proj_weight,
    bottle_weight,
    bottle_bias,
    out_weight,
    dec_weight,
    dec_bias,
):
    channels, fine_x, merged = features.shape
    fine_z = FZ
    fine_y = merged // fine_z
    field = features.reshape(channels, fine_x, fine_y, fine_z)
    x_devices = lax.axis_size("sx")
    y_devices = lax.axis_size("sy")
    x_position = lax.axis_index("sx")
    y_position = lax.axis_index("sy")
    cells_x, cells_y, cells_z = (fine_x // POOL, fine_y // POOL, fine_z // POOL)
    extra = 1
    extended = padded_2(field, (("sx", 1), ("sy", 2)), extra + 1)
    encoded = jax.nn.relu(
        convolve(extended, enc_weight, 0, 0) + enc_bias[:, None, None, None]
    ).astype(jnp.bfloat16)
    own_part = encoded[:, extra : extra + fine_x, extra : extra + fine_y]
    pooled = jnp.max(
        own_part.reshape(channels, cells_x, POOL, cells_y, POOL, cells_z, POOL), axis=(2, 4, 6)
    )
    gathered = collect(pooled, "sy", 2)
    rimmed = padded_2(gathered, (("sx", 1),), 1)
    projected = project(proj_weight, rimmed)
    bottleneck = jax.nn.relu(
        convolve(projected, bottle_weight, 0, 1) + bottle_bias[:, None, None, None]
    ).astype(jnp.bfloat16)
    partial_value = jnp.einsum(
        "kc,kxyz->cxyz", out_weight, bottleneck, preferred_element_type=jnp.float32
    )
    summed = of_everyone(partial_value, "sy")
    lowres = padded_2(summed, (("sx", 1),), 1)
    y_first = 0
    y_count = summed.shape[2]
    along_x = interpolate(
        fine_x + 2 * extra,
        fine_x * x_position - extra,
        cells_x + 2,
        cells_x * x_position - 1,
        cells_x * x_devices,
    )
    along_y = interpolate(
        fine_y + 2 * extra, fine_y * y_position - extra, y_count, y_first, cells_y * y_devices
    )
    along_z = interpolate(fine_z, 0, cells_z, 0, cells_z)
    highest = lax.Precision.HIGHEST
    step_one = jnp.einsum("kabc,zc->kabz", lowres, along_z, precision=highest)
    step_two = jnp.einsum("kabz,yb->kayz", step_one, along_y, precision=highest)
    upsampled = jnp.einsum("kayz,xa->kxyz", step_two, along_x, precision=highest)
    joined = (encoded.astype(jnp.float32) + upsampled).astype(jnp.bfloat16)
    global_x = fine_x * x_position - 1 + jnp.arange(fine_x + 2, dtype=jnp.int32)
    global_y = fine_y * y_position - 1 + jnp.arange(fine_y + 2, dtype=jnp.int32)
    inside_x = (global_x >= 0) & (global_x < fine_x * x_devices)
    inside_y = (global_y >= 0) & (global_y < fine_y * y_devices)
    inside = inside_x[:, None] & inside_y[None, :]
    padded = jnp.where(inside[None, :, :, None], joined, jnp.zeros((), jnp.bfloat16))
    decoded = (convolve(padded, dec_weight, 0, 0) + dec_bias[:, None, None, None]).astype(
        jnp.bfloat16
    )
    return decoded.reshape(channels, fine_x, merged)


def solution(mesh):
    in_specs = (
        P(None, "sx", "sy"),
        P(),
        P(),
        P(),
        P(None, None, None, "sy", None),
        P("sy"),
        P("sy", None),
        P(),
        P(),
    )
    out_specs = P(None, "sx", "sy")
    return jax.shard_map(
        per_device, mesh=mesh, in_specs=in_specs, out_specs=out_specs, check_vma=False
    )
```

profile of v0, /device:TPU:97, one launch (start us, length us, event | category | flops | bytes accessed | tf_op | source)
XLA Modules:
  0.0 101.2 jit_solution(13830094049171249805)
XLA Ops:
  0.0 1.3 %copy.47 = bf16[64,16,128]{0,2,1:T(8,128)(2,1)S(1)} copy(bf16[64,16,128]{2,1,0:T(8,128)(2,1)} %param.9) | data formatting | bytes 524288 | tf_op args[0]
  1.4 5.3 %collective-permute-start = (bf16[64,2,8,16]{0,3,2,1:T(8,128)(2,1)S(1)}, bf16[64,2,8,16]{0,3,2,1:T(8,128)(2,1)S(1)}, u32[]{:S(2)}, u32[]{:S(2)}) collective-permute-start(bf16[64,2,8,16]{0,3,2,1:T(8,128)(2,1)S(1)} %get-tuple-element.7), channel_id=1, source_target_pairs={{0,16},{16,32},{32,48},{48,64},{64,80},{80,96},{96,112},{112,128},... | collective-permute-start | bytes 98312 | tf_op jit(solution)/shard_map/ppermute | solution.py:20
  6.7 1.9 %collective-permute-start.1 = (bf16[64,2,8,16]{0,3,2,1:T(8,128)(2,1)S(1)}, bf16[64,2,8,16]{0,3,2,1:T(8,128)(2,1)S(1)}, u32[]{:S(2)}, u32[]{:S(2)}) collective-permute-start(bf16[64,2,8,16]{0,3,2,1:T(8,128)(2,1)S(1)} %get-tuple-element.8), channel_id=1, source_target_pairs={{16,0},{32,16},{48,32},{64,48},{80,64},{96,80},{112,96},{128,112},... | collective-permute-start | bytes 98312 | tf_op jit(solution)/shard_map/ppermute | solution.py:21
  8.7 4.8 %collective-permute-done.1 = bf16[64,2,8,16]{0,3,2,1:T(8,128)(2,1)S(1)} collective-permute-done((bf16[64,2,8,16]{0,3,2,1:T(8,128)(2,1)S(1)}, bf16[64,2,8,16]{0,3,2,1:T(8,128)(2,1)S(1)}, u32[]{:S(2)}, u32[]{:S(2)}) %collective-permute-start.1) | collective-permute-done | bytes 32800 | tf_op jit(solution)/shard_map/ppermute | solution.py:21
  13.6 3.2 %collective-permute-start.2 = (bf16[64,20,2,16]{0,3,2,1:T(8,128)(2,1)S(1)}, bf16[64,20,2,16]{0,3,2,1:T(8,128)(2,1)S(1)}, u32[]{:S(2)}, u32[]{:S(2)}) collective-permute-start(bf16[64,20,2,16]{0,3,2,1:T(8,128)(2,1)S(1)} %get-tuple-element.5), channel_id=1, source_target_pairs={{0,1},{1,2},{2,3},{3,4},{4,5},{5,6},{6,7},{7,8},{8,9},{9,10},{10,1... | collective-permute-start | bytes 245768 | tf_op jit(solution)/shard_map/ppermute | solution.py:20
  16.8 1.3 %collective-permute-start.3 = (bf16[64,20,2,16]{0,3,2,1:T(8,128)(2,1)S(1)}, bf16[64,20,2,16]{0,3,2,1:T(8,128)(2,1)S(1)}, u32[]{:S(2)}, u32[]{:S(2)}) collective-permute-start(bf16[64,20,2,16]{0,3,2,1:T(8,128)(2,1)S(1)} %get-tuple-element.6), channel_id=1, source_target_pairs={{1,0},{2,1},{3,2},{4,3},{5,4},{6,5},{7,6},{8,7},{9,8},{10,9},{11,1... | collective-permute-start | bytes 245768 | tf_op jit(solution)/shard_map/ppermute | solution.py:21
  19.0 3.8 %collective-permute-done.3 = bf16[64,20,2,16]{0,3,2,1:T(8,128)(2,1)S(1)} collective-permute-done((bf16[64,20,2,16]{0,3,2,1:T(8,128)(2,1)S(1)}, bf16[64,20,2,16]{0,3,2,1:T(8,128)(2,1)S(1)}, u32[]{:S(2)}, u32[]{:S(2)}) %collective-permute-start.3) | collective-permute-done | bytes 81952 | tf_op jit(solution)/shard_map/ppermute | solution.py:21
  25.2 8.6 %fusion.20 = f32[18,10,8,3,64]{4,2,3,1,0:T(8,128)S(1)} fusion(bf16[3,3,3,64,64]{4,3,2,1,0:T(8,128)(2,1)S(1)} %copy-done.6, bf16[64,20,12,1,7,2]{0,4,5,2,1,3:T(8,128)(2,1)S(1)} %slice.42, bf16[64,20,12,1,8,3]{0,4,5,2,1,3:T(8,128)(2,1)S(1)} %copy.50, pred[8,3]{0,1:T(4,128)(4,1)S(1)} %copy-done.8), kind=kOutput, calls=%fused_computation.22 | convolution fusion | flops 959477760 | bytes 2494488 | tf_op jit(solution)/shard_map/conv_general_dilated | solution.py:48
  35.9 8.0 %all-to-all-start = ((bf16[16,2,128]{2,1,0:T(2,128)(2,1)}), bf16[16,2,128]{2,1,0:T(2,128)(2,1)S(1)}, u32[]{:S(2)}, u32[]{:S(2)}) async-start(bf16[16,2,128]{2,1,0:T(2,128)(2,1)} %reshape.213), calls=%async_computation | async-start | bytes 16384 | tf_op jit(solution)/shard_map/all_to_all | solution.py:28
  43.9 6.3 %all-to-all-done = bf16[16,2,128]{2,1,0:T(2,128)(2,1)S(1)} async-done(((bf16[16,2,128]{2,1,0:T(2,128)(2,1)}), bf16[16,2,128]{2,1,0:T(2,128)(2,1)S(1)}, u32[]{:S(2)}, u32[]{:S(2)}) %all-to-all-start) | async-done | bytes 8224 | tf_op jit(solution)/shard_map/all_to_all | solution.py:28
  50.3 6.1 %collective-permute-start.4 = (bf16[64,1,16,2]{0,2,3,1:T(8,128)(2,1)S(1)}, bf16[64,1,16,2]{0,2,3,1:T(8,128)(2,1)S(1)}, u32[]{:S(2)}, u32[]{:S(2)}) collective-permute-start(bf16[64,1,16,2]{0,2,3,1:T(8,128)(2,1)S(1)} %get-tuple-element.11), channel_id=1, source_target_pairs={{0,16},{16,32},{32,48},{48,64},{64,80},{80,96},{96,112},{112,128},... | collective-permute-start | bytes 12296 | tf_op jit(solution)/shard_map/ppermute | solution.py:20
  56.4 2.1 %collective-permute-start.5 = (bf16[64,1,16,2]{0,2,3,1:T(8,128)(2,1)S(1)}, bf16[64,1,16,2]{0,2,3,1:T(8,128)(2,1)S(1)}, u32[]{:S(2)}, u32[]{:S(2)}) collective-permute-start(bf16[64,1,16,2]{0,2,3,1:T(8,128)(2,1)S(1)} %get-tuple-element.12), channel_id=1, source_target_pairs={{16,0},{32,16},{48,32},{64,48},{80,64},{96,80},{112,96},{128,112},... | collective-permute-start | bytes 12296 | tf_op jit(solution)/shard_map/ppermute | solution.py:21
  58.5 4.0 %collective-permute-done.5 = bf16[64,1,16,2]{0,2,3,1:T(8,128)(2,1)S(1)} collective-permute-done((bf16[64,1,16,2]{0,2,3,1:T(8,128)(2,1)S(1)}, bf16[64,1,16,2]{0,2,3,1:T(8,128)(2,1)S(1)}, u32[]{:S(2)}, u32[]{:S(2)}) %collective-permute-start.5) | collective-permute-done | bytes 4128 | tf_op jit(solution)/shard_map/ppermute | solution.py:21
  62.8 2.0 %fusion.33 = f32[1,32,2,16,2]{1,0,4,3,2:T(1,128)S(1)} fusion(bf16[3,3,3,32,512]{4,3,2,1,0:T(8,128)(2,1)S(1)} %copy-done, bf16[1,512,4,16,2]{1,3,4,2,0:T(8,128)(2,1)S(1)} %fusion.29), kind=kOutput, calls=%fused_computation.38 | convolution fusion | flops 36175872 | bytes 1024000 | tf_op jit(solution)/shard_map/conv_general_dilated | solution.py:48
  64.9 1.0 %reshape.215 = f32[16,1,4096]{2,1,0:T(1,128)} reshape(f32[16,2,2,16,64]{4,3,2,1,0:T(8,128)S(1)} %broadcast_bitcast_fusion) | data formatting | bytes 524288
  66.0 3.5 %all-to-all-start.1 = ((f32[16,1,4096]{2,1,0:T(1,128)}), f32[16,1,4096]{2,1,0:T(1,128)S(1)}, u32[]{:S(2)}, u32[]{:S(2)}) async-start(f32[16,1,4096]{2,1,0:T(1,128)} %reshape.215), calls=%async_computation.1 | async-start | bytes 524288 | tf_op jit(solution)/shard_map/all_to_all | solution.py:28
  69.6 7.2 %all-to-all-done.1 = f32[16,1,4096]{2,1,0:T(1,128)S(1)} async-done(((f32[16,1,4096]{2,1,0:T(1,128)}), f32[16,1,4096]{2,1,0:T(1,128)S(1)}, u32[]{:S(2)}, u32[]{:S(2)}) %all-to-all-start.1) | async-done | bytes 262176 | tf_op jit(solution)/shard_map/all_to_all | solution.py:28
  77.3 1.3 %reduce.3 = f32[16,4096]{1,0:T(8,128)S(1)} reduce(f32[16,1,4096]{2,1,0:T(1,128)S(1)} %all-to-all-done.1, f32[]{:T(128)} %broadcast.955), dimensions={1}, to_apply=%all_to_all.7.reduce_sub_computation | reduce | bytes 524292 | tf_op jit(solution)/shard_map/all_to_all | solution.py:28
  78.9 3.1 %collective-permute-start.6 = (f32[64,1,16,2]{0,2,3,1:T(8,128)S(1)}, f32[64,1,16,2]{0,2,3,1:T(8,128)S(1)}, u32[]{:S(2)}, u32[]{:S(2)}) collective-permute-start(f32[64,1,16,2]{0,2,3,1:T(8,128)S(1)} %get-tuple-element.9), channel_id=1, source_target_pairs={{0,16},{16,32},{32,48},{48,64},{64,80},{80,96},{96,112},{112,128},... | collective-permute-start | bytes 24584 | tf_op jit(solution)/shard_map/ppermute | solution.py:20
  82.0 1.9 %collective-permute-start.7 = (f32[64,1,16,2]{0,2,3,1:T(8,128)S(1)}, f32[64,1,16,2]{0,2,3,1:T(8,128)S(1)}, u32[]{:S(2)}, u32[]{:S(2)}) collective-permute-start(f32[64,1,16,2]{0,2,3,1:T(8,128)S(1)} %get-tuple-element.10), channel_id=1, source_target_pairs={{16,0},{32,16},{48,32},{64,48},{80,64},{96,80},{112,96},{128,112},... | collective-permute-start | bytes 24584 | tf_op jit(solution)/shard_map/ppermute | solution.py:21
  83.9 4.3 %collective-permute-done.7 = f32[64,1,16,2]{0,2,3,1:T(8,128)S(1)} collective-permute-done((f32[64,1,16,2]{0,2,3,1:T(8,128)S(1)}, f32[64,1,16,2]{0,2,3,1:T(8,128)S(1)}, u32[]{:S(2)}, u32[]{:S(2)}) %collective-permute-start.7) | collective-permute-done | bytes 8224 | tf_op jit(solution)/shard_map/ppermute | solution.py:21
  89.6 2.1 %fusion.27 = bf16[64,18,10,1,16]{0,1,4,2,3:T(8,128)(2,1)S(1)} fusion(bf16[64,18,10,16]{0,1,3,2:T(8,128)(2,1)S(1)} %fusion.11, pred[18,10]{0,1:T(8,128)(4,1)S(1)} %broadcast_and_fusion, f32[64,4,10,16]{0,2,3,1:T(8,128)S(1)} %convolution_bitcast_fusion, f32[18]{0:T(128)S(1)} %get-tuple-element.13, s32[18]{0:T(128)S(1)} %get-tuple-element.16, ...), kind=kOutput, calls=%fused_computation.25 | convolution fusion | flops 9585000 | bytes 901604 | tf_op jit(solution)/shard_map/kayz,xa->kxyz/dot_general | solution.py:136
  93.0 6.1 %fusion.23 = f32[16,8,8,3,64]{4,2,3,1,0:T(8,128)S(1)} fusion(bf16[3,3,3,64,64]{4,3,2,1,0:T(8,128)(2,1)S(1)} %copy-done.7, bf16[64,18,10,1,7,2]{0,4,5,2,1,3:T(8,128)(2,1)S(1)} %slice.49, bf16[64,18,10,1,8,3]{0,4,5,2,1,3:T(8,128)(2,1)S(1)} %copy.61, pred[8,3]{0,1:T(4,128)(4,1)S(1)} %copy-done.8), kind=kOutput, calls=%fused_computation.23 | convolution fusion | flops 682438656 | bytes 1883160 | tf_op jit(solution)/shard_map/conv_general_dilated | solution.py:48
  100.2 1.0 copy.64
  (66 shorter events, 10.3 us)
Async XLA Ops:
  0.0 62.8 %copy-start = (bf16[3,3,3,32,512]{4,3,2,1,0:T(8,128)(2,1)S(1)}, bf16[3,3,3,32,512]{4,3,2,1,0:T(8,128)(2,1)}, u32[]{:S(2)}) copy-start(bf16[3,3,3,32,512]{4,3,2,1,0:T(8,128)(2,1)} %param.13) | copy-start | bytes 2654212
  1.4 7.4 %collective-permute-start = (bf16[64,2,8,16]{0,3,2,1:T(8,128)(2,1)S(1)}, bf16[64,2,8,16]{0,3,2,1:T(8,128)(2,1)S(1)}, u32[]{:S(2)}, u32[]{:S(2)}) collective-permute-start(bf16[64,2,8,16]{0,3,2,1:T(8,128)(2,1)S(1)} %get-tuple-element.7), channel_id=1, source_target_pairs={{0,16},{16,32},{32,48},{48,64},{64,80},{80,96},{96,112},{112,128},... | collective-permute-start | bytes 98312 | tf_op jit(solution)/shard_map/ppermute | solution.py:20
  6.7 6.8 %collective-permute-start.1 = (bf16[64,2,8,16]{0,3,2,1:T(8,128)(2,1)S(1)}, bf16[64,2,8,16]{0,3,2,1:T(8,128)(2,1)S(1)}, u32[]{:S(2)}, u32[]{:S(2)}) collective-permute-start(bf16[64,2,8,16]{0,3,2,1:T(8,128)(2,1)S(1)} %get-tuple-element.8), channel_id=1, source_target_pairs={{16,0},{32,16},{48,32},{64,48},{80,64},{96,80},{112,96},{128,112},... | collective-permute-start | bytes 98312 | tf_op jit(solution)/shard_map/ppermute | solution.py:21
  13.6 5.5 %collective-permute-start.2 = (bf16[64,20,2,16]{0,3,2,1:T(8,128)(2,1)S(1)}, bf16[64,20,2,16]{0,3,2,1:T(8,128)(2,1)S(1)}, u32[]{:S(2)}, u32[]{:S(2)}) collective-permute-start(bf16[64,20,2,16]{0,3,2,1:T(8,128)(2,1)S(1)} %get-tuple-element.5), channel_id=1, source_target_pairs={{0,1},{1,2},{2,3},{3,4},{4,5},{5,6},{6,7},{7,8},{8,9},{9,10},{10,1... | collective-permute-start | bytes 245768 | tf_op jit(solution)/shard_map/ppermute | solution.py:20
  16.8 6.1 %collective-permute-start.3 = (bf16[64,20,2,16]{0,3,2,1:T(8,128)(2,1)S(1)}, bf16[64,20,2,16]{0,3,2,1:T(8,128)(2,1)S(1)}, u32[]{:S(2)}, u32[]{:S(2)}) collective-permute-start(bf16[64,20,2,16]{0,3,2,1:T(8,128)(2,1)S(1)} %get-tuple-element.6), channel_id=1, source_target_pairs={{1,0},{2,1},{3,2},{4,3},{5,4},{6,5},{7,6},{8,7},{9,8},{10,9},{11,1... | collective-permute-start | bytes 245768 | tf_op jit(solution)/shard_map/ppermute | solution.py:21
  24.2 1.0 %copy-start.6 = (bf16[3,3,3,64,64]{4,3,2,1,0:T(8,128)(2,1)S(1)}, bf16[3,3,3,64,64]{4,3,2,1,0:T(8,128)(2,1)}, u32[]{:S(2)}) copy-start(bf16[3,3,3,64,64]{4,3,2,1,0:T(8,128)(2,1)} %param.10) | copy-start | bytes 663556
  24.2 1.0 copy-start.8
  33.8 0.8 copy-start.3
  34.6 28.0 %copy-start.1 = (bf16[64,512]{1,0:T(8,128)(2,1)S(1)}, bf16[64,512]{1,0:T(8,128)(2,1)}, u32[]{:S(2)}) copy-start(bf16[64,512]{1,0:T(8,128)(2,1)} %param.12) | copy-start | bytes 196612
  34.8 29.9 %copy-start.2 = (bf16[32,64]{1,0:T(8,128)(2,1)S(1)}, bf16[32,64]{1,0:T(8,128)(2,1)}, u32[]{:S(2)}) copy-start(bf16[32,64]{1,0:T(8,128)(2,1)} %param.15) | copy-start | bytes 12292
  34.9 29.9 %copy-start.4 = (f32[32]{0:T(128)S(1)}, f32[32]{0:T(128)}, u32[]{:S(2)}) copy-start(f32[32]{0:T(128)} %param.14) | copy-start | bytes 388
  35.9 14.3 %all-to-all-start = ((bf16[16,2,128]{2,1,0:T(2,128)(2,1)}), bf16[16,2,128]{2,1,0:T(2,128)(2,1)S(1)}, u32[]{:S(2)}, u32[]{:S(2)}) async-start(bf16[16,2,128]{2,1,0:T(2,128)(2,1)} %reshape.213), calls=%async_computation | async-start | bytes 16384 | tf_op jit(solution)/shard_map/all_to_all | solution.py:28
  50.3 8.2 %collective-permute-start.4 = (bf16[64,1,16,2]{0,2,3,1:T(8,128)(2,1)S(1)}, bf16[64,1,16,2]{0,2,3,1:T(8,128)(2,1)S(1)}, u32[]{:S(2)}, u32[]{:S(2)}) collective-permute-start(bf16[64,1,16,2]{0,2,3,1:T(8,128)(2,1)S(1)} %get-tuple-element.11), channel_id=1, source_target_pairs={{0,16},{16,32},{32,48},{48,64},{64,80},{80,96},{96,112},{112,128},... | collective-permute-start | bytes 12296 | tf_op jit(solution)/shard_map/ppermute | solution.py:20
  56.4 6.2 %collective-permute-start.5 = (bf16[64,1,16,2]{0,2,3,1:T(8,128)(2,1)S(1)}, bf16[64,1,16,2]{0,2,3,1:T(8,128)(2,1)S(1)}, u32[]{:S(2)}, u32[]{:S(2)}) collective-permute-start(bf16[64,1,16,2]{0,2,3,1:T(8,128)(2,1)S(1)} %get-tuple-element.12), channel_id=1, source_target_pairs={{16,0},{32,16},{48,32},{64,48},{80,64},{96,80},{112,96},{128,112},... | collective-permute-start | bytes 12296 | tf_op jit(solution)/shard_map/ppermute | solution.py:21
  66.0 10.8 %all-to-all-start.1 = ((f32[16,1,4096]{2,1,0:T(1,128)}), f32[16,1,4096]{2,1,0:T(1,128)S(1)}, u32[]{:S(2)}, u32[]{:S(2)}) async-start(f32[16,1,4096]{2,1,0:T(1,128)} %reshape.215), calls=%async_computation.1 | async-start | bytes 524288 | tf_op jit(solution)/shard_map/all_to_all | solution.py:28
  78.9 5.1 %collective-permute-start.6 = (f32[64,1,16,2]{0,2,3,1:T(8,128)S(1)}, f32[64,1,16,2]{0,2,3,1:T(8,128)S(1)}, u32[]{:S(2)}, u32[]{:S(2)}) collective-permute-start(f32[64,1,16,2]{0,2,3,1:T(8,128)S(1)} %get-tuple-element.9), channel_id=1, source_target_pairs={{0,16},{16,32},{32,48},{48,64},{64,80},{80,96},{96,112},{112,128},... | collective-permute-start | bytes 24584 | tf_op jit(solution)/shard_map/ppermute | solution.py:20
  82.0 6.3 %collective-permute-start.7 = (f32[64,1,16,2]{0,2,3,1:T(8,128)S(1)}, f32[64,1,16,2]{0,2,3,1:T(8,128)S(1)}, u32[]{:S(2)}, u32[]{:S(2)}) collective-permute-start(f32[64,1,16,2]{0,2,3,1:T(8,128)S(1)} %get-tuple-element.10), channel_id=1, source_target_pairs={{16,0},{32,16},{48,32},{64,48},{80,64},{96,80},{112,96},{128,112},... | collective-permute-start | bytes 24584 | tf_op jit(solution)/shard_map/ppermute | solution.py:21
  92.0 1.0 %copy-start.7 = (bf16[3,3,3,64,64]{4,3,2,1,0:T(8,128)(2,1)S(1)}, bf16[3,3,3,64,64]{4,3,2,1,0:T(8,128)(2,1)}, u32[]{:S(2)}) copy-start(bf16[3,3,3,64,64]{4,3,2,1,0:T(8,128)(2,1)} %param.16) | copy-start | bytes 663556
  99.4 0.7 copy-start.5
where the time goes:
time: 102 us; the launch traced here: 101 us
  starting transfers between devices  36.5 us (36%)
  waiting for transfers between devices  31.4 us (31%)
  matrix products  20.4 us (20%)
  local copies, waits for them, and re-layouts  9.96 us (10%)
  other arithmetic  2.45 us (2%)
    ppermute x4, starting transfers between devices, padded_2(): before = lax.ppermute(last, axis, up)  17.7 us
    ppermute x4, waiting for transfers between devices, padded_2(): after = lax.ppermute(first, axis, down)  17 us
    conv_general_dilated x3, matrix products, convolve(): lax.conv_general_dilated(padded[None], kernel, (1, 1, 1), ((pad_x, pad_x)...  16.7 us
    all_to_all x2, waiting for transfers between devices, copy_for_each(): return lax.all_to_all(copies, axis, split_axis=0, concat_axis=0, tiled=True)  13.5 us
    all_to_all x2, starting transfers between devices, copy_for_each(): return lax.all_to_all(copies, axis, split_axis=0, concat_axis=0, tiled=True)  11.5 us
    ppermute x4, starting transfers between devices, padded_2(): after = lax.ppermute(first, axis, down)  7.23 us
    unnamed x26, local copies, waits for them, and re-layouts  5.63 us
    conv_general_dilated x8, local copies, waits for them, and re-layouts, convolve(): lax.conv_general_dilated(padded[None], kernel, (1, 1, 1), ((pad_x, pad_x)...  2.12 us
  transfers between devices with their start and end apart: 10, of which 7 were waited for; matrix products, arithmetic and copies ran while one was open for 0% of the time, Pallas kernels for 0%

commit v1 on v0

v1 whole, which is shorter than its diff:
```python
import jax
import jax.numpy as jnp
from jax import lax
from jax.experimental import pallas as pl
from jax.experimental.pallas import tpu as pltpu
from jax.sharding import PartitionSpec as P

F32 = jnp.float32
BF = jnp.bfloat16
C = 64
NSX = 32
NSY = 16
VM = pl.BlockSpec(memory_space=pltpu.VMEM)


def call(kernel, outs, *ins, name, scratch=(), flops=1000000, limit=16):
    return pl.pallas_call(
        kernel,
        out_shape=outs,
        in_specs=[VM] * len(ins),
        out_specs=jax.tree.map(lambda _: VM, outs),
        scratch_shapes=list(scratch),
        name=name,
        compiler_params=pltpu.CompilerParams(vmem_limit_bytes=limit * 2**20),
        cost_estimate=pl.CostEstimate(flops=flops, transcendentals=0, bytes_accessed=100000),
    )(*ins)


def S(shape, dtype):
    return jax.ShapeDtypeStruct(shape, dtype)


def dot(a, b):
    return jnp.dot(a, b, preferred_element_type=F32)


def dot_nt(a, b):
    return lax.dot_general(a, b, (((1,), (1,)), ((), ())), preferred_element_type=F32)


def lanes_of(rows):
    return lax.broadcasted_iota(jnp.int32, (rows, 128), 1)


def roll(v, shift):
    shift = shift % 128
    return v if shift == 0 else pltpu.roll(v, shift, 1)


def k_features(x_ref, ft_ref, lo_ref, hi_ref, buf):
    buf[...] = x_ref[...].reshape(C * 16, 128).astype(F32)
    for x in range(16):
        row = buf[pl.ds(x, C, stride=16), :].astype(BF)
        ft_ref[x] = row
        if x < 2:
            lo_ref[x] = row
        if x >= 14:
            hi_ref[x - 14] = row


def row_of(r, lo_ref, ft_ref, hi_ref):
    if r < 2:
        return lo_ref[r]
    if r < 18:
        return ft_ref[r - 2]
    return hi_ref[r - 18]


def k_faces(lo_ref, ft_ref, hi_ref, left_ref, right_ref):
    lane = lanes_of(C)
    for g in range(5):
        left = None
        for q in range(4):
            row = row_of(4 * g + q, lo_ref, ft_ref, hi_ref).astype(F32)
            a, b = roll(row, 32 * q), roll(row, 32 * q - 96)
            if q == 0:
                left, right = a, b
            else:
                here = lane >= 32 * q
                left, right = jnp.where(here, a, left), jnp.where(here, b, right)
        left_ref[g] = left.astype(BF)
        right_ref[g] = right.astype(BF)


def arranged(w_ref, out_ref):
    for a in range(3):
        for pair in range(5):
            blocks = [w_ref[a * 9 + t] for t in range(2 * pair, min(2 * pair + 2, 9))]
            wide = blocks[0] if len(blocks) == 1 else jnp.concatenate(blocks, axis=1)
            out_ref[pl.ds(a * C, C), pl.ds(128 * pair, wide.shape[1])] = wide


def column(b_ref):
    row = jnp.broadcast_to(b_ref[...], (C, C))
    same = lax.broadcasted_iota(jnp.int32, (C, C), 0) == lax.broadcasted_iota(jnp.int32, (C, C), 1)
    return jnp.broadcast_to(jnp.sum(jnp.where(same, row, 0.0), axis=1, keepdims=True), (C, 128))


def k_enc_weights(w_ref, b_ref, out_ref, bias_ref):
    arranged(w_ref, out_ref)
    bias_ref[...] = column(b_ref)


def interp_weight(g, cell, count, cells):
    num = 2 * g - 7
    low = jnp.right_shift(num, 4)
    w = (num - 16 * low).astype(F32) * (1.0 / 16.0)
    w = jnp.where((low < 0) | (low >= cells - 1), 0.0, w)
    low = jnp.clip(low, 0, cells - 1)
    value = jnp.where(cell == low, 1.0 - w, jnp.where(cell == low + 1, w, 0.0))
    return jnp.where((g >= 0) & (g < count), value, 0.0)


def k_dec_weights(w_ref, b_ref, bw_ref, proj_ref, ow_ref, bb_ref, out_ref, bias_ref, vt_ref, ow2_ref, bb2_ref, s_ref):
    arranged(w_ref, out_ref)
    bias_ref[...] = column(b_ref)
    proj = proj_ref[...]
    r = dot_nt(bw_ref[...], jnp.concatenate([proj, proj], axis=0))
    half = lanes_of(C) < C
    for ab in range(9):
        both = jnp.where(half, r[96 * ab : 96 * ab + 64], r[96 * ab + 32 : 96 * ab + 96])
        vt_ref[:, pl.ds(128 * ab, 128)] = both.astype(BF)
    ow = ow_ref[...]
    none = jnp.zeros_like(ow)
    ow2_ref[...] = jnp.concatenate(
        [jnp.concatenate([ow, none], axis=1), jnp.concatenate([none, ow], axis=1)], axis=0
    )
    bb2_ref[...] = jnp.concatenate([bb_ref[...], bb_ref[...]], axis=1)
    j = lax.axis_index("sy")
    row = lax.broadcasted_iota(jnp.int32, (32, 128), 0)
    lane = lax.broadcasted_iota(jnp.int32, (32, 128), 1)
    y, z = jnp.right_shift(lane, 4), jnp.bitwise_and(lane, 15)
    cell_y = j - 1 + jnp.right_shift(row, 3)
    zero = jnp.zeros((96, 128), BF)
    for b in range(3):
        wy = interp_weight(8 * j + y + (b - 1), cell_y, 8 * NSY, NSY)
        wy = jnp.where(row < 24, wy, 0.0)
        for c in range(3):
            for zo in range(2):
                wz = interp_weight(z + (c - 1), 1 - zo, 16, 2)
                at = pl.ds(128 * (3 * b + c), 128)
                s_ref[pl.ds(128 * zo, 32), at] = (wy * wz).astype(BF)
                s_ref[pl.ds(128 * zo + 32, 96), at] = zero


def z_taps(v, out_ref, b, at, z):
    k = 3 * C * b
    out_ref[pl.ds(k, C), at] = jnp.where(z == 0, 0.0, roll(v, 1)).astype(BF)
    out_ref[pl.ds(k + C, C), at] = v.astype(BF)
    out_ref[pl.ds(k + 2 * C, C), at] = jnp.where(z == 15, 0.0, roll(v, -1)).astype(BF)


def y_taps(own, left, left_at, right, right_at, out_ref, at, lane, z):
    z_taps(roll(jnp.where(lane >= 112, roll(left, 112 - left_at), own), 16), out_ref, 0, at, z)
    z_taps(own, out_ref, 1, at, z)
    z_taps(roll(jnp.where(lane < 16, roll(right, -right_at), own), -16), out_ref, 2, at, z)


def k_encode(
    lo_ref, ft_ref, hi_ref, fl_ref, fr_ref, hl_ref, hr_ref, w_ref, bias_ref, em_ref, eh_ref, pool_ref, xm, g_ref
):
    lane = lanes_of(C)
    z = jnp.bitwise_and(lane, 15)
    even = jnp.bitwise_and(lane, 16) == 0
    s, j = lax.axis_index("sx"), lax.axis_index("sy")
    for g in range(5):
        hl, hr = hl_ref[g].astype(F32), hr_ref[g].astype(F32)
        fl, fr = fl_ref[g].astype(F32), fr_ref[g].astype(F32)
        for q in range(4):
            r = 4 * g + q
            own = row_of(r, lo_ref, ft_ref, hi_ref).astype(F32)
            y_taps(own, hl, 32 * q + 16, hr, 32 * q, xm, pl.ds(128 * r, 128), lane, z)
        at = pl.ds(128 * (20 + g), 128)
        z_taps(jnp.where(even, hl, fr), xm, 0, at, z)
        z_taps(jnp.where(even, roll(hl, -16), roll(hr, 16)), xm, 1, at, z)
        z_taps(jnp.where(even, fl, hr), xm, 2, at, z)
    w = w_ref[...]
    for n in range(0, 25, 5):
        g_ref[:, pl.ds(128 * n, 640)] = dot(w, xm[:, pl.ds(128 * n, 640)])
    bias = bias_ref[...]
    best = [None, None]
    for r in range(18):
        v = g_ref[pl.ds(0, C), pl.ds(128 * r, 128)] + g_ref[pl.ds(C, C), pl.ds(128 * (r + 1), 128)]
        v = v + g_ref[pl.ds(2 * C, C), pl.ds(128 * (r + 2), 128)] + bias
        v = jnp.maximum(v, 0.0)
        if r == 0:
            v = jnp.where(s == 0, 0.0, v)
        if r == 17:
            v = jnp.where(s == NSX - 1, 0.0, v)
        v = v.astype(BF)
        em_ref[r] = v
        if 1 <= r <= 16:
            cell = (r - 1) // 8
            v = v.astype(F32)
            best[cell] = v if best[cell] is None else jnp.maximum(best[cell], v)
    outside = (even & (j == 0)) | (~even & (j == NSY - 1))
    for g in range(5):
        v = g_ref[pl.ds(0, C), pl.ds(128 * (20 + g), 128)] + bias
        for a in (1, 2):
            this = g_ref[pl.ds(a * C, C), pl.ds(128 * (20 + g), 128)]
            after = g_ref[pl.ds(a * C, C), pl.ds(128 * (20 + min(g + 1, 4)), 128)]
            v = v + roll(jnp.where(lane < 32 * a, after, this), -32 * a)
        v = jnp.where(outside, 0.0, jnp.maximum(v, 0.0))
        if g == 0:
            v = jnp.where((lane < 32) & (s == 0), 0.0, v)
        if g == 4:
            v = jnp.where((lane >= 64) | ((lane >= 32) & (s == NSX - 1)), 0.0, v)
        eh_ref[g] = v.astype(BF)
    for cell in range(2):
        m = best[cell]
        for shift in (64, 32, 16, -1, -2, -4):
            m = jnp.maximum(m, roll(m, shift))
        best[cell] = m
    first = lane == 0
    both = [jnp.where(first, best[0], roll(best[1], 1)), jnp.where(first, roll(best[0], -8), roll(best[1], -7))]
    pool_ref[...] = jnp.transpose(jnp.concatenate(both, axis=0))[:8]


def k_decode(em_ref, eh_ref, w_ref, bias_ref, d_ref, xm, g_ref):
    lane = lanes_of(C)
    z = jnp.bitwise_and(lane, 15)
    for r in range(18):
        own = em_ref[r].astype(F32)
        eh = eh_ref[r // 4].astype(F32)
        q = r % 4
        y_taps(own, eh, 32 * q, eh, 32 * q + 16, xm, pl.ds(128 * r, 128), lane, z)
    w = w_ref[...]
    for n in range(0, 18, 6):
        g_ref[:, pl.ds(128 * n, 768)] = dot(w, xm[:, pl.ds(128 * n, 768)])
    bias = bias_ref[...]
    for x in range(16):
        v = g_ref[pl.ds(0, C), pl.ds(128 * x, 128)] + g_ref[pl.ds(C, C), pl.ds(128 * (x + 1), 128)]
        d_ref[x] = v + g_ref[pl.ds(2 * C, C), pl.ds(128 * (x + 2), 128)] + bias


def k_message(left_ref, own_ref, right_ref, out_ref):
    message = jnp.concatenate(
        [left_ref[0:2], own_ref[0:2], right_ref[0:2], jnp.zeros((2, 128), F32)], axis=0
    )
    for i in range(NSY):
        out_ref[i] = message


def k_bottleneck(p_ref, vt_ref, bb_ref, ow_ref, out_ref):
    p = p_ref[...]
    pieces = []
    none = jnp.zeros((1, 8, 128), F32)
    for a in range(3):
        moved = p if a == 0 else jnp.concatenate([p[:, a:], p[:, :a]], axis=1)
        for b in range(3):
            if b == 0:
                v = jnp.concatenate([none, moved[:-1]], axis=0)
            elif b == 1:
                v = moved
            else:
                v = jnp.concatenate([moved[1:], none], axis=0)
            pieces.append(v.reshape(128, 128).astype(BF))
    h = dot_nt(jnp.concatenate(pieces, axis=1), vt_ref[...])
    h = jnp.maximum(h + bb_ref[...], 0.0).astype(BF)
    low = dot(h, ow_ref[...]).astype(BF).astype(F32)
    zero = jnp.zeros((8, 128), F32)
    for i in range(NSY):
        before = low[8 * (i - 1) : 8 * i] if i else zero
        after = low[8 * (i + 1) : 8 * (i + 2)] if i < NSY - 1 else zero
        out_ref[i] = jnp.concatenate([before, low[8 * i : 8 * i + 8], after], axis=0).astype(BF)


def k_final(parts_ref, s_ref, w_ref, d_ref, out_ref, xt, q_ref, buf):
    total = parts_ref[0].astype(F32)
    for i in range(1, NSY):
        total = total + parts_ref[i].astype(F32)
    total = jnp.concatenate([total, jnp.zeros((104, 128), F32)], axis=0)
    lt = jnp.transpose(total)
    lane = lanes_of(C)
    left = []
    for cell in range(4):
        here = jnp.bitwise_and(lane, 7) == cell
        left.append(jnp.concatenate([jnp.where(here, lt[:C], 0.0), jnp.where(here, lt[C:], 0.0)], axis=1).astype(BF))
    t = dot(jnp.concatenate(left, axis=0), s_ref[...])
    for cell in range(4):
        for bc in range(9):
            xt[pl.ds(C * bc, C), pl.ds(128 * cell, 128)] = t[
                C * cell : C * cell + C, 128 * bc : 128 * bc + 128
            ].astype(BF)
    q_ref[...] = dot(w_ref[...], xt[...])
    s = lax.axis_index("sx")
    for x in range(16):
        v = d_ref[x]
        for a in range(3):
            g = x + a - 1
            num = 2 * g - 7
            low = num // 16
            high = (num - 16 * low) / 16.0
            cell = low + 1
            w_low, w_high = jnp.float32(1.0 - high), jnp.float32(high)
            first, last = s == 0, s == NSX - 1
            if cell == 0:
                w_low = jnp.where(first, 0.0, w_low)
                w_high = jnp.where(first, 0.0 if g < 0 else 1.0, w_high)
            if cell == 2:
                w_low = jnp.where(last, 0.0 if g > 15 else 1.0, w_low)
                w_high = jnp.where(last, 0.0, w_high)
            v = v + w_low * q_ref[pl.ds(C * a, C), pl.ds(128 * cell, 128)]
            v = v + w_high * q_ref[pl.ds(C * a, C), pl.ds(128 * (cell + 1), 128)]
        buf[pl.ds(x, C, stride=16), :] = v
    out_ref[...] = buf[...].reshape(C, 16, 128).astype(BF)


def shifted(v, axis, step):
    size = lax.axis_size(axis)
    return lax.ppermute(v, axis, [(i, i + step) for i in range(size) if 0 <= i + step < size])


def per_device(features, enc_weight, enc_bias, proj_weight, bottle_weight, bottle_bias, out_weight, dec_weight, dec_bias):
    ft, lo, hi = call(
        k_features,
        (S((16, C, 128), BF), S((2, C, 128), BF), S((2, C, 128), BF)),
        features,
        name="features",
        scratch=[pltpu.VMEM((C * 16, 128), F32)],
    )
    x_lo, x_hi = shifted(hi, "sx", 1), shifted(lo, "sx", -1)
    we, be = call(
        k_enc_weights,
        (S((3 * C, 9 * C), BF), S((C, 128), F32)),
        enc_weight.reshape(27, C, C),
        enc_bias.reshape(1, C),
        name="enc_weights",
        flops=10**8,
    )
    fl, fr = call(k_faces, (S((5, C, 128), BF), S((5, C, 128), BF)), x_lo, ft, x_hi, name="faces")
    hl, hr = shifted(fr, "sy", 1), shifted(fl, "sy", -1)
    wd, bd, vt, ow2, bb2, smat = call(
        k_dec_weights,
        (
            S((3 * C, 9 * C), BF),
            S((C, 128), F32),
            S((C, 9 * 128), BF),
            S((C, 128), BF),
            S((1, C), F32),
            S((256, 9 * 128), BF),
        ),
        dec_weight.reshape(27, C, C),
        dec_bias.reshape(1, C),
        bottle_weight.reshape(27 * 32, 512),
        proj_weight,
        out_weight,
        bottle_bias.reshape(1, 32),
        name="dec_weights",
        flops=4 * 10**8,
    )
    em, eh, pooled = call(
        k_encode,
        (S((18, C, 128), BF), S((5, C, 128), BF), S((8, 128), F32)),
        x_lo,
        ft,
        x_hi,
        fl,
        fr,
        hl,
        hr,
        we,
        be,
        name="encode",
        scratch=[pltpu.VMEM((9 * C, 25 * 128), BF), pltpu.VMEM((3 * C, 25 * 128), F32)],
    )
    p_lo, p_hi = shifted(pooled, "sx", 1), shifted(pooled, "sx", -1)
    d = call(
        k_decode,
        S((16, C, 128), F32),
        em,
        eh,
        wd,
        bd,
        name="decode",
        scratch=[pltpu.VMEM((9 * C, 18 * 128), BF), pltpu.VMEM((3 * C, 18 * 128), F32)],
        flops=4 * 10**8,
    )
    message = call(k_message, S((NSY, 8, 128), F32), p_lo, pooled, p_hi, name="message")
    everyone = lax.all_to_all(message, "sy", 0, 0, tiled=True)
    partial = call(k_bottleneck, S((NSY, 24, 128), BF), everyone, vt, bb2, ow2, name="bottleneck")
    parts = lax.all_to_all(partial, "sy", 0, 0, tiled=True)
    return call(
        k_final,
        S((C, 16, 128), BF),
        parts,
        smat,
        wd,
        d,
        name="final",
        scratch=[
            pltpu.VMEM((9 * C, 512), BF),
            pltpu.VMEM((3 * C, 512), F32),
            pltpu.VMEM((C * 16, 128), F32),
        ],
    )


def solution(mesh):
    in_specs = (P(None, "sx", "sy"), P(), P(), P(), P(None, None, None, "sy", None), P("sy"), P("sy", None), P(), P())
    return jax.shard_map(per_device, mesh=mesh, in_specs=in_specs, out_specs=P(None, "sx", "sy"), check_vma=False)
```

time: 102 us -> 65 us (0.64)
  the two profiles are of different devices: /device:TPU:97 before, /device:TPU:384 now
where the time goes in v1:
time: 65 us; the launch traced here: 64.6 us
  starting transfers between devices  31.5 us (48%)
  waiting for transfers between devices  18.3 us (28%)
  Pallas kernels  12.3 us (19%)
  local copies, waits for them, and re-layouts  2.27 us (3%)
    ppermute x6, starting transfers between devices, shifted(): lax.ppermute(v, axis, [(i, i + step) for i in range(size) if 0 <= i + ste...  18.3 us
    pallas_call x9, Pallas kernels, call(): pl.pallas_call(kernel, out_shape=outs, in_specs=[VM] * len(ins), out_spec...  12.3 us
    all_to_all x1, starting transfers between devices, per_device(): everyone = lax.all_to_all(message, 'sy', 0, 0, tiled=True)  9.72 us
    ppermute x6, waiting for transfers between devices, shifted(): lax.ppermute(v, axis, [(i, i + step) for i in range(size) if 0 <= i + ste...  6.99 us
    all_to_all x1, waiting for transfers between devices, per_device(): everyone = lax.all_to_all(message, 'sy', 0, 0, tiled=True)  6.59 us
    all_to_all x1, waiting for transfers between devices, per_device(): parts = lax.all_to_all(partial, 'sy', 0, 0, tiled=True)  4.73 us
    all_to_all x1, starting transfers between devices, per_device(): parts = lax.all_to_all(partial, 'sy', 0, 0, tiled=True)  3.51 us
    unnamed x18, local copies, waits for them, and re-layouts  2.27 us
  transfers between devices with their start and end apart: 8, of which 5 were waited for; matrix products, arithmetic and copies ran while one was open for 0% of the time, Pallas kernels for 5%

profile of v1, /device:TPU:384, one launch (start us, length us, event | category | flops | bytes accessed | tf_op | source)
XLA Modules:
  0.0 64.6 jit_solution(6206443330883978064)
XLA Ops:
  0.0 1.0 %copy-done.1 = bf16[64,16,128]{2,1,0:T(8,128)(2,1)S(1)} copy-done((bf16[64,16,128]{2,1,0:T(8,128)(2,1)S(1)}, bf16[64,16,128]{2,1,0:T(8,128)(2,1)}, u32[]{:S(2)}) %copy-start.1) | copy-done | bytes 262168
  1.0 0.2 features.1
  1.2 1.9 %collective-permute-start = (bf16[2,64,128]{2,1,0:T(8,128)(2,1)S(1)}, bf16[2,64,128]{2,1,0:T(8,128)(2,1)S(1)}, u32[]{:S(2)}, u32[]{:S(2)}) collective-permute-start(bf16[2,64,128]{2,1,0:T(8,128)(2,1)S(1)} %get-tuple-element.21), channel_id=1, source_target_pairs={{0,16},{16,32},{32,48},{48,64},{64,80},{80,96},{96,112},{112,128},... | collective-permute-start | bytes 98312 | tf_op jit(solution)/shard_map/ppermute | solution.py:311
  3.1 4.9 %collective-permute-start.1 = (bf16[2,64,128]{2,1,0:T(8,128)(2,1)S(1)}, bf16[2,64,128]{2,1,0:T(8,128)(2,1)S(1)}, u32[]{:S(2)}, u32[]{:S(2)}) collective-permute-start(bf16[2,64,128]{2,1,0:T(8,128)(2,1)S(1)} %get-tuple-element.23), channel_id=1, source_target_pairs={{16,0},{32,16},{48,32},{64,48},{80,64},{96,80},{112,96},{128,112},... | collective-permute-start | bytes 98312 | tf_op jit(solution)/shard_map/ppermute | solution.py:311
  8.0 1.6 %collective-permute-done.1.hi_ref = bf16[2,64,128]{2,1,0:T(8,128)(2,1)S(1)} collective-permute-done((bf16[2,64,128]{2,1,0:T(8,128)(2,1)S(1)}, bf16[2,64,128]{2,1,0:T(8,128)(2,1)S(1)}, u32[]{:S(2)}, u32[]{:S(2)}) %collective-permute-start.1) | collective-permute-done | bytes 32800 | tf_op jit(solution)/shard_map/ppermute | solution.py:311
  9.6 0.2 faces.1
  9.8 1.3 %collective-permute-start.3 = (bf16[5,64,128]{2,1,0:T(8,128)(2,1)S(1)}, bf16[5,64,128]{2,1,0:T(8,128)(2,1)S(1)}, u32[]{:S(2)}, u32[]{:S(2)}) collective-permute-start(bf16[5,64,128]{2,1,0:T(8,128)(2,1)S(1)} %get-tuple-element.24.fl_ref), channel_id=1, source_target_pairs={{1,0},{2,1},{3,2},{4,3},{5,4},{6,5},{7,6},{8,7},{9,8},{10,9},{11,1... | collective-permute-start | bytes 245768 | tf_op jit(solution)/shard_map/ppermute | solution.py:311
  11.1 4.6 %collective-permute-start.2 = (bf16[5,64,128]{2,1,0:T(8,128)(2,1)S(1)}, bf16[5,64,128]{2,1,0:T(8,128)(2,1)S(1)}, u32[]{:S(2)}, u32[]{:S(2)}) collective-permute-start(bf16[5,64,128]{2,1,0:T(8,128)(2,1)S(1)} %get-tuple-element.25.fr_ref), channel_id=1, source_target_pairs={{0,1},{1,2},{2,3},{3,4},{4,5},{5,6},{6,7},{7,8},{8,9},{9,10},{10,1... | collective-permute-start | bytes 245768 | tf_op jit(solution)/shard_map/ppermute | solution.py:311
  15.7 0.6 copy-done.2
  16.4 1.2 %collective-permute-done.2.hl_ref = bf16[5,64,128]{2,1,0:T(8,128)(2,1)S(1)} collective-permute-done((bf16[5,64,128]{2,1,0:T(8,128)(2,1)S(1)}, bf16[5,64,128]{2,1,0:T(8,128)(2,1)S(1)}, u32[]{:S(2)}, u32[]{:S(2)}) %collective-permute-start.2) | collective-permute-done | bytes 81952 | tf_op jit(solution)/shard_map/ppermute | solution.py:311
  17.7 5.2 %encode.1 = (bf16[18,64,128]{2,1,0:T(8,128)(2,1)S(1)}, bf16[5,64,128]{2,1,0:T(8,128)(2,1)S(1)}, f32[8,128]{1,0:T(8,128)S(1)}) custom-call(bf16[2,64,128]{2,1,0:T(8,128)(2,1)S(1)} %collective-permute-done.lo_ref, bf16[16,64,128]{2,1,0:T(8,128)(2,1)S(1)} %get-tuple-element.22.ft_ref, bf16[2,64,128]{2,1,0:T(8,128)(2,1)S(1)} %collective-permute-done.1.hi_ref, ...), custom_call_target="tpu_custom_call" | custom-call | flops 1000000 | bytes 100000 | tf_op jit(solution)/shard_map/encode/pallas_call | solution.py:17
  22.9 3.7 %collective-permute-start.5 = (f32[8,128]{1,0:T(8,128)S(1)}, f32[8,128]{1,0:T(8,128)S(1)}, u32[]{:S(2)}, u32[]{:S(2)}) collective-permute-start(f32[8,128]{1,0:T(8,128)S(1)} %get-tuple-element.28.own_ref), channel_id=1, source_target_pairs={{16,0},{32,16},{48,32},{64,48},{80,64},{96,80},{112,96},{128,112},... | collective-permute-start | bytes 12296 | tf_op jit(solution)/shard_map/ppermute | solution.py:311
  26.6 1.9 %collective-permute-start.4 = (f32[8,128]{1,0:T(8,128)S(1)}, f32[8,128]{1,0:T(8,128)S(1)}, u32[]{:S(2)}, u32[]{:S(2)}) collective-permute-start(f32[8,128]{1,0:T(8,128)S(1)} %get-tuple-element.28.own_ref), channel_id=1, source_target_pairs={{0,16},{16,32},{32,48},{48,64},{64,80},{80,96},{96,112},{112,128},... | collective-permute-start | bytes 12296 | tf_op jit(solution)/shard_map/ppermute | solution.py:311
  28.5 4.2 %collective-permute-done.4.left_ref = f32[8,128]{1,0:T(8,128)S(1)} collective-permute-done((f32[8,128]{1,0:T(8,128)S(1)}, f32[8,128]{1,0:T(8,128)S(1)}, u32[]{:S(2)}, u32[]{:S(2)}) %collective-permute-start.4) | collective-permute-done | bytes 4128 | tf_op jit(solution)/shard_map/ppermute | solution.py:311
  32.7 0.6 message.1
  33.4 9.7 %all-to-all-start = ((f32[16,8,128]{2,1,0:T(8,128)}), f32[16,8,128]{2,1,0:T(8,128)S(1)}, u32[]{:S(2)}, u32[]{:S(2)}) async-start(f32[16,8,128]{2,1,0:T(8,128)} %message.1), calls=%async_computation | async-start | bytes 131072 | tf_op jit(solution)/shard_map/all_to_all | solution.py:380
  43.2 0.6 copy-done.7
  43.8 0.4 dec_weights.1
  44.2 6.6 %all-to-all-done.p_ref = f32[16,8,128]{2,1,0:T(8,128)S(1)} async-done(((f32[16,8,128]{2,1,0:T(8,128)}), f32[16,8,128]{2,1,0:T(8,128)S(1)}, u32[]{:S(2)}, u32[]{:S(2)}) %all-to-all-start) | async-done | bytes 65568 | tf_op jit(solution)/shard_map/all_to_all | solution.py:380
  50.8 1.0 %bottleneck.1 = bf16[16,24,128]{2,1,0:T(8,128)(2,1)} custom-call(f32[16,8,128]{2,1,0:T(8,128)S(1)} %all-to-all-done.p_ref, bf16[64,1152]{1,0:T(8,128)(2,1)S(1)} %get-tuple-element.29.vt_ref, f32[1,64]{1,0:T(1,128)S(1)} %get-tuple-element.30.bb_ref, bf16[64,128]{1,0:T(8,128)(2,1)S(1)} %get-tuple-element.31.ow_ref), custom_call_target="tpu_custom_call" | custom-call | flops 1000000 | bytes 100000 | tf_op jit(solution)/shard_map/bottleneck/pallas_call | solution.py:17
  51.8 3.5 %all-to-all-start.1 = ((bf16[16,24,128]{2,1,0:T(8,128)(2,1)}), bf16[16,24,128]{2,1,0:T(8,128)(2,1)S(1)}, u32[]{:S(2)}, u32[]{:S(2)}) async-start(bf16[16,24,128]{2,1,0:T(8,128)(2,1)} %bottleneck.1), calls=%async_computation.1 | async-start | bytes 196608 | tf_op jit(solution)/shard_map/all_to_all | solution.py:382
  55.3 3.0 %decode.1.d_ref = f32[16,64,128]{2,1,0:T(8,128)S(1)} custom-call(bf16[18,64,128]{2,1,0:T(8,128)(2,1)S(1)} %get-tuple-element.34.em_ref, bf16[5,64,128]{2,1,0:T(8,128)(2,1)S(1)} %get-tuple-element.35.eh_ref, bf16[192,576]{1,0:T(8,128)(2,1)S(1)} %get-tuple-element.33.w_ref, f32[64,128]{1,0:T(8,128)S(1)} %get-tuple-element.36.bias_ref), custom_call_target="tpu_custom_call" | custom-call | flops 400000000 | bytes 100000 | tf_op jit(solution)/shard_map/decode/pallas_call | solution.py:17
  58.2 4.7 %all-to-all-done.1.parts_ref = bf16[16,24,128]{2,1,0:T(8,128)(2,1)S(1)} async-done(((bf16[16,24,128]{2,1,0:T(8,128)(2,1)}), bf16[16,24,128]{2,1,0:T(8,128)(2,1)S(1)}, u32[]{:S(2)}, u32[]{:S(2)}) %all-to-all-start.1) | async-done | bytes 98336 | tf_op jit(solution)/shard_map/all_to_all | solution.py:382
  63.0 1.6 %final.1 = bf16[64,16,128]{2,1,0:T(8,128)(2,1)} custom-call(bf16[16,24,128]{2,1,0:T(8,128)(2,1)S(1)} %all-to-all-done.1.parts_ref, bf16[256,1152]{1,0:T(8,128)(2,1)S(1)} %get-tuple-element.32.s_ref, bf16[192,576]{1,0:T(8,128)(2,1)S(1)} %get-tuple-element.33.w_ref, f32[16,64,128]{2,1,0:T(8,128)S(1)} %decode.1.d_ref), custom_call_target="tpu_custom_call" | custom-call | flops 1000000 | bytes 100000 | tf_op jit(solution)/shard_map/final/pallas_call | solution.py:17
  (19 shorter events, 0.2 us)
Async XLA Ops:
  0.0 15.6 %copy-start = (bf16[3,3,3,64,64]{4,3,2,1,0:T(8,128)(2,1)S(1)}, bf16[3,3,3,64,64]{4,3,2,1,0:T(8,128)(2,1)}, u32[]{:S(2)}) copy-start(bf16[3,3,3,64,64]{4,3,2,1,0:T(8,128)(2,1)} %param.10) | copy-start | bytes 663556
  0.0 1.0 %copy-start.1 = (bf16[64,16,128]{2,1,0:T(8,128)(2,1)S(1)}, bf16[64,16,128]{2,1,0:T(8,128)(2,1)}, u32[]{:S(2)}) copy-start(bf16[64,16,128]{2,1,0:T(8,128)(2,1)} %x_ref.1) | copy-start | bytes 786436
  1.2 6.8 %collective-permute-start = (bf16[2,64,128]{2,1,0:T(8,128)(2,1)S(1)}, bf16[2,64,128]{2,1,0:T(8,128)(2,1)S(1)}, u32[]{:S(2)}, u32[]{:S(2)}) collective-permute-start(bf16[2,64,128]{2,1,0:T(8,128)(2,1)S(1)} %get-tuple-element.21), channel_id=1, source_target_pairs={{0,16},{16,32},{32,48},{48,64},{64,80},{80,96},{96,112},{112,128},... | collective-permute-start | bytes 98312 | tf_op jit(solution)/shard_map/ppermute | solution.py:311
  3.1 6.4 %collective-permute-start.1 = (bf16[2,64,128]{2,1,0:T(8,128)(2,1)S(1)}, bf16[2,64,128]{2,1,0:T(8,128)(2,1)S(1)}, u32[]{:S(2)}, u32[]{:S(2)}) collective-permute-start(bf16[2,64,128]{2,1,0:T(8,128)(2,1)S(1)} %get-tuple-element.23), channel_id=1, source_target_pairs={{16,0},{32,16},{48,32},{64,48},{80,64},{96,80},{112,96},{128,112},... | collective-permute-start | bytes 98312 | tf_op jit(solution)/shard_map/ppermute | solution.py:311
  9.8 6.7 %collective-permute-start.3 = (bf16[5,64,128]{2,1,0:T(8,128)(2,1)S(1)}, bf16[5,64,128]{2,1,0:T(8,128)(2,1)S(1)}, u32[]{:S(2)}, u32[]{:S(2)}) collective-permute-start(bf16[5,64,128]{2,1,0:T(8,128)(2,1)S(1)} %get-tuple-element.24.fl_ref), channel_id=1, source_target_pairs={{1,0},{2,1},{3,2},{4,3},{5,4},{6,5},{7,6},{8,7},{9,8},{10,9},{11,1... | collective-permute-start | bytes 245768 | tf_op jit(solution)/shard_map/ppermute | solution.py:311
  11.1 6.6 %collective-permute-start.2 = (bf16[5,64,128]{2,1,0:T(8,128)(2,1)S(1)}, bf16[5,64,128]{2,1,0:T(8,128)(2,1)S(1)}, u32[]{:S(2)}, u32[]{:S(2)}) collective-permute-start(bf16[5,64,128]{2,1,0:T(8,128)(2,1)S(1)} %get-tuple-element.25.fr_ref), channel_id=1, source_target_pairs={{0,1},{1,2},{2,3},{3,4},{4,5},{5,6},{6,7},{7,8},{8,9},{9,10},{10,1... | collective-permute-start | bytes 245768 | tf_op jit(solution)/shard_map/ppermute | solution.py:311
  15.6 0.7 %copy-start.2 = (f32[64]{0:T(128)S(1)}, f32[64]{0:T(128)}, u32[]{:S(2)}) copy-start(f32[64]{0:T(128)} %param.11) | copy-start | bytes 772
  15.6 27.5 %copy-start.3 = (bf16[3,3,3,32,512]{4,3,2,1,0:T(8,128)(2,1)S(1)}, bf16[3,3,3,32,512]{4,3,2,1,0:T(8,128)(2,1)}, u32[]{:S(2)}) copy-start(bf16[3,3,3,32,512]{4,3,2,1,0:T(8,128)(2,1)} %param.13) | copy-start | bytes 2654212
  17.7 25.5 %copy-start.4 = (bf16[3,3,3,64,64]{4,3,2,1,0:T(8,128)(2,1)S(1)}, bf16[3,3,3,64,64]{4,3,2,1,0:T(8,128)(2,1)}, u32[]{:S(2)}) copy-start(bf16[3,3,3,64,64]{4,3,2,1,0:T(8,128)(2,1)} %param.16) | copy-start | bytes 663556
  22.9 5.7 %collective-permute-start.5 = (f32[8,128]{1,0:T(8,128)S(1)}, f32[8,128]{1,0:T(8,128)S(1)}, u32[]{:S(2)}, u32[]{:S(2)}) collective-permute-start(f32[8,128]{1,0:T(8,128)S(1)} %get-tuple-element.28.own_ref), channel_id=1, source_target_pairs={{16,0},{32,16},{48,32},{64,48},{80,64},{96,80},{112,96},{128,112},... | collective-permute-start | bytes 12296 | tf_op jit(solution)/shard_map/ppermute | solution.py:311
  26.6 6.1 %collective-permute-start.4 = (f32[8,128]{1,0:T(8,128)S(1)}, f32[8,128]{1,0:T(8,128)S(1)}, u32[]{:S(2)}, u32[]{:S(2)}) collective-permute-start(f32[8,128]{1,0:T(8,128)S(1)} %get-tuple-element.28.own_ref), channel_id=1, source_target_pairs={{0,16},{16,32},{32,48},{48,64},{64,80},{80,96},{96,112},{112,128},... | collective-permute-start | bytes 12296 | tf_op jit(solution)/shard_map/ppermute | solution.py:311
  33.4 9.8 %copy-start.5 = (bf16[64,512]{1,0:T(8,128)(2,1)S(1)}, bf16[64,512]{1,0:T(8,128)(2,1)}, u32[]{:S(2)}) copy-start(bf16[64,512]{1,0:T(8,128)(2,1)} %proj_ref.1) | copy-start | bytes 196612
  33.4 9.8 %copy-start.6 = (bf16[32,64]{1,0:T(8,128)(2,1)S(1)}, bf16[32,64]{1,0:T(8,128)(2,1)}, u32[]{:S(2)}) copy-start(bf16[32,64]{1,0:T(8,128)(2,1)} %ow_ref.1) | copy-start | bytes 12292
  33.4 17.4 %all-to-all-start = ((f32[16,8,128]{2,1,0:T(8,128)}), f32[16,8,128]{2,1,0:T(8,128)S(1)}, u32[]{:S(2)}, u32[]{:S(2)}) async-start(f32[16,8,128]{2,1,0:T(8,128)} %message.1), calls=%async_computation | async-start | bytes 131072 | tf_op jit(solution)/shard_map/all_to_all | solution.py:380
  43.1 0.7 %copy-start.7 = (f32[64]{0:T(128)S(1)}, f32[64]{0:T(128)}, u32[]{:S(2)}) copy-start(f32[64]{0:T(128)} %param.17) | copy-start | bytes 772
  43.1 0.7 %copy-start.8 = (f32[32]{0:T(128)S(1)}, f32[32]{0:T(128)}, u32[]{:S(2)}) copy-start(f32[32]{0:T(128)} %param.14) | copy-start | bytes 388
  51.8 11.2 %all-to-all-start.1 = ((bf16[16,24,128]{2,1,0:T(8,128)(2,1)}), bf16[16,24,128]{2,1,0:T(8,128)(2,1)S(1)}, u32[]{:S(2)}, u32[]{:S(2)}) async-start(bf16[16,24,128]{2,1,0:T(8,128)(2,1)} %bottleneck.1), calls=%async_computation.1 | async-start | bytes 196608 | tf_op jit(solution)/shard_map/all_to_all | solution.py:382

commit v2 on v1

--- a/solution.py
+++ b/solution.py
@@ -47,32 +47,39 @@
     return v if shift == 0 else pltpu.roll(v, shift, 1)
 
 
-def k_features(x_ref, ft_ref, lo_ref, hi_ref, buf):
+def even_of(axis):
+    return lax.rem(lax.axis_index(axis), 2) == 0
+
+
+def k_features(x_ref, ft_ref, inner_ref, outer_ref, buf):
     buf[...] = x_ref[...].reshape(C * 16, 128).astype(F32)
+    even = even_of("sx")
+
+    def row(x):
+        return buf[pl.ds(x, C, stride=16), :]
+
+    for k in range(2):
+        low, high = row(k), row(14 + k)
+        inner_ref[k] = jnp.where(even, high, low).astype(BF)
+        outer_ref[k] = jnp.where(even, low, high).astype(BF)
     for x in range(16):
-        row = buf[pl.ds(x, C, stride=16), :].astype(BF)
-        ft_ref[x] = row
-        if x < 2:
-            lo_ref[x] = row
-        if x >= 14:
-            hi_ref[x - 14] = row
-
-
-def row_of(r, lo_ref, ft_ref, hi_ref):
-    if r < 2:
-        return lo_ref[r]
-    if r < 18:
-        return ft_ref[r - 2]
-    return hi_ref[r - 18]
-
-
-def k_faces(lo_ref, ft_ref, hi_ref, left_ref, right_ref):
+        ft_ref[x + 2] = row(x).astype(BF)
+
+
+def k_faces(inner_ref, outer_ref, ft_ref, x_ref, left_ref, right_ref, s_inner_ref, s_outer_ref):
     lane = lanes_of(C)
+    even_x, even_y = even_of("sx"), even_of("sy")
+    for k in range(2):
+        inner, outer = inner_ref[k], outer_ref[k]
+        x_ref[k] = jnp.where(even_x, outer, inner)
+        x_ref[2 + k] = jnp.where(even_x, inner, outer)
     for g in range(5):
         left = None
         for q in range(4):
-            row = row_of(4 * g + q, lo_ref, ft_ref, hi_ref).astype(F32)
-            a, b = roll(row, 32 * q), roll(row, 32 * q - 96)
+            r = 4 * g + q
+            v = x_ref[r] if r < 2 else ft_ref[r] if r < 18 else x_ref[r - 16]
+            v = v.astype(F32)
+            a, b = roll(v, 32 * q), roll(v, 32 * q - 96)
             if q == 0:
                 left, right = a, b
             else:
@@ -80,6 +87,8 @@
                 left, right = jnp.where(here, a, left), jnp.where(here, b, right)
         left_ref[g] = left.astype(BF)
         right_ref[g] = right.astype(BF)
+        s_inner_ref[g] = jnp.where(even_y, right, left).astype(BF)
+        s_outer_ref[g] = jnp.where(even_y, left, right).astype(BF)
 
 
 def arranged(w_ref, out_ref):
@@ -145,9 +154,10 @@
 
 def z_taps(v, out_ref, b, at, z):
     k = 3 * C * b
-    out_ref[pl.ds(k, C), at] = jnp.where(z == 0, 0.0, roll(v, 1)).astype(BF)
-    out_ref[pl.ds(k + C, C), at] = v.astype(BF)
-    out_ref[pl.ds(k + 2 * C, C), at] = jnp.where(z == 15, 0.0, roll(v, -1)).astype(BF)
+    zero = jnp.zeros_like(v)
+    out_ref[at, pl.ds(k, C), :] = jnp.where(z == 0, zero, roll(v, 1))
+    out_ref[at, pl.ds(k + C, C), :] = v
+    out_ref[at, pl.ds(k + 2 * C, C), :] = jnp.where(z == 15, zero, roll(v, -1))
 
 
 def y_taps(own, left, left_at, right, right_at, out_ref, at, lane, z):
@@ -156,49 +166,57 @@
     z_taps(roll(jnp.where(lane < 16, roll(right, -right_at), own), -16), out_ref, 2, at, z)
 
 
+def products(w_ref, xm, g_ref, first, last):
+    w = w_ref[...]
+    for n in range(first, last, 2):
+        if n + 1 < last:
+            g = dot(w, jnp.concatenate([xm[n], xm[n + 1]], axis=1))
+            g_ref[n] = g[:, :128]
+            g_ref[n + 1] = g[:, 128:]
+        else:
+            g_ref[n] = dot(w, xm[n])
+
+
 def k_encode(
-    lo_ref, ft_ref, hi_ref, fl_ref, fr_ref, hl_ref, hr_ref, w_ref, bias_ref, em_ref, eh_ref, pool_ref, xm, g_ref
+    ft_ref, x_ref, fl_ref, fr_ref, inner_ref, outer_ref, w_ref, bias_ref, em_ref, eh_ref, pool_ref, xm, g_ref
 ):
     lane = lanes_of(C)
     z = jnp.bitwise_and(lane, 15)
     even = jnp.bitwise_and(lane, 16) == 0
     s, j = lax.axis_index("sx"), lax.axis_index("sy")
+    even_y = even_of("sy")
     for g in range(5):
-        hl, hr = hl_ref[g].astype(F32), hr_ref[g].astype(F32)
-        fl, fr = fl_ref[g].astype(F32), fr_ref[g].astype(F32)
+        inner, outer = inner_ref[g], outer_ref[g]
+        hl, hr = jnp.where(even_y, outer, inner), jnp.where(even_y, inner, outer)
+        fl, fr = fl_ref[g], fr_ref[g]
         for q in range(4):
             r = 4 * g + q
-            own = row_of(r, lo_ref, ft_ref, hi_ref).astype(F32)
-            y_taps(own, hl, 32 * q + 16, hr, 32 * q, xm, pl.ds(128 * r, 128), lane, z)
-        at = pl.ds(128 * (20 + g), 128)
+            own = x_ref[r] if r < 2 else ft_ref[r] if r < 18 else x_ref[r - 16]
+            y_taps(own, hl, 32 * q + 16, hr, 32 * q, xm, r, lane, z)
+        at = 20 + g
         z_taps(jnp.where(even, hl, fr), xm, 0, at, z)
         z_taps(jnp.where(even, roll(hl, -16), roll(hr, 16)), xm, 1, at, z)
         z_taps(jnp.where(even, fl, hr), xm, 2, at, z)
-    w = w_ref[...]
-    for n in range(0, 25, 5):
-        g_ref[:, pl.ds(128 * n, 640)] = dot(w, xm[:, pl.ds(128 * n, 640)])
+    products(w_ref, xm, g_ref, 0, 25)
     bias = bias_ref[...]
     best = [None, None]
     for r in range(18):
-        v = g_ref[pl.ds(0, C), pl.ds(128 * r, 128)] + g_ref[pl.ds(C, C), pl.ds(128 * (r + 1), 128)]
-        v = v + g_ref[pl.ds(2 * C, C), pl.ds(128 * (r + 2), 128)] + bias
+        v = g_ref[r, pl.ds(0, C), :] + g_ref[r + 1, pl.ds(C, C), :] + g_ref[r + 2, pl.ds(2 * C, C), :] + bias
         v = jnp.maximum(v, 0.0)
         if r == 0:
             v = jnp.where(s == 0, 0.0, v)
         if r == 17:
             v = jnp.where(s == NSX - 1, 0.0, v)
-        v = v.astype(BF)
-        em_ref[r] = v
+        em_ref[r] = v.astype(BF)
         if 1 <= r <= 16:
             cell = (r - 1) // 8
-            v = v.astype(F32)
             best[cell] = v if best[cell] is None else jnp.maximum(best[cell], v)
     outside = (even & (j == 0)) | (~even & (j == NSY - 1))
     for g in range(5):
-        v = g_ref[pl.ds(0, C), pl.ds(128 * (20 + g), 128)] + bias
+        v = g_ref[20 + g, pl.ds(0, C), :] + bias
         for a in (1, 2):
-            this = g_ref[pl.ds(a * C, C), pl.ds(128 * (20 + g), 128)]
-            after = g_ref[pl.ds(a * C, C), pl.ds(128 * (20 + min(g + 1, 4)), 128)]
+            this = g_ref[20 + g, pl.ds(a * C, C), :]
+            after = g_ref[20 + min(g + 1, 4), pl.ds(a * C, C), :]
             v = v + roll(jnp.where(lane < 32 * a, after, this), -32 * a)
         v = jnp.where(outside, 0.0, jnp.maximum(v, 0.0))
         if g == 0:
@@ -207,7 +225,7 @@
             v = jnp.where((lane >= 64) | ((lane >= 32) & (s == NSX - 1)), 0.0, v)
         eh_ref[g] = v.astype(BF)
     for cell in range(2):
-        m = best[cell]
+        m = best[cell].astype(BF).astype(F32)
         for shift in (64, 32, 16, -1, -2, -4):
             m = jnp.maximum(m, roll(m, shift))
         best[cell] = m
@@ -220,23 +238,20 @@
     lane = lanes_of(C)
     z = jnp.bitwise_and(lane, 15)
     for r in range(18):
-        own = em_ref[r].astype(F32)
-        eh = eh_ref[r // 4].astype(F32)
+        eh = eh_ref[r // 4]
         q = r % 4
-        y_taps(own, eh, 32 * q, eh, 32 * q + 16, xm, pl.ds(128 * r, 128), lane, z)
-    w = w_ref[...]
-    for n in range(0, 18, 6):
-        g_ref[:, pl.ds(128 * n, 768)] = dot(w, xm[:, pl.ds(128 * n, 768)])
+        y_taps(em_ref[r], eh, 32 * q, eh, 32 * q + 16, xm, r, lane, z)
+    products(w_ref, xm, g_ref, 0, 18)
     bias = bias_ref[...]
     for x in range(16):
-        v = g_ref[pl.ds(0, C), pl.ds(128 * x, 128)] + g_ref[pl.ds(C, C), pl.ds(128 * (x + 1), 128)]
-        d_ref[x] = v + g_ref[pl.ds(2 * C, C), pl.ds(128 * (x + 2), 128)] + bias
-
-
-def k_message(left_ref, own_ref, right_ref, out_ref):
-    message = jnp.concatenate(
-        [left_ref[0:2], own_ref[0:2], right_ref[0:2], jnp.zeros((2, 128), F32)], axis=0
-    )
+        d_ref[x] = g_ref[x, pl.ds(0, C), :] + g_ref[x + 1, pl.ds(C, C), :] + g_ref[x + 2, pl.ds(2 * C, C), :] + bias
+
+
+def k_message(inner_ref, own_ref, outer_ref, _d, _w, out_ref):
+    even = even_of("sx")
+    inner, outer = inner_ref[0:2], outer_ref[0:2]
+    left, right = jnp.where(even, outer, inner), jnp.where(even, inner, outer)
+    message = jnp.concatenate([left, own_ref[0:2], right, jnp.zeros((2, 128), F32)], axis=0)
     for i in range(NSY):
         out_ref[i] = message
 
@@ -279,10 +294,10 @@
     t = dot(jnp.concatenate(left, axis=0), s_ref[...])
     for cell in range(4):
         for bc in range(9):
-            xt[pl.ds(C * bc, C), pl.ds(128 * cell, 128)] = t[
+            xt[cell, pl.ds(C * bc, C), :] = t[
                 C * cell : C * cell + C, 128 * bc : 128 * bc + 128
             ].astype(BF)
-    q_ref[...] = dot(w_ref[...], xt[...])
+    products(w_ref, xt, q_ref, 0, 4)
     s = lax.axis_index("sx")
     for x in range(16):
         v = d_ref[x]
@@ -300,26 +315,27 @@
             if cell == 2:
                 w_low = jnp.where(last, 0.0 if g > 15 else 1.0, w_low)
                 w_high = jnp.where(last, 0.0, w_high)
-            v = v + w_low * q_ref[pl.ds(C * a, C), pl.ds(128 * cell, 128)]
-            v = v + w_high * q_ref[pl.ds(C * a, C), pl.ds(128 * (cell + 1), 128)]
+            v = v + w_low * q_ref[cell, pl.ds(C * a, C), :]
+            v = v + w_high * q_ref[cell + 1, pl.ds(C * a, C), :]
         buf[pl.ds(x, C, stride=16), :] = v
     out_ref[...] = buf[...].reshape(C, 16, 128).astype(BF)
 
 
-def shifted(v, axis, step):
+def swapped(v, axis, start):
     size = lax.axis_size(axis)
-    return lax.ppermute(v, axis, [(i, i + step) for i in range(size) if 0 <= i + step < size])
+    low = range(start, size - 1, 2)
+    return lax.ppermute(v, axis, [(i, i + 1) for i in low] + [(i + 1, i) for i in low])
 
 
 def per_device(features, enc_weight, enc_bias, proj_weight, bottle_weight, bottle_bias, out_weight, dec_weight, dec_bias):
-    ft, lo, hi = call(
+    ft, inner, outer = call(
         k_features,
-        (S((16, C, 128), BF), S((2, C, 128), BF), S((2, C, 128), BF)),
+        (S((18, C, 128), BF), S((2, C, 128), BF), S((2, C, 128), BF)),
         features,
         name="features",
         scratch=[pltpu.VMEM((C * 16, 128), F32)],
     )
-    x_lo, x_hi = shifted(hi, "sx", 1), shifted(lo, "sx", -1)
+    outer, inner = swapped(outer, "sx", 1), swapped(inner, "sx", 0)
     we, be = call(
         k_enc_weights,
         (S((3 * C, 9 * C), BF), S((C, 128), F32)),
@@ -328,8 +344,10 @@
         name="enc_weights",
         flops=10**8,
     )
-    fl, fr = call(k_faces, (S((5, C, 128), BF), S((5, C, 128), BF)), x_lo, ft, x_hi, name="faces")
-    hl, hr = shifted(fr, "sy", 1), shifted(fl, "sy", -1)
+    xh, fl, fr, inner, outer = call(
+        k_faces, (S((4, C, 128), BF),) + (S((5, C, 128), BF),) * 4, inner, outer, ft, name="faces"
+    )
+    outer, inner = swapped(outer, "sy", 1), swapped(inner, "sy", 0)
     wd, bd, vt, ow2, bb2, smat = call(
         k_dec_weights,
         (
@@ -352,19 +370,18 @@
     em, eh, pooled = call(
         k_encode,
         (S((18, C, 128), BF), S((5, C, 128), BF), S((8, 128), F32)),
-        x_lo,
         ft,
-        x_hi,
+        xh,
         fl,
         fr,
-        hl,
-        hr,
+        inner,
+        outer,
         we,
         be,
         name="encode",
-        scratch=[pltpu.VMEM((9 * C, 25 * 128), BF), pltpu.VMEM((3 * C, 25 * 128), F32)],
-    )
-    p_lo, p_hi = shifted(pooled, "sx", 1), shifted(pooled, "sx", -1)
+        scratch=[pltpu.VMEM((25, 9 * C, 128), BF), pltpu.VMEM((25, 3 * C, 128), F32)],
+    )
+    outer, inner = swapped(pooled, "sx", 1), swapped(pooled, "sx", 0)
     d = call(
         k_decode,
         S((16, C, 128), F32),
@@ -373,10 +390,10 @@
         wd,
         bd,
         name="decode",
-        scratch=[pltpu.VMEM((9 * C, 18 * 128), BF), pltpu.VMEM((3 * C, 18 * 128), F32)],
+        scratch=[pltpu.VMEM((18, 9 * C, 128), BF), pltpu.VMEM((18, 3 * C, 128), F32)],
         flops=4 * 10**8,
     )
-    message = call(k_message, S((NSY, 8, 128), F32), p_lo, pooled, p_hi, name="message")
+    message = call(k_message, S((NSY, 8, 128), F32), inner, pooled, outer, d, vt, name="message")
     everyone = lax.all_to_all(message, "sy", 0, 0, tiled=True)
     partial = call(k_bottleneck, S((NSY, 24, 128), BF), everyone, vt, bb2, ow2, name="bottleneck")
     parts = lax.all_to_all(partial, "sy", 0, 0, tiled=True)
@@ -389,8 +406,8 @@
         d,
         name="final",
         scratch=[
-            pltpu.VMEM((9 * C, 512), BF),
-            pltpu.VMEM((3 * C, 512), F32),
+            pltpu.VMEM((4, 9 * C, 128), BF),
+            pltpu.VMEM((4, 3 * C, 128), F32),
             pltpu.VMEM((C * 16, 128), F32),
         ],
     )

time: 65 us -> 59.5 us (0.915)
  the two profiles are of different devices: /device:TPU:384 before, /device:TPU:256 now
where the time goes in v2:
time: 59.5 us; the launch traced here: 59 us
  blocking collectives  29.1 us (49%)
  starting transfers between devices  12 us (20%)
  Pallas kernels  7.76 us (13%)
  waiting for transfers between devices  6.45 us (11%)
  local copies, waits for them, and re-layouts  3.49 us (6%)
    all_to_all x1, blocking collectives, per_device(): everyone = lax.all_to_all(message, 'sy', 0, 0, tiled=True)  18.1 us
    ppermute x6, starting transfers between devices, swapped(): lax.ppermute(v, axis, [(i, i + 1) for i in low] + [(i + 1, i) for i in low])  12 us
    all_to_all x1, blocking collectives, per_device(): parts = lax.all_to_all(partial, 'sy', 0, 0, tiled=True)  11 us
    pallas_call x9, Pallas kernels, call(): pl.pallas_call(kernel, out_shape=outs, in_specs=[VM] * len(ins), out_spec...  7.76 us
    ppermute x6, waiting for transfers between devices, swapped(): lax.ppermute(v, axis, [(i, i + 1) for i in low] + [(i + 1, i) for i in low])  6.45 us
    unnamed x18, local copies, waits for them, and re-layouts  3.49 us
  transfers between devices with their start and end apart: 6, of which 2 were waited for; matrix products, arithmetic and copies ran while one was open for 0% of the time, Pallas kernels for 4%

profile of v2, /device:TPU:256, one launch (start us, length us, event | category | flops | bytes accessed | tf_op | source)
XLA Modules:
  0.0 59.0 jit_solution(12430833454515784419)
XLA Ops:
  0.0 1.0 %copy-done.1 = bf16[64,16,128]{2,1,0:T(8,128)(2,1)S(1)} copy-done((bf16[64,16,128]{2,1,0:T(8,128)(2,1)S(1)}, bf16[64,16,128]{2,1,0:T(8,128)(2,1)}, u32[]{:S(2)}) %copy-start.1) | copy-done | bytes 262168
  1.0 0.2 features.1
  1.2 1.9 %collective-permute-start = (bf16[2,64,128]{2,1,0:T(8,128)(2,1)S(1)}, bf16[2,64,128]{2,1,0:T(8,128)(2,1)S(1)}, u32[]{:S(2)}, u32[]{:S(2)}) collective-permute-start(bf16[2,64,128]{2,1,0:T(8,128)(2,1)S(1)} %get-tuple-element.25), channel_id=1, source_target_pairs={{0,16},{32,48},{64,80},{96,112},{128,144},{160,176},{192,208},{224... | collective-permute-start | bytes 98312 | tf_op jit(solution)/shard_map/ppermute | solution.py:327
  3.1 2.1 %collective-permute-start.1 = (bf16[2,64,128]{2,1,0:T(8,128)(2,1)S(1)}, bf16[2,64,128]{2,1,0:T(8,128)(2,1)S(1)}, u32[]{:S(2)}, u32[]{:S(2)}) collective-permute-start(bf16[2,64,128]{2,1,0:T(8,128)(2,1)S(1)} %get-tuple-element.26), channel_id=1, source_target_pairs={{16,32},{48,64},{80,96},{112,128},{144,160},{176,192},{208,224},{2... | collective-permute-start | bytes 98312 | tf_op jit(solution)/shard_map/ppermute | solution.py:327
  5.3 4.3 %collective-permute-done.1.outer_ref = bf16[2,64,128]{2,1,0:T(8,128)(2,1)S(1)} collective-permute-done((bf16[2,64,128]{2,1,0:T(8,128)(2,1)S(1)}, bf16[2,64,128]{2,1,0:T(8,128)(2,1)S(1)}, u32[]{:S(2)}, u32[]{:S(2)}) %collective-permute-start.1) | collective-permute-done | bytes 32800 | tf_op jit(solution)/shard_map/ppermute | solution.py:327
  9.6 0.2 faces.1
  9.8 3.5 %collective-permute-start.2 = (bf16[5,64,128]{2,1,0:T(8,128)(2,1)S(1)}, bf16[5,64,128]{2,1,0:T(8,128)(2,1)S(1)}, u32[]{:S(2)}, u32[]{:S(2)}) collective-permute-start(bf16[5,64,128]{2,1,0:T(8,128)(2,1)S(1)} %get-tuple-element.30), channel_id=1, source_target_pairs={{0,1},{2,3},{4,5},{6,7},{8,9},{10,11},{12,13},{14,15},{1,0},{3,2},... | collective-permute-start | bytes 245768 | tf_op jit(solution)/shard_map/ppermute | solution.py:327
  13.3 0.7 %collective-permute-start.3 = (bf16[5,64,128]{2,1,0:T(8,128)(2,1)S(1)}, bf16[5,64,128]{2,1,0:T(8,128)(2,1)S(1)}, u32[]{:S(2)}, u32[]{:S(2)}) collective-permute-start(bf16[5,64,128]{2,1,0:T(8,128)(2,1)S(1)} %get-tuple-element.31), channel_id=1, source_target_pairs={{1,2},{3,4},{5,6},{7,8},{9,10},{11,12},{13,14},{2,1},{4,3},{6,5},{... | collective-permute-start | bytes 245768 | tf_op jit(solution)/shard_map/ppermute | solution.py:327
  14.0 0.6 %copy-done.2 = f32[64]{0:T(128)S(1)} copy-done((f32[64]{0:T(128)S(1)}, f32[64]{0:T(128)}, u32[]{:S(2)}) %copy-start.2) | copy-done | bytes 280
  14.6 0.1 enc_weights.1
  14.8 0.2 copy-done.4
  15.0 0.4 copy-done.6
  15.4 0.1 copy-done.7
  15.5 1.2 %copy-done.3 = bf16[3,3,3,32,512]{4,3,2,1,0:T(8,128)(2,1)S(1)} copy-done((bf16[3,3,3,32,512]{4,3,2,1,0:T(8,128)(2,1)S(1)}, bf16[3,3,3,32,512]{4,3,2,1,0:T(8,128)(2,1)}, u32[]{:S(2)}) %copy-start.3) | copy-done | bytes 884760
  16.7 0.4 dec_weights.1
  17.1 2.7 %encode.1 = (bf16[18,64,128]{2,1,0:T(8,128)(2,1)S(1)}, bf16[5,64,128]{2,1,0:T(8,128)(2,1)S(1)}, f32[8,128]{1,0:T(8,128)S(1)}) custom-call(bf16[18,64,128]{2,1,0:T(8,128)(2,1)S(1)} %get-tuple-element.24.ft_ref, bf16[4,64,128]{2,1,0:T(8,128)(2,1)S(1)} %get-tuple-element.27.x_ref, bf16[5,64,128]{2,1,0:T(8,128)(2,1)S(1)} %get-tuple-element.28.fl_ref, ...), custom_call_target="tpu_custom_call" | custom-call | flops 1000000 | bytes 100000 | tf_op jit(solution)/shard_map/encode/pallas_call | solution.py:17
  19.8 1.9 %collective-permute-start.4 = (f32[8,128]{1,0:T(8,128)S(1)}, f32[8,128]{1,0:T(8,128)S(1)}, u32[]{:S(2)}, u32[]{:S(2)}) collective-permute-start(f32[8,128]{1,0:T(8,128)S(1)} %get-tuple-element.34.own_ref), channel_id=1, source_target_pairs={{0,16},{32,48},{64,80},{96,112},{128,144},{160,176},{192,208},{224... | collective-permute-start | bytes 12296 | tf_op jit(solution)/shard_map/ppermute | solution.py:327
  21.8 1.9 %collective-permute-start.5 = (f32[8,128]{1,0:T(8,128)S(1)}, f32[8,128]{1,0:T(8,128)S(1)}, u32[]{:S(2)}, u32[]{:S(2)}) collective-permute-start(f32[8,128]{1,0:T(8,128)S(1)} %get-tuple-element.34.own_ref), channel_id=1, source_target_pairs={{16,32},{48,64},{80,96},{112,128},{144,160},{176,192},{208,224},{2... | collective-permute-start | bytes 12296 | tf_op jit(solution)/shard_map/ppermute | solution.py:327
  23.7 2.1 %decode.1._d.d_ref = f32[16,64,128]{2,1,0:T(8,128)S(1)} custom-call(bf16[18,64,128]{2,1,0:T(8,128)(2,1)S(1)} %get-tuple-element.35.em_ref, bf16[5,64,128]{2,1,0:T(8,128)(2,1)S(1)} %get-tuple-element.36.eh_ref, bf16[192,576]{1,0:T(8,128)(2,1)S(1)} %get-tuple-element.37.w_ref, f32[64,128]{1,0:T(8,128)S(1)} %get-tuple-element.38.bias_ref), custom_call_target="tpu_custom_call" | custom-call | flops 400000000 | bytes 100000 | tf_op jit(solution)/shard_map/decode/pallas_call | solution.py:17
  25.8 2.1 %collective-permute-done.5.outer_ref = f32[8,128]{1,0:T(8,128)S(1)} collective-permute-done((f32[8,128]{1,0:T(8,128)S(1)}, f32[8,128]{1,0:T(8,128)S(1)}, u32[]{:S(2)}, u32[]{:S(2)}) %collective-permute-start.5) | collective-permute-done | bytes 4128 | tf_op jit(solution)/shard_map/ppermute | solution.py:327
  27.9 18.1 %all_to_all.10.p_ref = f32[16,8,128]{2,1,0:T(8,128)S(1)} all-to-all(f32[16,8,128]{2,1,0:T(8,128)S(1)} %message.1), channel_id=1, replica_groups=mesh['sx'=32,'sy'=16] {'sy'}, dimensions={0} | all-to-all | bytes 131072 | tf_op jit(solution)/shard_map/all_to_all | solution.py:397
  46.0 0.3 bottleneck.1
  46.4 11.0 %all_to_all.11.parts_ref = bf16[16,24,128]{2,1,0:T(8,128)(2,1)S(1)} all-to-all(bf16[16,24,128]{2,1,0:T(8,128)(2,1)S(1)} %bottleneck.1), channel_id=1, replica_groups=mesh['sx'=32,'sy'=16] {'sy'}, dimensions={0} | all-to-all | bytes 196608 | tf_op jit(solution)/shard_map/all_to_all | solution.py:399
  57.4 1.7 %final.1 = bf16[64,16,128]{2,1,0:T(8,128)(2,1)} custom-call(bf16[16,24,128]{2,1,0:T(8,128)(2,1)S(1)} %all_to_all.11.parts_ref, bf16[256,1152]{1,0:T(8,128)(2,1)S(1)} %get-tuple-element.42.s_ref, bf16[192,576]{1,0:T(8,128)(2,1)S(1)} %get-tuple-element.37.w_ref, f32[16,64,128]{2,1,0:T(8,128)S(1)} %decode.1._d.d_ref), custom_call_target="tpu_custom_call" | custom-call | flops 1000000 | bytes 100000 | tf_op jit(solution)/shard_map/final/pallas_call | solution.py:17
  (17 shorter events, 0.1 us)
Async XLA Ops:
  0.0 14.0 %copy-start = (bf16[3,3,3,64,64]{4,3,2,1,0:T(8,128)(2,1)S(1)}, bf16[3,3,3,64,64]{4,3,2,1,0:T(8,128)(2,1)}, u32[]{:S(2)}) copy-start(bf16[3,3,3,64,64]{4,3,2,1,0:T(8,128)(2,1)} %param.10) | copy-start | bytes 663556
  0.0 1.0 %copy-start.1 = (bf16[64,16,128]{2,1,0:T(8,128)(2,1)S(1)}, bf16[64,16,128]{2,1,0:T(8,128)(2,1)}, u32[]{:S(2)}) copy-start(bf16[64,16,128]{2,1,0:T(8,128)(2,1)} %x_ref.1) | copy-start | bytes 786436
  1.2 4.1 %collective-permute-start = (bf16[2,64,128]{2,1,0:T(8,128)(2,1)S(1)}, bf16[2,64,128]{2,1,0:T(8,128)(2,1)S(1)}, u32[]{:S(2)}, u32[]{:S(2)}) collective-permute-start(bf16[2,64,128]{2,1,0:T(8,128)(2,1)S(1)} %get-tuple-element.25), channel_id=1, source_target_pairs={{0,16},{32,48},{64,80},{96,112},{128,144},{160,176},{192,208},{224... | collective-permute-start | bytes 98312 | tf_op jit(solution)/shard_map/ppermute | solution.py:327
  3.1 6.4 %collective-permute-start.1 = (bf16[2,64,128]{2,1,0:T(8,128)(2,1)S(1)}, bf16[2,64,128]{2,1,0:T(8,128)(2,1)S(1)}, u32[]{:S(2)}, u32[]{:S(2)}) collective-permute-start(bf16[2,64,128]{2,1,0:T(8,128)(2,1)S(1)} %get-tuple-element.26), channel_id=1, source_target_pairs={{16,32},{48,64},{80,96},{112,128},{144,160},{176,192},{208,224},{2... | collective-permute-start | bytes 98312 | tf_op jit(solution)/shard_map/ppermute | solution.py:327
  9.6 5.2 %copy-start.5 = (bf16[64,512]{1,0:T(8,128)(2,1)S(1)}, bf16[64,512]{1,0:T(8,128)(2,1)}, u32[]{:S(2)}) copy-start(bf16[64,512]{1,0:T(8,128)(2,1)} %proj_ref.1) | copy-start | bytes 196612
  9.8 7.3 %collective-permute-start.2 = (bf16[5,64,128]{2,1,0:T(8,128)(2,1)S(1)}, bf16[5,64,128]{2,1,0:T(8,128)(2,1)S(1)}, u32[]{:S(2)}, u32[]{:S(2)}) collective-permute-start(bf16[5,64,128]{2,1,0:T(8,128)(2,1)S(1)} %get-tuple-element.30), channel_id=1, source_target_pairs={{0,1},{2,3},{4,5},{6,7},{8,9},{10,11},{12,13},{14,15},{1,0},{3,2},... | collective-permute-start | bytes 245768 | tf_op jit(solution)/shard_map/ppermute | solution.py:327
  13.3 3.8 %collective-permute-start.3 = (bf16[5,64,128]{2,1,0:T(8,128)(2,1)S(1)}, bf16[5,64,128]{2,1,0:T(8,128)(2,1)S(1)}, u32[]{:S(2)}, u32[]{:S(2)}) collective-permute-start(bf16[5,64,128]{2,1,0:T(8,128)(2,1)S(1)} %get-tuple-element.31), channel_id=1, source_target_pairs={{1,2},{3,4},{5,6},{7,8},{9,10},{11,12},{13,14},{2,1},{4,3},{6,5},{... | collective-permute-start | bytes 245768 | tf_op jit(solution)/shard_map/ppermute | solution.py:327
  14.0 0.7 %copy-start.2 = (f32[64]{0:T(128)S(1)}, f32[64]{0:T(128)}, u32[]{:S(2)}) copy-start(f32[64]{0:T(128)} %param.11) | copy-start | bytes 772
  14.0 1.0 %copy-start.4 = (bf16[3,3,3,64,64]{4,3,2,1,0:T(8,128)(2,1)S(1)}, bf16[3,3,3,64,64]{4,3,2,1,0:T(8,128)(2,1)}, u32[]{:S(2)}) copy-start(bf16[3,3,3,64,64]{4,3,2,1,0:T(8,128)(2,1)} %param.16) | copy-start | bytes 663556
  14.6 0.7 %copy-start.6 = (bf16[32,64]{1,0:T(8,128)(2,1)S(1)}, bf16[32,64]{1,0:T(8,128)(2,1)}, u32[]{:S(2)}) copy-start(bf16[32,64]{1,0:T(8,128)(2,1)} %ow_ref.1) | copy-start | bytes 12292
  14.8 0.7 %copy-start.7 = (f32[64]{0:T(128)S(1)}, f32[64]{0:T(128)}, u32[]{:S(2)}) copy-start(f32[64]{0:T(128)} %param.17) | copy-start | bytes 772
  14.8 0.7 %copy-start.8 = (f32[32]{0:T(128)S(1)}, f32[32]{0:T(128)}, u32[]{:S(2)}) copy-start(f32[32]{0:T(128)} %param.14) | copy-start | bytes 388
  15.5 1.2 %copy-start.3 = (bf16[3,3,3,32,512]{4,3,2,1,0:T(8,128)(2,1)S(1)}, bf16[3,3,3,32,512]{4,3,2,1,0:T(8,128)(2,1)}, u32[]{:S(2)}) copy-start(bf16[3,3,3,32,512]{4,3,2,1,0:T(8,128)(2,1)} %param.13) | copy-start | bytes 2654212
  19.8 5.9 %collective-permute-start.4 = (f32[8,128]{1,0:T(8,128)S(1)}, f32[8,128]{1,0:T(8,128)S(1)}, u32[]{:S(2)}, u32[]{:S(2)}) collective-permute-start(f32[8,128]{1,0:T(8,128)S(1)} %get-tuple-element.34.own_ref), channel_id=1, source_target_pairs={{0,16},{32,48},{64,80},{96,112},{128,144},{160,176},{192,208},{224... | collective-permute-start | bytes 12296 | tf_op jit(solution)/shard_map/ppermute | solution.py:327
  21.8 6.1 %collective-permute-start.5 = (f32[8,128]{1,0:T(8,128)S(1)}, f32[8,128]{1,0:T(8,128)S(1)}, u32[]{:S(2)}, u32[]{:S(2)}) collective-permute-start(f32[8,128]{1,0:T(8,128)S(1)} %get-tuple-element.34.own_ref), channel_id=1, source_target_pairs={{16,32},{48,64},{80,96},{112,128},{144,160},{176,192},{208,224},{2... | collective-permute-start | bytes 12296 | tf_op jit(solution)/shard_map/ppermute | solution.py:327

commit v3 on v2

v3 whole, which is shorter than its diff:
```python
import jax
import jax.numpy as jnp
from jax import lax
from jax.experimental import pallas as pl
from jax.experimental.pallas import tpu as pltpu
from jax.sharding import PartitionSpec as P


F32 = jnp.float32
BF = jnp.bfloat16
C = 64
NSX = 32
NSY = 16


def call(kernel, outs, *ins, scratch=(), flops=1000000, limit=16, in_space=pltpu.VMEM, out_space=pltpu.VMEM):
    return pl.pallas_call(
        kernel,
        out_shape=outs,
        in_specs=[pl.BlockSpec(memory_space=in_space)] * len(ins),
        out_specs=jax.tree.map(lambda _: pl.BlockSpec(memory_space=out_space), outs),
        scratch_shapes=list(scratch),
        compiler_params=pltpu.CompilerParams(vmem_limit_bytes=limit * 2**20),
        cost_estimate=pl.CostEstimate(flops=flops, transcendentals=0, bytes_accessed=100000),
    )(*ins)


def S(shape, dtype):
    return jax.ShapeDtypeStruct(shape, dtype)


def dot(a, b):
    return jnp.dot(a, b, preferred_element_type=F32)


def dot_nt(a, b):
    return lax.dot_general(a, b, (((1,), (1,)), ((), ())), preferred_element_type=F32)


def lanes_of(rows):
    return lax.broadcasted_iota(jnp.int32, (rows, 128), 1)


def roll(v, shift):
    shift = shift % 128
    return v if shift == 0 else pltpu.roll(v, shift, 1)


def even_of(axis):
    return lax.rem(lax.axis_index(axis), 2) == 0


def k_features(x_ref, ft_ref, inner_ref, outer_ref, buf):
    buf[...] = x_ref[...].reshape(C * 16, 128).astype(F32)
    even = even_of("sx")

    def row(x):
        return buf[pl.ds(x, C, stride=16), :]

    for k in range(2):
        low, high = row(k), row(14 + k)
        inner_ref[k] = jnp.where(even, high, low).astype(BF)
        outer_ref[k] = jnp.where(even, low, high).astype(BF)
    for x in range(16):
        ft_ref[x + 2] = row(x).astype(BF)


def k_faces(inner_ref, outer_ref, ft_ref, x_ref, left_ref, right_ref, s_inner_ref, s_outer_ref):
    lane = lanes_of(C)
    even_x, even_y = even_of("sx"), even_of("sy")
    for k in range(2):
        inner, outer = inner_ref[k], outer_ref[k]
        x_ref[k] = jnp.where(even_x, outer, inner)
        x_ref[2 + k] = jnp.where(even_x, inner, outer)
    for g in range(5):
        left = None
        for q in range(4):
            r = 4 * g + q
            v = x_ref[r] if r < 2 else ft_ref[r] if r < 18 else x_ref[r - 16]
            v = v.astype(F32)
            a, b = roll(v, 32 * q), roll(v, 32 * q - 96)
            if q == 0:
                left, right = a, b
            else:
                here = lane >= 32 * q
                left, right = jnp.where(here, a, left), jnp.where(here, b, right)
        left_ref[g] = left.astype(BF)
        right_ref[g] = right.astype(BF)
        s_inner_ref[g] = jnp.where(even_y, right, left).astype(BF)
        s_outer_ref[g] = jnp.where(even_y, left, right).astype(BF)


def arranged(w_ref, out_ref, taps):
    for a in range(3):
        for at in range(0, len(taps), 2):
            blocks = [w_ref[a * 9 + t] for t in taps[at : at + 2]]
            wide = blocks[0] if len(blocks) == 1 else jnp.concatenate(blocks, axis=1)
            out_ref[pl.ds(a * C, C), pl.ds(C * at, wide.shape[1])] = wide


def column(b_ref):
    row = jnp.broadcast_to(b_ref[...], (C, C))
    same = lax.broadcasted_iota(jnp.int32, (C, C), 0) == lax.broadcasted_iota(jnp.int32, (C, C), 1)
    return jnp.broadcast_to(jnp.sum(jnp.where(same, row, 0.0), axis=1, keepdims=True), (C, 128))


def interp_weight(g, cell, count, cells):
    num = 2 * g - 7
    low = jnp.right_shift(num, 4)
    w = (num - 16 * low).astype(F32) * (1.0 / 16.0)
    w = jnp.where((low < 0) | (low >= cells - 1), 0.0, w)
    low = jnp.clip(low, 0, cells - 1)
    value = jnp.where(cell == low, 1.0 - w, jnp.where(cell == low + 1, w, 0.0))
    return jnp.where((g >= 0) & (g < count), value, 0.0)


def k_weights(*refs):
    hbm, outs, held, sem = refs[:8], refs[8:17], refs[17:25], refs[25]
    copies = [pltpu.make_async_copy(h, v, sem.at[i]) for i, (h, v) in enumerate(zip(hbm, held))]
    for c in copies:
        c.start()
    ew, eb, dw, db, bw, proj, ow, bb = held
    we_ref, wedge_ref, be_ref, wd_ref, bd_ref, vt_ref, ow2_ref, bb2_ref, s_ref = outs
    j = lax.axis_index("sy")
    row = lax.broadcasted_iota(jnp.int32, (32, 128), 0)
    lane = lax.broadcasted_iota(jnp.int32, (32, 128), 1)
    y, z = jnp.right_shift(lane, 4), jnp.bitwise_and(lane, 15)
    cell_y = j - 1 + jnp.right_shift(row, 3)
    zero = jnp.zeros((96, 128), BF)
    for b in range(3):
        wy = interp_weight(8 * j + y + (b - 1), cell_y, 8 * NSY, NSY)
        wy = jnp.where(row < 24, wy, 0.0)
        for c in range(3):
            for zo in range(2):
                wz = interp_weight(z + (c - 1), 1 - zo, 16, 2)
                at = pl.ds(128 * (3 * b + c), 128)
                s_ref[pl.ds(128 * zo, 32), at] = (wy * wz).astype(BF)
                s_ref[pl.ds(128 * zo + 32, 96), at] = zero
    for c in copies:
        c.wait()
    arranged(ew, we_ref, range(9))
    arranged(ew, wedge_ref, (0, 1, 2, 6, 7, 8))
    arranged(dw, wd_ref, range(9))
    be_ref[...] = column(eb)
    bd_ref[...] = column(db)
    p = proj[...]
    r = dot_nt(bw[...], jnp.concatenate([p, p], axis=0))
    half = lanes_of(C) < C
    for ab in range(9):
        both = jnp.where(half, r[96 * ab : 96 * ab + 64], r[96 * ab + 32 : 96 * ab + 96])
        vt_ref[:, pl.ds(128 * ab, 128)] = both.astype(BF)
    o = ow[...]
    none = jnp.zeros_like(o)
    ow2_ref[...] = jnp.concatenate([jnp.concatenate([o, none], axis=1), jnp.concatenate([none, o], axis=1)], axis=0)
    bb2_ref[...] = jnp.concatenate([bb[...], bb[...]], axis=1)


def taps_of(v, z):
    zero = jnp.zeros_like(v)
    return [jnp.where(z == 0, zero, roll(v, 1)), v, jnp.where(z == 15, zero, roll(v, -1))]


def put_taps(parts, xm, n, z):
    for b, v in enumerate(parts):
        for c, tap in enumerate(taps_of(v, z)):
            xm[n, 3 * b + c, pl.ds(0, C), :] = tap


def products(w_ref, xm, first, last, store):
    w = w_ref[...]

    def block(n):
        return jnp.concatenate([xm[n, t, pl.ds(0, C), :] for t in range(9)], axis=0)

    for n in range(first, last, 2):
        if n + 1 < last:
            g = dot(w, jnp.concatenate([block(n), block(n + 1)], axis=1))
            store(n, g[:, :128])
            store(n + 1, g[:, 128:])
        else:
            store(n, dot(w, block(n)))


def into(g_ref):
    def store(n, g):
        g_ref[n, pl.ds(0, 3 * C), :] = g

    return store


def summed(g_ref, r):
    return g_ref[r, pl.ds(0, C), :] + g_ref[r + 1, pl.ds(C, C), :] + g_ref[r + 2, pl.ds(2 * C, C), :]


def summed_packed(packed, g, lane):
    v = packed[g][:C]
    for a in (1, 2):
        this, after = packed[g][a * C : a * C + C], packed[min(g + 1, 4)][a * C : a * C + C]
        v = v + roll(jnp.where(lane < 32 * a, after, this), -32 * a)
    return v


def packed_products(w, blocks):
    out = []
    for n in range(0, 5, 2):
        if n + 1 < 5:
            g = dot(w, jnp.concatenate([blocks[n], blocks[n + 1]], axis=1))
            out += [g[:, :128], g[:, 128:]]
        else:
            out.append(dot(w, blocks[n]))
    return out


def y_halos(inner_ref, outer_ref, g):
    even_y = even_of("sy")
    inner, outer = inner_ref[g], outer_ref[g]
    return jnp.where(even_y, outer, inner), jnp.where(even_y, inner, outer)


def k_interior(ft_ref, x_ref, w_ref, g_ref, xm):
    lane = lanes_of(C)
    z = jnp.bitwise_and(lane, 15)
    for r in range(20):
        v = x_ref[r] if r < 2 else ft_ref[r] if r < 18 else x_ref[r - 16]
        zero = jnp.zeros_like(v)
        put_taps(
            [jnp.where(lane < 16, zero, roll(v, 16)), v, jnp.where(lane >= 112, zero, roll(v, -16))], xm, r, z
        )
    products(w_ref, xm, 0, 20, into(g_ref))


def k_encode(g_ref, inner_ref, outer_ref, w_ref, bias_ref, em_ref, pool_ref):
    lane = lanes_of(C)
    z = jnp.bitwise_and(lane, 15)
    even = jnp.bitwise_and(lane, 16) == 0
    edge = (lane < 16) | (lane >= 112)
    s = lax.axis_index("sx")
    blocks = []
    for g in range(5):
        hl, hr = y_halos(inner_ref, outer_ref, g)
        zero = jnp.zeros_like(hl)
        low, high = jnp.where(even, zero, hl), jnp.where(even, hr, zero)
        blocks.append(jnp.concatenate(taps_of(low, z) + taps_of(high, z), axis=0))
    packed = packed_products(w_ref[...], blocks)
    bias = bias_ref[...]
    best = [None, None]
    for r in range(18):
        if r % 4 == 0:
            at_edge = summed_packed(packed, r // 4, lane)
        v = summed(g_ref, r) + bias
        v = v + jnp.where(edge, roll(at_edge, -(32 * (r % 4) + 16)), 0.0)
        v = jnp.maximum(v, 0.0)
        if r == 0:
            v = jnp.where(s == 0, 0.0, v)
        if r == 17:
            v = jnp.where(s == NSX - 1, 0.0, v)
        em_ref[r] = v.astype(BF)
        if 1 <= r <= 16:
            cell = (r - 1) // 8
            best[cell] = v if best[cell] is None else jnp.maximum(best[cell], v)
    for cell in range(2):
        m = best[cell].astype(BF).astype(F32)
        for shift in (64, 32, 16, -1, -2, -4):
            m = jnp.maximum(m, roll(m, shift))
        best[cell] = m
    first = lane == 0
    both = [jnp.where(first, best[0], roll(best[1], 1)), jnp.where(first, roll(best[0], -8), roll(best[1], -7))]
    pool_ref[...] = jnp.transpose(jnp.concatenate(both, axis=0))[:8]


def k_decode(
    fl_ref, fr_ref, inner_ref, outer_ref, em_ref, we_ref, be_ref, w_ref, bias_ref, d_ref, xm, g_ref
):
    lane = lanes_of(C)
    z = jnp.bitwise_and(lane, 15)
    even = jnp.bitwise_and(lane, 16) == 0
    s, j = lax.axis_index("sx"), lax.axis_index("sy")
    blocks = []
    for g in range(5):
        hl, hr = y_halos(inner_ref, outer_ref, g)
        fl, fr = fl_ref[g], fr_ref[g]
        parts = [
            jnp.where(even, roll(fr, -16), roll(hl, 16)),
            jnp.where(even, hr, hl),
            jnp.where(even, roll(hr, -16), roll(fl, 16)),
        ]
        blocks.append(jnp.concatenate([tap for v in parts for tap in taps_of(v, z)], axis=0))
    packed = packed_products(we_ref[...], blocks)
    outside = (even & (j == NSY - 1)) | (~even & (j == 0))
    halo = []
    for g in range(5):
        v = summed_packed(packed, g, lane) + be_ref[...]
        v = jnp.where(outside, 0.0, jnp.maximum(v, 0.0))
        if g == 0:
            v = jnp.where((lane < 32) & (s == 0), 0.0, v)
        if g == 4:
            v = jnp.where((lane >= 64) | ((lane >= 32) & (s == NSX - 1)), 0.0, v)
        halo.append(v.astype(BF))
    for r in range(18):
        v = em_ref[r]
        beside = roll(halo[r // 4], -(32 * (r % 4) + 16))
        put_taps(
            [jnp.where(lane < 16, beside, roll(v, 16)), v, jnp.where(lane >= 112, beside, roll(v, -16))], xm, r, z
        )
    products(w_ref, xm, 0, 18, into(g_ref))
    bias = bias_ref[...]
    for x in range(16):
        d_ref[x] = summed(g_ref, x) + bias


def k_message(inner_ref, own_ref, outer_ref, _d, out_ref):
    even = even_of("sx")
    inner, outer = inner_ref[0:2], outer_ref[0:2]
    left, right = jnp.where(even, outer, inner), jnp.where(even, inner, outer)
    message = jnp.concatenate([left, own_ref[0:2], right, jnp.zeros((2, 128), F32)], axis=0)
    for i in range(NSY):
        out_ref[i] = message


def k_bottleneck(p_ref, vt_ref, bb_ref, ow_ref, out_ref):
    p = p_ref[...]
    pieces = []
    none = jnp.zeros((1, 8, 128), F32)
    for a in range(3):
        moved = p if a == 0 else jnp.concatenate([p[:, a:], p[:, :a]], axis=1)
        for b in range(3):
            if b == 0:
                v = jnp.concatenate([none, moved[:-1]], axis=0)
            elif b == 1:
                v = moved
            else:
                v = jnp.concatenate([moved[1:], none], axis=0)
            pieces.append(v.reshape(128, 128).astype(BF))
    h = dot_nt(jnp.concatenate(pieces, axis=1), vt_ref[...])
    h = jnp.maximum(h + bb_ref[...], 0.0).astype(BF)
    low = dot(h, ow_ref[...]).astype(BF).astype(F32)
    zero = jnp.zeros((8, 128), F32)
    for i in range(NSY):
        before = low[8 * (i - 1) : 8 * i] if i else zero
        after = low[8 * (i + 1) : 8 * (i + 2)] if i < NSY - 1 else zero
        out_ref[i] = jnp.concatenate([before, low[8 * i : 8 * i + 8], after], axis=0).astype(BF)


def k_final(parts_ref, s_ref, w_ref, d_ref, out_ref, xt, q_ref, buf, done, sem):
    total = parts_ref[0].astype(F32)
    for i in range(1, NSY):
        total = total + parts_ref[i].astype(F32)
    total = jnp.concatenate([total, jnp.zeros((104, 128), F32)], axis=0)
    lt = jnp.transpose(total)
    lane = lanes_of(C)
    left = []
    for cell in range(4):
        here = jnp.bitwise_and(lane, 7) == cell
        left.append(jnp.concatenate([jnp.where(here, lt[:C], 0.0), jnp.where(here, lt[C:], 0.0)], axis=1).astype(BF))
    t = dot(jnp.concatenate(left, axis=0), s_ref[...])
    for cell in range(4):
        for bc in range(9):
            xt[cell, bc, pl.ds(0, C), :] = t[C * cell : C * cell + C, 128 * bc : 128 * bc + 128].astype(BF)
    products(w_ref, xt, 0, 4, into(q_ref))
    s = lax.axis_index("sx")
    first, last = s == 0, s == NSX - 1
    copies = []
    for part in range(4):
        rows = 16
        for x in range(16):
            v = d_ref[x, pl.ds(rows * part, rows), :]
            for a in range(3):
                g = x + a - 1
                num = 2 * g - 7
                low = num // 16
                high = (num - 16 * low) / 16.0
                cell = low + 1
                w_low, w_high = jnp.float32(1.0 - high), jnp.float32(high)
                if cell == 0:
                    w_low = jnp.where(first, 0.0, w_low)
                    w_high = jnp.where(first, 0.0 if g < 0 else 1.0, w_high)
                if cell == 2:
                    w_low = jnp.where(last, 0.0 if g > 15 else 1.0, w_low)
                    w_high = jnp.where(last, 0.0, w_high)
                at = pl.ds(C * a + rows * part, rows)
                v = v + w_low * q_ref[cell, at, :]
                v = v + w_high * q_ref[cell + 1, at, :]
            buf[part, pl.ds(x, rows, stride=16), :] = v
        at = pl.ds(rows * part, rows)
        done[at] = buf[part].reshape(rows, 16, 128).astype(BF)
        copy = pltpu.make_async_copy(done.at[at], out_ref.at[at], sem.at[part])
        copy.start()
        copies.append(copy)
    for copy in copies:
        copy.wait()


def swapped(v, axis, start):
    size = lax.axis_size(axis)
    low = range(start, size - 1, 2)
    return lax.ppermute(v, axis, [(i, i + 1) for i in low] + [(i + 1, i) for i in low])


def per_device(features, enc_weight, enc_bias, proj_weight, bottle_weight, bottle_bias, out_weight, dec_weight, dec_bias):
    ft, inner, outer = call(
        k_features,
        (S((18, C, 128), BF), S((2, C, 128), BF), S((2, C, 128), BF)),
        features,
        scratch=[pltpu.VMEM((C * 16, 128), F32)],
    )
    outer, inner = swapped(outer, "sx", 1), swapped(inner, "sx", 0)
    sources = (
        enc_weight.reshape(27, C, C),
        enc_bias.reshape(1, C),
        dec_weight.reshape(27, C, C),
        dec_bias.reshape(1, C),
        bottle_weight.reshape(27 * 32, 512),
        proj_weight,
        out_weight,
        bottle_bias.reshape(1, 32),
    )
    sources = tuple(pltpu.with_memory_space_constraint(v, pltpu.HBM) for v in sources)
    we, wedge, be, wd, bd, vt, ow2, bb2, smat = call(
        k_weights,
        (
            S((3 * C, 9 * C), BF),
            S((3 * C, 6 * C), BF),
            S((C, 128), F32),
            S((3 * C, 9 * C), BF),
            S((C, 128), F32),
            S((C, 9 * 128), BF),
            S((C, 128), BF),
            S((1, C), F32),
            S((256, 9 * 128), BF),
        ),
        *sources,
        scratch=[pltpu.VMEM(v.shape, v.dtype) for v in sources] + [pltpu.SemaphoreType.DMA((8,))],
        flops=4 * 10**8,
        in_space=pltpu.HBM,
    )
    xh, fl, fr, inner, outer = call(k_faces, (S((4, C, 128), BF),) + (S((5, C, 128), BF),) * 4, inner, outer, ft)
    outer, inner = swapped(outer, "sy", 1), swapped(inner, "sy", 0)
    product = call(
        k_interior,
        S((20, 3 * C + 8, 128), F32),
        ft,
        xh,
        we,
        scratch=[pltpu.VMEM((20, 9, C + 16, 128), BF)],
        flops=4 * 10**8,
    )
    em, pooled = call(k_encode, (S((18, C, 128), BF), S((8, 128), F32)), product, inner, outer, wedge, be)
    p_outer, p_inner = swapped(pooled, "sx", 1), swapped(pooled, "sx", 0)
    d = call(
        k_decode,
        S((16, C, 128), F32),
        fl,
        fr,
        inner,
        outer,
        em,
        we,
        be,
        wd,
        bd,
        scratch=[pltpu.VMEM((18, 9, C + 16, 128), BF), pltpu.VMEM((18, 3 * C + 8, 128), F32)],
        flops=4 * 10**8,
    )
    message = call(k_message, S((NSY, 8, 128), F32), p_inner, pooled, p_outer, d)
    everyone = lax.all_to_all(message, "sy", 0, 0, tiled=True)
    partial = call(k_bottleneck, S((NSY, 24, 128), BF), everyone, vt, bb2, ow2)
    parts = lax.all_to_all(partial, "sy", 0, 0, tiled=True)
    return call(
        k_final,
        S((C, 16, 128), BF),
        parts,
        smat,
        wd,
        d,
        scratch=[
            pltpu.VMEM((4, 9, C + 16, 128), BF),
            pltpu.VMEM((4, 3 * C + 8, 128), F32),
            pltpu.VMEM((4, 256, 128), F32),
            pltpu.VMEM((C, 16, 128), BF),
            pltpu.SemaphoreType.DMA((4,)),
        ],
        out_space=pltpu.HBM,
    )


def solution(mesh):
    in_specs = (P(None, "sx", "sy"), P(), P(), P(), P(None, None, None, "sy", None), P("sy"), P("sy", None), P(), P())

    return jax.shard_map(per_device, mesh=mesh, in_specs=in_specs, out_specs=P(None, "sx", "sy"), check_vma=False)
```

time: 59.5 us -> 59.1 us (level)
  the two profiles are of different devices: /device:TPU:256 before, /device:TPU:96 now
where the time goes in v3:
time: 59.1 us; the launch traced here: 58.8 us
  blocking collectives  28.6 us (48%)
  starting transfers between devices  16.5 us (28%)
  Pallas kernels  9.53 us (16%)
  waiting for transfers between devices  3.11 us (5%)
  local copies, waits for them, and re-layouts  0.95 us (2%)
    all_to_all x1, blocking collectives, per_device(): everyone = lax.all_to_all(message, 'sy', 0, 0, tiled=True)  17.6 us
    ppermute x6, starting transfers between devices, swapped(): lax.ppermute(v, axis, [(i, i + 1) for i in low] + [(i + 1, i) for i in low])  16.5 us
    all_to_all x1, blocking collectives, per_device(): parts = lax.all_to_all(partial, 'sy', 0, 0, tiled=True)  11 us
    pallas_call x9, Pallas kernels, call(): pl.pallas_call(kernel, out_shape=outs, in_specs=[pl.BlockSpec(memory_spac...  9.53 us
    ppermute x6, waiting for transfers between devices, swapped(): lax.ppermute(v, axis, [(i, i + 1) for i in low] + [(i + 1, i) for i in low])  3.11 us
  transfers between devices with their start and end apart: 6, of which 1 were waited for; matrix products, arithmetic and copies ran while one was open for 0% of the time, Pallas kernels for 10%

profile of v3, /device:TPU:96, one launch (start us, length us, event | category | flops | bytes accessed | tf_op | source)
XLA Modules:
  0.0 58.8 jit_solution(14792848947518417743)
XLA Ops:
  0.0 0.0 copy-start
  0.0 0.9 %copy-done = bf16[64,16,128]{2,1,0:T(8,128)(2,1)S(1)} copy-done((bf16[64,16,128]{2,1,0:T(8,128)(2,1)S(1)}, bf16[64,16,128]{2,1,0:T(8,128)(2,1)}, u32[]{:S(2)}) %copy-start) | copy-done | bytes 262168
  1.0 0.2 shard_map.91
  1.2 1.9 %collective-permute-start = (bf16[2,64,128]{2,1,0:T(8,128)(2,1)S(1)}, bf16[2,64,128]{2,1,0:T(8,128)(2,1)S(1)}, u32[]{:S(2)}, u32[]{:S(2)}) collective-permute-start(bf16[2,64,128]{2,1,0:T(8,128)(2,1)S(1)} %get-tuple-element.25), channel_id=1, source_target_pairs={{0,16},{32,48},{64,80},{96,112},{128,144},{160,176},{192,208},{224... | collective-permute-start | bytes 98312 | tf_op jit(solution)/shard_map/ppermute | solution.py:396
  3.1 2.1 %collective-permute-start.1 = (bf16[2,64,128]{2,1,0:T(8,128)(2,1)S(1)}, bf16[2,64,128]{2,1,0:T(8,128)(2,1)S(1)}, u32[]{:S(2)}, u32[]{:S(2)}) collective-permute-start(bf16[2,64,128]{2,1,0:T(8,128)(2,1)S(1)} %get-tuple-element.26), channel_id=1, source_target_pairs={{16,32},{48,64},{80,96},{112,128},{144,160},{176,192},{208,224},{2... | collective-permute-start | bytes 98312 | tf_op jit(solution)/shard_map/ppermute | solution.py:396
  5.2 0.0 collective-permute-done.inner_ref
  5.2 3.1 %collective-permute-done.1.outer_ref = bf16[2,64,128]{2,1,0:T(8,128)(2,1)S(1)} collective-permute-done((bf16[2,64,128]{2,1,0:T(8,128)(2,1)S(1)}, bf16[2,64,128]{2,1,0:T(8,128)(2,1)S(1)}, u32[]{:S(2)}, u32[]{:S(2)}) %collective-permute-start.1) | collective-permute-done | bytes 32800 | tf_op jit(solution)/shard_map/ppermute | solution.py:396
  8.3 0.2 shard_map.92
  8.5 3.5 %collective-permute-start.2 = (bf16[5,64,128]{2,1,0:T(8,128)(2,1)S(1)}, bf16[5,64,128]{2,1,0:T(8,128)(2,1)S(1)}, u32[]{:S(2)}, u32[]{:S(2)}) collective-permute-start(bf16[5,64,128]{2,1,0:T(8,128)(2,1)S(1)} %get-tuple-element.29), channel_id=1, source_target_pairs={{0,1},{2,3},{4,5},{6,7},{8,9},{10,11},{12,13},{14,15},{1,0},{3,2},... | collective-permute-start | bytes 245768 | tf_op jit(solution)/shard_map/ppermute | solution.py:396
  12.0 0.7 %collective-permute-start.3 = (bf16[5,64,128]{2,1,0:T(8,128)(2,1)S(1)}, bf16[5,64,128]{2,1,0:T(8,128)(2,1)S(1)}, u32[]{:S(2)}, u32[]{:S(2)}) collective-permute-start(bf16[5,64,128]{2,1,0:T(8,128)(2,1)S(1)} %get-tuple-element.30), channel_id=1, source_target_pairs={{1,2},{3,4},{5,6},{7,8},{9,10},{11,12},{13,14},{2,1},{4,3},{6,5},{... | collective-permute-start | bytes 245768 | tf_op jit(solution)/shard_map/ppermute | solution.py:396
  12.7 2.0 %shard_map.93 = (bf16[192,576]{1,0:T(8,128)(2,1)S(1)}, bf16[192,384]{1,0:T(8,128)(2,1)S(1)}, f32[64,128]{1,0:T(8,128)S(1)}, bf16[192,576]{1,0:T(8,128)(2,1)S(1)}...) custom-call(bf16[27,64,64]{2,1,0:T(8,128)(2,1)} %bitcast.7, ...), custom_call_target="tpu_custom_call" | custom-call | flops 400000000 | bytes 100000 | tf_op jit(solution)/shard_map/pallas_call | solution.py:17
  14.7 1.6 %shard_map.94.g_ref = f32[20,200,128]{2,1,0:T(8,128)S(1)} custom-call(bf16[18,64,128]{2,1,0:T(8,128)(2,1)S(1)} %get-tuple-element.24.ft_ref, bf16[4,64,128]{2,1,0:T(8,128)(2,1)S(1)} %get-tuple-element.27.x_ref, bf16[192,576]{1,0:T(8,128)(2,1)S(1)} %get-tuple-element.28.w_ref.we_ref), custom_call_target="tpu_custom_call" | custom-call | flops 400000000 | bytes 100000 | tf_op jit(solution)/shard_map/pallas_call | solution.py:17
  16.3 0.0 collective-permute-done.2.inner_ref
  16.3 0.0 collective-permute-done.3.outer_ref
  16.4 1.2 %shard_map.95 = (bf16[18,64,128]{2,1,0:T(8,128)(2,1)S(1)}, f32[8,128]{1,0:T(8,128)S(1)}) custom-call(f32[20,200,128]{2,1,0:T(8,128)S(1)} %shard_map.94.g_ref, bf16[5,64,128]{2,1,0:T(8,128)(2,1)S(1)} %collective-permute-done.2.inner_ref, bf16[5,64,128]{2,1,0:T(8,128)(2,1)S(1)} %collective-permute-done.3.outer_ref, ...), custom_call_target="tpu_custom_call" | custom-call | flops 1000000 | bytes 100000 | tf_op jit(solution)/shard_map/pallas_call | solution.py:17
  17.5 1.9 %collective-permute-start.5 = (f32[8,128]{1,0:T(8,128)S(1)}, f32[8,128]{1,0:T(8,128)S(1)}, u32[]{:S(2)}, u32[]{:S(2)}) collective-permute-start(f32[8,128]{1,0:T(8,128)S(1)} %get-tuple-element.33.own_ref), channel_id=1, source_target_pairs={{16,32},{48,64},{80,96},{112,128},{144,160},{176,192},{208,224},{2... | collective-permute-start | bytes 12296 | tf_op jit(solution)/shard_map/ppermute | solution.py:396
  19.5 6.3 %collective-permute-start.4 = (f32[8,128]{1,0:T(8,128)S(1)}, f32[8,128]{1,0:T(8,128)S(1)}, u32[]{:S(2)}, u32[]{:S(2)}) collective-permute-start(f32[8,128]{1,0:T(8,128)S(1)} %get-tuple-element.33.own_ref), channel_id=1, source_target_pairs={{0,16},{32,48},{64,80},{96,112},{128,144},{160,176},{192,208},{224... | collective-permute-start | bytes 12296 | tf_op jit(solution)/shard_map/ppermute | solution.py:396
  25.8 2.4 %shard_map.96._d.d_ref = f32[16,64,128]{2,1,0:T(8,128)S(1)} custom-call(bf16[5,64,128]{2,1,0:T(8,128)(2,1)S(1)} %get-tuple-element.34.fl_ref, bf16[5,64,128]{2,1,0:T(8,128)(2,1)S(1)} %get-tuple-element.35.fr_ref, bf16[5,64,128]{2,1,0:T(8,128)(2,1)S(1)} %collective-permute-done.2.inner_ref, bf16[5,64,128]{2,1,0:T(8,128)(2,1)S(1)} %collective-permute-done.3.outer_ref, ...), custom_call_target="tpu_custom_call" | custom-call | flops 400000000 | bytes 100000 | tf_op jit(solution)/shard_map/pallas_call | solution.py:17
  28.2 0.0 collective-permute-done.5.outer_ref
  28.2 0.0 collective-permute-done.4.inner_ref
  28.2 17.6 %all_to_all.10.p_ref = f32[16,8,128]{2,1,0:T(8,128)S(1)} all-to-all(f32[16,8,128]{2,1,0:T(8,128)S(1)} %shard_map.97), channel_id=1, replica_groups=mesh['sx'=32,'sy'=16] {'sy'}, dimensions={0} | all-to-all | bytes 131072 | tf_op jit(solution)/shard_map/all_to_all | solution.py:465
  45.8 0.3 shard_map.98
  46.2 11.0 %all_to_all.11.parts_ref = bf16[16,24,128]{2,1,0:T(8,128)(2,1)S(1)} all-to-all(bf16[16,24,128]{2,1,0:T(8,128)(2,1)S(1)} %shard_map.98), channel_id=1, replica_groups=mesh['sx'=32,'sy'=16] {'sy'}, dimensions={0} | all-to-all | bytes 196608 | tf_op jit(solution)/shard_map/all_to_all | solution.py:467
  57.2 1.6 %shard_map.99 = bf16[64,16,128]{2,1,0:T(8,128)(2,1)} custom-call(bf16[16,24,128]{2,1,0:T(8,128)(2,1)S(1)} %all_to_all.11.parts_ref, bf16[256,1152]{1,0:T(8,128)(2,1)S(1)} %get-tuple-element.42.s_ref, bf16[192,576]{1,0:T(8,128)(2,1)S(1)} %get-tuple-element.37.w_ref, f32[16,64,128]{2,1,0:T(8,128)S(1)} %shard_map.96._d.d_ref), custom_call_target="tpu_custom_call" | custom-call | flops 1000000 | bytes 100000 | tf_op jit(solution)/shard_map/pallas_call | solution.py:17
  (1 shorter events, 0.0 us)
Async XLA Ops:
  0.0 0.9 %copy-start = (bf16[64,16,128]{2,1,0:T(8,128)(2,1)S(1)}, bf16[64,16,128]{2,1,0:T(8,128)(2,1)}, u32[]{:S(2)}) copy-start(bf16[64,16,128]{2,1,0:T(8,128)(2,1)} %x_ref.1) | copy-start | bytes 786436
  1.2 4.1 %collective-permute-start = (bf16[2,64,128]{2,1,0:T(8,128)(2,1)S(1)}, bf16[2,64,128]{2,1,0:T(8,128)(2,1)S(1)}, u32[]{:S(2)}, u32[]{:S(2)}) collective-permute-start(bf16[2,64,128]{2,1,0:T(8,128)(2,1)S(1)} %get-tuple-element.25), channel_id=1, source_target_pairs={{0,16},{32,48},{64,80},{96,112},{128,144},{160,176},{192,208},{224... | collective-permute-start | bytes 98312 | tf_op jit(solution)/shard_map/ppermute | solution.py:396
  3.1 5.2 %collective-permute-start.1 = (bf16[2,64,128]{2,1,0:T(8,128)(2,1)S(1)}, bf16[2,64,128]{2,1,0:T(8,128)(2,1)S(1)}, u32[]{:S(2)}, u32[]{:S(2)}) collective-permute-start(bf16[2,64,128]{2,1,0:T(8,128)(2,1)S(1)} %get-tuple-element.26), channel_id=1, source_target_pairs={{16,32},{48,64},{80,96},{112,128},{144,160},{176,192},{208,224},{2... | collective-permute-start | bytes 98312 | tf_op jit(solution)/shard_map/ppermute | solution.py:396
  8.5 7.8 %collective-permute-start.2 = (bf16[5,64,128]{2,1,0:T(8,128)(2,1)S(1)}, bf16[5,64,128]{2,1,0:T(8,128)(2,1)S(1)}, u32[]{:S(2)}, u32[]{:S(2)}) collective-permute-start(bf16[5,64,128]{2,1,0:T(8,128)(2,1)S(1)} %get-tuple-element.29), channel_id=1, source_target_pairs={{0,1},{2,3},{4,5},{6,7},{8,9},{10,11},{12,13},{14,15},{1,0},{3,2},... | collective-permute-start | bytes 245768 | tf_op jit(solution)/shard_map/ppermute | solution.py:396
  12.0 4.3 %collective-permute-start.3 = (bf16[5,64,128]{2,1,0:T(8,128)(2,1)S(1)}, bf16[5,64,128]{2,1,0:T(8,128)(2,1)S(1)}, u32[]{:S(2)}, u32[]{:S(2)}) collective-permute-start(bf16[5,64,128]{2,1,0:T(8,128)(2,1)S(1)} %get-tuple-element.30), channel_id=1, source_target_pairs={{1,2},{3,4},{5,6},{7,8},{9,10},{11,12},{13,14},{2,1},{4,3},{6,5},{... | collective-permute-start | bytes 245768 | tf_op jit(solution)/shard_map/ppermute | solution.py:396
  17.5 10.7 %collective-permute-start.5 = (f32[8,128]{1,0:T(8,128)S(1)}, f32[8,128]{1,0:T(8,128)S(1)}, u32[]{:S(2)}, u32[]{:S(2)}) collective-permute-start(f32[8,128]{1,0:T(8,128)S(1)} %get-tuple-element.33.own_ref), channel_id=1, source_target_pairs={{16,32},{48,64},{80,96},{112,128},{144,160},{176,192},{208,224},{2... | collective-permute-start | bytes 12296 | tf_op jit(solution)/shard_map/ppermute | solution.py:396
  19.5 8.7 %collective-permute-start.4 = (f32[8,128]{1,0:T(8,128)S(1)}, f32[8,128]{1,0:T(8,128)S(1)}, u32[]{:S(2)}, u32[]{:S(2)}) collective-permute-start(f32[8,128]{1,0:T(8,128)S(1)} %get-tuple-element.33.own_ref), channel_id=1, source_target_pairs={{0,16},{32,48},{64,80},{96,112},{128,144},{160,176},{192,208},{224... | collective-permute-start | bytes 12296 | tf_op jit(solution)/shard_map/ppermute | solution.py:396

commit v4 on v3

--- a/solution.py
+++ b/solution.py
@@ -13,11 +13,12 @@
 NSY = 16
 
 
-def call(kernel, outs, *ins, scratch=(), flops=1000000, limit=16, in_space=pltpu.VMEM, out_space=pltpu.VMEM):
+def call(kernel, outs, *ins, scratch=(), flops=1000000, limit=16, hbm=(), out_space=pltpu.VMEM):
+    ins = [pltpu.with_memory_space_constraint(v, pltpu.HBM) if i in hbm else v for i, v in enumerate(ins)]
     return pl.pallas_call(
         kernel,
         out_shape=outs,
-        in_specs=[pl.BlockSpec(memory_space=in_space)] * len(ins),
+        in_specs=[pl.BlockSpec(memory_space=pltpu.HBM if i in hbm else pltpu.VMEM) for i in range(len(ins))],
         out_specs=jax.tree.map(lambda _: pl.BlockSpec(memory_space=out_space), outs),
         scratch_shapes=list(scratch),
         compiler_params=pltpu.CompilerParams(vmem_limit_bytes=limit * 2**20),
@@ -50,9 +51,18 @@
     return lax.rem(lax.axis_index(axis), 2) == 0
 
 
-def k_features(x_ref, ft_ref, inner_ref, outer_ref, buf):
-    buf[...] = x_ref[...].reshape(C * 16, 128).astype(F32)
+def fetches(sources, targets, sem):
+    copies = [pltpu.make_async_copy(a, b, sem.at[i]) for i, (a, b) in enumerate(zip(sources, targets))]
+    for copy in copies:
+        copy.start()
+    return copies
+
+
+def k_features(x_ref, ew_hbm, eb_hbm, ft_ref, inner_ref, outer_ref, ew_ref, eb_ref, held, buf, sem):
+    copies = fetches((x_ref, ew_hbm, eb_hbm), (held, ew_ref, eb_ref), sem)
     even = even_of("sx")
+    copies[0].wait()
+    buf[...] = held[...].reshape(C * 16, 128).astype(F32)
 
     def row(x):
         return buf[pl.ds(x, C, stride=16), :]
@@ -63,6 +73,8 @@
         outer_ref[k] = jnp.where(even, low, high).astype(BF)
     for x in range(16):
         ft_ref[x + 2] = row(x).astype(BF)
+    for copy in copies[1:]:
+        copy.wait()
 
 
 def k_faces(inner_ref, outer_ref, ft_ref, x_ref, left_ref, right_ref, s_inner_ref, s_outer_ref):
@@ -114,13 +126,13 @@
     return jnp.where((g >= 0) & (g < count), value, 0.0)
 
 
-def k_weights(*refs):
-    hbm, outs, held, sem = refs[:8], refs[8:17], refs[17:25], refs[25]
-    copies = [pltpu.make_async_copy(h, v, sem.at[i]) for i, (h, v) in enumerate(zip(hbm, held))]
-    for c in copies:
-        c.start()
-    ew, eb, dw, db, bw, proj, ow, bb = held
-    we_ref, wedge_ref, be_ref, wd_ref, bd_ref, vt_ref, ow2_ref, bb2_ref, s_ref = outs
+def k_enc_weights(ew, eb, we_ref, wedge_ref, be_ref):
+    arranged(ew, we_ref, range(9))
+    arranged(ew, wedge_ref, (0, 1, 2, 6, 7, 8))
+    be_ref[...] = column(eb)
+
+
+def k_weights(dw, db, bw, proj, ow, bb, wd_ref, bd_ref, vt_ref, ow2_ref, bb2_ref, s_ref):
     j = lax.axis_index("sy")
     row = lax.broadcasted_iota(jnp.int32, (32, 128), 0)
     lane = lax.broadcasted_iota(jnp.int32, (32, 128), 1)
@@ -136,12 +148,7 @@
                 at = pl.ds(128 * (3 * b + c), 128)
                 s_ref[pl.ds(128 * zo, 32), at] = (wy * wz).astype(BF)
                 s_ref[pl.ds(128 * zo + 32, 96), at] = zero
-    for c in copies:
-        c.wait()
-    arranged(ew, we_ref, range(9))
-    arranged(ew, wedge_ref, (0, 1, 2, 6, 7, 8))
     arranged(dw, wd_ref, range(9))
-    be_ref[...] = column(eb)
     bd_ref[...] = column(db)
     p = proj[...]
     r = dot_nt(bw[...], jnp.concatenate([p, p], axis=0))
@@ -217,7 +224,9 @@
     return jnp.where(even_y, outer, inner), jnp.where(even_y, inner, outer)
 
 
-def k_interior(ft_ref, x_ref, w_ref, g_ref, xm):
+def k_interior(ft_ref, x_ref, w_ref, *refs):
+    sources, g_ref, targets, xm, sem = refs[:6], refs[6], refs[7:13], refs[13], refs[14]
+    copies = fetches(sources, targets, sem)
     lane = lanes_of(C)
     z = jnp.bitwise_and(lane, 15)
     for r in range(20):
@@ -227,6 +236,8 @@
             [jnp.where(lane < 16, zero, roll(v, 16)), v, jnp.where(lane >= 112, zero, roll(v, -16))], xm, r, z
         )
     products(w_ref, xm, 0, 20, into(g_ref))
+    for copy in copies:
+        copy.wait()
 
 
 def k_encode(g_ref, inner_ref, outer_ref, w_ref, bias_ref, em_ref, pool_ref):
@@ -308,7 +319,7 @@
         d_ref[x] = summed(g_ref, x) + bias
 
 
-def k_message(inner_ref, own_ref, outer_ref, _d, out_ref):
+def k_message(inner_ref, own_ref, outer_ref, _vt, out_ref):
     even = even_of("sx")
     inner, outer = inner_ref[0:2], outer_ref[0:2]
     left, right = jnp.where(even, outer, inner), jnp.where(even, inner, outer)
@@ -397,16 +408,8 @@
 
 
 def per_device(features, enc_weight, enc_bias, proj_weight, bottle_weight, bottle_bias, out_weight, dec_weight, dec_bias):
-    ft, inner, outer = call(
-        k_features,
-        (S((18, C, 128), BF), S((2, C, 128), BF), S((2, C, 128), BF)),
-        features,
-        scratch=[pltpu.VMEM((C * 16, 128), F32)],
-    )
-    outer, inner = swapped(outer, "sx", 1), swapped(inner, "sx", 0)
-    sources = (
-        enc_weight.reshape(27, C, C),
-        enc_bias.reshape(1, C),
+    first = (features, enc_weight.reshape(27, C, C), enc_bias.reshape(1, C))
+    later = (
         dec_weight.reshape(27, C, C),
         dec_bias.reshape(1, C),
         bottle_weight.reshape(27 * 32, 512),
@@ -414,13 +417,35 @@
         out_weight,
         bottle_bias.reshape(1, 32),
     )
-    sources = tuple(pltpu.with_memory_space_constraint(v, pltpu.HBM) for v in sources)
-    we, wedge, be, wd, bd, vt, ow2, bb2, smat = call(
+    ft, inner, outer, ew, eb = call(
+        k_features,
+        (S((18, C, 128), BF), S((2, C, 128), BF), S((2, C, 128), BF)) + tuple(S(v.shape, v.dtype) for v in first[1:]),
+        *first,
+        scratch=[pltpu.VMEM((C, 16, 128), BF), pltpu.VMEM((C * 16, 128), F32), pltpu.SemaphoreType.DMA((3,))],
+        hbm=range(3),
+    )
+    outer, inner = swapped(outer, "sx", 1), swapped(inner, "sx", 0)
+    we, wedge, be = call(
+        k_enc_weights, (S((3 * C, 9 * C), BF), S((3 * C, 6 * C), BF), S((C, 128), F32)), ew, eb, flops=10**8
+    )
+    xh, fl, fr, inner, outer = call(k_faces, (S((4, C, 128), BF),) + (S((5, C, 128), BF),) * 4, inner, outer, ft)
+    outer, inner = swapped(outer, "sy", 1), swapped(inner, "sy", 0)
+    product, *later = call(
+        k_interior,
+        (S((20, 3 * C + 8, 128), F32),) + tuple(S(v.shape, v.dtype) for v in later),
+        ft,
+        xh,
+        we,
+        *later,
+        scratch=[pltpu.VMEM((20, 9, C + 16, 128), BF), pltpu.SemaphoreType.DMA((6,))],
+        flops=4 * 10**8,
+        hbm=range(3, 9),
+    )
+    em, pooled = call(k_encode, (S((18, C, 128), BF), S((8, 128), F32)), product, inner, outer, wedge, be)
+    p_outer, p_inner = swapped(pooled, "sx", 1), swapped(pooled, "sx", 0)
+    wd, bd, vt, ow2, bb2, smat = call(
         k_weights,
         (
-            S((3 * C, 9 * C), BF),
-            S((3 * C, 6 * C), BF),
-            S((C, 128), F32),
             S((3 * C, 9 * C), BF),
             S((C, 128), F32),
             S((C, 9 * 128), BF),
@@ -428,24 +453,9 @@
             S((1, C), F32),
             S((256, 9 * 128), BF),
         ),
-        *sources,
-        scratch=[pltpu.VMEM(v.shape, v.dtype) for v in sources] + [pltpu.SemaphoreType.DMA((8,))],
+        *later,
         flops=4 * 10**8,
-        in_space=pltpu.HBM,
-    )
-    xh, fl, fr, inner, outer = call(k_faces, (S((4, C, 128), BF),) + (S((5, C, 128), BF),) * 4, inner, outer, ft)
-    outer, inner = swapped(outer, "sy", 1), swapped(inner, "sy", 0)
-    product = call(
-        k_interior,
-        S((20, 3 * C + 8, 128), F32),
-        ft,
-        xh,
-        we,
-        scratch=[pltpu.VMEM((20, 9, C + 16, 128), BF)],
-        flops=4 * 10**8,
-    )
-    em, pooled = call(k_encode, (S((18, C, 128), BF), S((8, 128), F32)), product, inner, outer, wedge, be)
-    p_outer, p_inner = swapped(pooled, "sx", 1), swapped(pooled, "sx", 0)
+    )
     d = call(
         k_decode,
         S((16, C, 128), F32),
@@ -461,7 +471,7 @@
         scratch=[pltpu.VMEM((18, 9, C + 16, 128), BF), pltpu.VMEM((18, 3 * C + 8, 128), F32)],
         flops=4 * 10**8,
     )
-    message = call(k_message, S((NSY, 8, 128), F32), p_inner, pooled, p_outer, d)
+    message = call(k_message, S((NSY, 8, 128), F32), p_inner, pooled, p_outer, vt)
     everyone = lax.all_to_all(message, "sy", 0, 0, tiled=True)
     partial = call(k_bottleneck, S((NSY, 24, 128), BF), everyone, vt, bb2, ow2)
     parts = lax.all_to_all(partial, "sy", 0, 0, tiled=True)

time: 59.1 us -> 58.5 us (0.990)
  the two profiles are of different devices: /device:TPU:96 before, /device:TPU:224 now
where the time goes in v4:
time: 58.5 us; the launch traced here: 58.1 us
  starting transfers between devices  20 us (34%)
  blocking collectives  18.8 us (32%)
  Pallas kernels  10.4 us (18%)
  waiting for transfers between devices  8.77 us (15%)
    all_to_all x1, blocking collectives, per_device(): everyone = lax.all_to_all(message, 'sy', 0, 0, tiled=True)  18.8 us
    ppermute x6, starting transfers between devices, swapped(): lax.ppermute(v, axis, [(i, i + 1) for i in low] + [(i + 1, i) for i in low])  16.5 us
    pallas_call x10, Pallas kernels, call(): pl.pallas_call(kernel, out_shape=outs, in_specs=[pl.BlockSpec(memory_spac...  10.4 us
    all_to_all x1, waiting for transfers between devices, per_device(): parts = lax.all_to_all(partial, 'sy', 0, 0, tiled=True)  5.33 us
    all_to_all x1, starting transfers between devices, per_device(): parts = lax.all_to_all(partial, 'sy', 0, 0, tiled=True)  3.51 us
    ppermute x6, waiting for transfers between devices, swapped(): lax.ppermute(v, axis, [(i, i + 1) for i in low] + [(i + 1, i) for i in low])  3.44 us
  transfers between devices with their start and end apart: 7, of which 3 were waited for; matrix products, arithmetic and copies ran while one was open for 0% of the time, Pallas kernels for 9%

profile of v4, /device:TPU:224, one launch (start us, length us, event | category | flops | bytes accessed | tf_op | source)
XLA Modules:
  0.0 58.1 jit_solution(12236490042291457375)
XLA Ops:
  0.0 1.2 %shard_map.91 = (bf16[18,64,128]{2,1,0:T(8,128)(2,1)S(1)}, bf16[2,64,128]{2,1,0:T(8,128)(2,1)S(1)}, bf16[2,64,128]{2,1,0:T(8,128)(2,1)S(1)}, bf16[27,64,64]{2,1,0:T(8,128)(2,1)S(1)}, f32[1,64]{1,0:T(1,128)S(1)}) custom-call(bf16[64,16,128]{2,1,0:T(8,128)(2,1)} %x_ref.1, bf16[27,64,64]{2,1,0:T(8,128)(2,1)} %bitcast.8, f32[1,64]{1,0:T(1,128)} %bitcast.9), custom_call_target="tpu_custom_call" | custom-call | flops 1000000 | bytes 100000 | tf_op jit(solution)/shard_map/pallas_call | solution.py:18
  1.2 1.9 %collective-permute-start = (bf16[2,64,128]{2,1,0:T(8,128)(2,1)S(1)}, bf16[2,64,128]{2,1,0:T(8,128)(2,1)S(1)}, u32[]{:S(2)}, u32[]{:S(2)}) collective-permute-start(bf16[2,64,128]{2,1,0:T(8,128)(2,1)S(1)} %get-tuple-element.34), channel_id=1, source_target_pairs={{0,16},{32,48},{64,80},{96,112},{128,144},{160,176},{192,208},{224... | collective-permute-start | bytes 98312 | tf_op jit(solution)/shard_map/ppermute | solution.py:407
  3.1 2.1 %collective-permute-start.1 = (bf16[2,64,128]{2,1,0:T(8,128)(2,1)S(1)}, bf16[2,64,128]{2,1,0:T(8,128)(2,1)S(1)}, u32[]{:S(2)}, u32[]{:S(2)}) collective-permute-start(bf16[2,64,128]{2,1,0:T(8,128)(2,1)S(1)} %get-tuple-element.35), channel_id=1, source_target_pairs={{16,32},{48,64},{80,96},{112,128},{144,160},{176,192},{208,224},{2... | collective-permute-start | bytes 98312 | tf_op jit(solution)/shard_map/ppermute | solution.py:407
  5.3 0.0 collective-permute-done.inner_ref
  5.3 3.1 %collective-permute-done.1.outer_ref = bf16[2,64,128]{2,1,0:T(8,128)(2,1)S(1)} collective-permute-done((bf16[2,64,128]{2,1,0:T(8,128)(2,1)S(1)}, bf16[2,64,128]{2,1,0:T(8,128)(2,1)S(1)}, u32[]{:S(2)}, u32[]{:S(2)}) %collective-permute-start.1) | collective-permute-done | bytes 32800 | tf_op jit(solution)/shard_map/ppermute | solution.py:407
  8.4 0.2 shard_map.92
  8.6 3.5 %collective-permute-start.2 = (bf16[5,64,128]{2,1,0:T(8,128)(2,1)S(1)}, bf16[5,64,128]{2,1,0:T(8,128)(2,1)S(1)}, u32[]{:S(2)}, u32[]{:S(2)}) collective-permute-start(bf16[5,64,128]{2,1,0:T(8,128)(2,1)S(1)} %get-tuple-element.41), channel_id=1, source_target_pairs={{0,1},{2,3},{4,5},{6,7},{8,9},{10,11},{12,13},{14,15},{1,0},{3,2},... | collective-permute-start | bytes 245768 | tf_op jit(solution)/shard_map/ppermute | solution.py:407
  12.1 0.7 %collective-permute-start.3 = (bf16[5,64,128]{2,1,0:T(8,128)(2,1)S(1)}, bf16[5,64,128]{2,1,0:T(8,128)(2,1)S(1)}, u32[]{:S(2)}, u32[]{:S(2)}) collective-permute-start(bf16[5,64,128]{2,1,0:T(8,128)(2,1)S(1)} %get-tuple-element.42), channel_id=1, source_target_pairs={{1,2},{3,4},{5,6},{7,8},{9,10},{11,12},{13,14},{2,1},{4,3},{6,5},{... | collective-permute-start | bytes 245768 | tf_op jit(solution)/shard_map/ppermute | solution.py:407
  12.7 0.2 shard_map.93
  12.9 2.2 %shard_map.94 = (f32[20,200,128]{2,1,0:T(8,128)S(1)}, bf16[27,64,64]{2,1,0:T(8,128)(2,1)S(1)}, f32[1,64]{1,0:T(1,128)S(1)}, bf16[864,512]{1,0:T(8,128)(2,1)S(1)}...) custom-call(bf16[18,64,128]{2,1,0:T(8,128)(2,1)S(1)} %get-tuple-element.33.ft_ref, ...), custom_call_target="tpu_custom_call" | custom-call | flops 400000000 | bytes 100000 | tf_op jit(solution)/shard_map/pallas_call | solution.py:18
  15.2 0.0 collective-permute-done.2.inner_ref
  15.2 0.0 collective-permute-done.3.outer_ref
  15.2 1.2 %shard_map.95 = (bf16[18,64,128]{2,1,0:T(8,128)(2,1)S(1)}, f32[8,128]{1,0:T(8,128)S(1)}) custom-call(f32[20,200,128]{2,1,0:T(8,128)S(1)} %get-tuple-element.40.g_ref, bf16[5,64,128]{2,1,0:T(8,128)(2,1)S(1)} %collective-permute-done.2.inner_ref, bf16[5,64,128]{2,1,0:T(8,128)(2,1)S(1)} %collective-permute-done.3.outer_ref, ...), custom_call_target="tpu_custom_call" | custom-call | flops 1000000 | bytes 100000 | tf_op jit(solution)/shard_map/pallas_call | solution.py:18
  16.3 1.9 %collective-permute-start.5 = (f32[8,128]{1,0:T(8,128)S(1)}, f32[8,128]{1,0:T(8,128)S(1)}, u32[]{:S(2)}, u32[]{:S(2)}) collective-permute-start(f32[8,128]{1,0:T(8,128)S(1)} %get-tuple-element.45.own_ref), channel_id=1, source_target_pairs={{16,32},{48,64},{80,96},{112,128},{144,160},{176,192},{208,224},{2... | collective-permute-start | bytes 12296 | tf_op jit(solution)/shard_map/ppermute | solution.py:407
  18.3 6.3 %collective-permute-start.4 = (f32[8,128]{1,0:T(8,128)S(1)}, f32[8,128]{1,0:T(8,128)S(1)}, u32[]{:S(2)}, u32[]{:S(2)}) collective-permute-start(f32[8,128]{1,0:T(8,128)S(1)} %get-tuple-element.45.own_ref), channel_id=1, source_target_pairs={{0,16},{32,48},{64,80},{96,112},{128,144},{160,176},{192,208},{224... | collective-permute-start | bytes 12296 | tf_op jit(solution)/shard_map/ppermute | solution.py:407
  24.6 0.4 shard_map.96
  25.1 0.0 collective-permute-done.5.outer_ref
  25.1 0.3 collective-permute-done.4.inner_ref
  25.4 18.8 %all_to_all.10.p_ref = f32[16,8,128]{2,1,0:T(8,128)S(1)} all-to-all(f32[16,8,128]{2,1,0:T(8,128)S(1)} %shard_map.97), channel_id=1, replica_groups=mesh['sx'=32,'sy'=16] {'sy'}, dimensions={0} | all-to-all | bytes 131072 | tf_op jit(solution)/shard_map/all_to_all | solution.py:475
  44.3 1.0 %shard_map.98 = bf16[16,24,128]{2,1,0:T(8,128)(2,1)} custom-call(f32[16,8,128]{2,1,0:T(8,128)S(1)} %all_to_all.10.p_ref, bf16[64,1152]{1,0:T(8,128)(2,1)S(1)} %get-tuple-element.52._vt.vt_ref, f32[1,64]{1,0:T(1,128)S(1)} %get-tuple-element.53.bb_ref, bf16[64,128]{1,0:T(8,128)(2,1)S(1)} %get-tuple-element.54.ow_ref), custom_call_target="tpu_custom_call" | custom-call | flops 1000000 | bytes 100000 | tf_op jit(solution)/shard_map/pallas_call | solution.py:18
  45.3 3.5 %all-to-all-start.1 = ((bf16[16,24,128]{2,1,0:T(8,128)(2,1)}), bf16[16,24,128]{2,1,0:T(8,128)(2,1)S(1)}, u32[]{:S(2)}, u32[]{:S(2)}) async-start(bf16[16,24,128]{2,1,0:T(8,128)(2,1)} %shard_map.98), calls=%async_computation.1 | async-start | bytes 196608 | tf_op jit(solution)/shard_map/all_to_all | solution.py:477
  48.8 2.4 %shard_map.99.d_ref = f32[16,64,128]{2,1,0:T(8,128)S(1)} custom-call(bf16[5,64,128]{2,1,0:T(8,128)(2,1)S(1)} %get-tuple-element.57.fl_ref, bf16[5,64,128]{2,1,0:T(8,128)(2,1)S(1)} %get-tuple-element.58.fr_ref, bf16[5,64,128]{2,1,0:T(8,128)(2,1)S(1)} %collective-permute-done.2.inner_ref, bf16[5,64,128]{2,1,0:T(8,128)(2,1)S(1)} %collective-permute-done.3.outer_ref, ...), custom_call_target="tpu_custom_call" | custom-call | flops 400000000 | bytes 100000 | tf_op jit(solution)/shard_map/pallas_call | solution.py:18
  51.1 5.3 %all-to-all-done.1.parts_ref = bf16[16,24,128]{2,1,0:T(8,128)(2,1)S(1)} async-done(((bf16[16,24,128]{2,1,0:T(8,128)(2,1)}), bf16[16,24,128]{2,1,0:T(8,128)(2,1)S(1)}, u32[]{:S(2)}, u32[]{:S(2)}) %all-to-all-start.1) | async-done | bytes 98336 | tf_op jit(solution)/shard_map/all_to_all | solution.py:477
  56.5 1.6 %shard_map.100 = bf16[64,16,128]{2,1,0:T(8,128)(2,1)} custom-call(bf16[16,24,128]{2,1,0:T(8,128)(2,1)S(1)} %all-to-all-done.1.parts_ref, bf16[256,1152]{1,0:T(8,128)(2,1)S(1)} %get-tuple-element.55.s_ref, bf16[192,576]{1,0:T(8,128)(2,1)S(1)} %get-tuple-element.56.w_ref, f32[16,64,128]{2,1,0:T(8,128)S(1)} %shard_map.99.d_ref), custom_call_target="tpu_custom_call" | custom-call | flops 1000000 | bytes 100000 | tf_op jit(solution)/shard_map/pallas_call | solution.py:18
  (1 shorter events, 0.0 us)
Async XLA Ops:
  1.2 4.1 %collective-permute-start = (bf16[2,64,128]{2,1,0:T(8,128)(2,1)S(1)}, bf16[2,64,128]{2,1,0:T(8,128)(2,1)S(1)}, u32[]{:S(2)}, u32[]{:S(2)}) collective-permute-start(bf16[2,64,128]{2,1,0:T(8,128)(2,1)S(1)} %get-tuple-element.34), channel_id=1, source_target_pairs={{0,16},{32,48},{64,80},{96,112},{128,144},{160,176},{192,208},{224... | collective-permute-start | bytes 98312 | tf_op jit(solution)/shard_map/ppermute | solution.py:407
  3.1 5.2 %collective-permute-start.1 = (bf16[2,64,128]{2,1,0:T(8,128)(2,1)S(1)}, bf16[2,64,128]{2,1,0:T(8,128)(2,1)S(1)}, u32[]{:S(2)}, u32[]{:S(2)}) collective-permute-start(bf16[2,64,128]{2,1,0:T(8,128)(2,1)S(1)} %get-tuple-element.35), channel_id=1, source_target_pairs={{16,32},{48,64},{80,96},{112,128},{144,160},{176,192},{208,224},{2... | collective-permute-start | bytes 98312 | tf_op jit(solution)/shard_map/ppermute | solution.py:407
  8.6 6.6 %collective-permute-start.2 = (bf16[5,64,128]{2,1,0:T(8,128)(2,1)S(1)}, bf16[5,64,128]{2,1,0:T(8,128)(2,1)S(1)}, u32[]{:S(2)}, u32[]{:S(2)}) collective-permute-start(bf16[5,64,128]{2,1,0:T(8,128)(2,1)S(1)} %get-tuple-element.41), channel_id=1, source_target_pairs={{0,1},{2,3},{4,5},{6,7},{8,9},{10,11},{12,13},{14,15},{1,0},{3,2},... | collective-permute-start | bytes 245768 | tf_op jit(solution)/shard_map/ppermute | solution.py:407
  12.1 3.1 %collective-permute-start.3 = (bf16[5,64,128]{2,1,0:T(8,128)(2,1)S(1)}, bf16[5,64,128]{2,1,0:T(8,128)(2,1)S(1)}, u32[]{:S(2)}, u32[]{:S(2)}) collective-permute-start(bf16[5,64,128]{2,1,0:T(8,128)(2,1)S(1)} %get-tuple-element.42), channel_id=1, source_target_pairs={{1,2},{3,4},{5,6},{7,8},{9,10},{11,12},{13,14},{2,1},{4,3},{6,5},{... | collective-permute-start | bytes 245768 | tf_op jit(solution)/shard_map/ppermute | solution.py:407
  16.3 8.7 %collective-permute-start.5 = (f32[8,128]{1,0:T(8,128)S(1)}, f32[8,128]{1,0:T(8,128)S(1)}, u32[]{:S(2)}, u32[]{:S(2)}) collective-permute-start(f32[8,128]{1,0:T(8,128)S(1)} %get-tuple-element.45.own_ref), channel_id=1, source_target_pairs={{16,32},{48,64},{80,96},{112,128},{144,160},{176,192},{208,224},{2... | collective-permute-start | bytes 12296 | tf_op jit(solution)/shard_map/ppermute | solution.py:407
  18.3 7.2 %collective-permute-start.4 = (f32[8,128]{1,0:T(8,128)S(1)}, f32[8,128]{1,0:T(8,128)S(1)}, u32[]{:S(2)}, u32[]{:S(2)}) collective-permute-start(f32[8,128]{1,0:T(8,128)S(1)} %get-tuple-element.45.own_ref), channel_id=1, source_target_pairs={{0,16},{32,48},{64,80},{96,112},{128,144},{160,176},{192,208},{224... | collective-permute-start | bytes 12296 | tf_op jit(solution)/shard_map/ppermute | solution.py:407
  45.3 11.2 %all-to-all-start.1 = ((bf16[16,24,128]{2,1,0:T(8,128)(2,1)}), bf16[16,24,128]{2,1,0:T(8,128)(2,1)S(1)}, u32[]{:S(2)}, u32[]{:S(2)}) async-start(bf16[16,24,128]{2,1,0:T(8,128)(2,1)} %shard_map.98), calls=%async_computation.1 | async-start | bytes 196608 | tf_op jit(solution)/shard_map/all_to_all | solution.py:477

commit v5 on v4

--- a/solution.py
+++ b/solution.py
@@ -77,11 +77,11 @@
         copy.wait()
 
 
-def k_faces(inner_ref, outer_ref, ft_ref, x_ref, left_ref, right_ref, s_inner_ref, s_outer_ref):
+def k_faces(pair_ref, outer_ref, ft_ref, x_ref, left_ref, right_ref, s_inner_ref, s_outer_ref):
     lane = lanes_of(C)
     even_x, even_y = even_of("sx"), even_of("sy")
     for k in range(2):
-        inner, outer = inner_ref[k], outer_ref[k]
+        inner, outer = jnp.where(even_x, pair_ref[1, k], pair_ref[0, k]), outer_ref[k]
         x_ref[k] = jnp.where(even_x, outer, inner)
         x_ref[2 + k] = jnp.where(even_x, inner, outer)
     for g in range(5):
@@ -132,7 +132,22 @@
     be_ref[...] = column(eb)
 
 
-def k_weights(dw, db, bw, proj, ow, bb, wd_ref, bd_ref, vt_ref, ow2_ref, bb2_ref, s_ref):
+def k_weights(bw, proj, ow, bb, vt_ref, ow2_ref, bb2_ref):
+    p = proj[...]
+    r = dot_nt(bw[...], jnp.concatenate([p, p], axis=0))
+    half = lanes_of(C) < C
+    for ab in range(9):
+        both = jnp.where(half, r[96 * ab : 96 * ab + 64], r[96 * ab + 32 : 96 * ab + 96])
+        vt_ref[:, pl.ds(128 * ab, 128)] = both.astype(BF)
+    o = ow[...]
+    none = jnp.zeros_like(o)
+    ow2_ref[...] = jnp.concatenate([jnp.concatenate([o, none], axis=1), jnp.concatenate([none, o], axis=1)], axis=0)
+    bb2_ref[...] = jnp.concatenate([bb[...], bb[...]], axis=1)
+
+
+def k_dec_weights(dw, db, wd_ref, bd_ref, s_ref):
+    arranged(dw, wd_ref, range(9))
+    bd_ref[...] = column(db)
     j = lax.axis_index("sy")
     row = lax.broadcasted_iota(jnp.int32, (32, 128), 0)
     lane = lax.broadcasted_iota(jnp.int32, (32, 128), 1)
@@ -148,18 +163,6 @@
                 at = pl.ds(128 * (3 * b + c), 128)
                 s_ref[pl.ds(128 * zo, 32), at] = (wy * wz).astype(BF)
                 s_ref[pl.ds(128 * zo + 32, 96), at] = zero
-    arranged(dw, wd_ref, range(9))
-    bd_ref[...] = column(db)
-    p = proj[...]
-    r = dot_nt(bw[...], jnp.concatenate([p, p], axis=0))
-    half = lanes_of(C) < C
-    for ab in range(9):
-        both = jnp.where(half, r[96 * ab : 96 * ab + 64], r[96 * ab + 32 : 96 * ab + 96])
-        vt_ref[:, pl.ds(128 * ab, 128)] = both.astype(BF)
-    o = ow[...]
-    none = jnp.zeros_like(o)
-    ow2_ref[...] = jnp.concatenate([jnp.concatenate([o, none], axis=1), jnp.concatenate([none, o], axis=1)], axis=0)
-    bb2_ref[...] = jnp.concatenate([bb[...], bb[...]], axis=1)
 
 
 def taps_of(v, z):
@@ -319,9 +322,9 @@
         d_ref[x] = summed(g_ref, x) + bias
 
 
-def k_message(inner_ref, own_ref, outer_ref, _vt, out_ref):
+def k_message(pair_ref, own_ref, outer_ref, out_ref):
     even = even_of("sx")
-    inner, outer = inner_ref[0:2], outer_ref[0:2]
+    inner, outer = jnp.where(even, pair_ref[1, 0:2], pair_ref[0, 0:2]), outer_ref[0:2]
     left, right = jnp.where(even, outer, inner), jnp.where(even, inner, outer)
     message = jnp.concatenate([left, own_ref[0:2], right, jnp.zeros((2, 128), F32)], axis=0)
     for i in range(NSY):
@@ -407,6 +410,11 @@
     return lax.ppermute(v, axis, [(i, i + 1) for i in low] + [(i + 1, i) for i in low])
 
 
+def paired(v, axis):
+    pairs = [[i, i + 1] for i in range(0, lax.axis_size(axis), 2)]
+    return lax.all_gather(v, axis, axis_index_groups=pairs)
+
+
 def per_device(features, enc_weight, enc_bias, proj_weight, bottle_weight, bottle_bias, out_weight, dec_weight, dec_bias):
     first = (features, enc_weight.reshape(27, C, C), enc_bias.reshape(1, C))
     later = (
@@ -424,11 +432,11 @@
         scratch=[pltpu.VMEM((C, 16, 128), BF), pltpu.VMEM((C * 16, 128), F32), pltpu.SemaphoreType.DMA((3,))],
         hbm=range(3),
     )
-    outer, inner = swapped(outer, "sx", 1), swapped(inner, "sx", 0)
+    outer, pair = swapped(outer, "sx", 1), paired(inner, "sx")
     we, wedge, be = call(
         k_enc_weights, (S((3 * C, 9 * C), BF), S((3 * C, 6 * C), BF), S((C, 128), F32)), ew, eb, flops=10**8
     )
-    xh, fl, fr, inner, outer = call(k_faces, (S((4, C, 128), BF),) + (S((5, C, 128), BF),) * 4, inner, outer, ft)
+    xh, fl, fr, inner, outer = call(k_faces, (S((4, C, 128), BF),) + (S((5, C, 128), BF),) * 4, pair, outer, ft)
     outer, inner = swapped(outer, "sy", 1), swapped(inner, "sy", 0)
     product, *later = call(
         k_interior,
@@ -442,19 +450,10 @@
         hbm=range(3, 9),
     )
     em, pooled = call(k_encode, (S((18, C, 128), BF), S((8, 128), F32)), product, inner, outer, wedge, be)
-    p_outer, p_inner = swapped(pooled, "sx", 1), swapped(pooled, "sx", 0)
-    wd, bd, vt, ow2, bb2, smat = call(
-        k_weights,
-        (
-            S((3 * C, 9 * C), BF),
-            S((C, 128), F32),
-            S((C, 9 * 128), BF),
-            S((C, 128), BF),
-            S((1, C), F32),
-            S((256, 9 * 128), BF),
-        ),
-        *later,
-        flops=4 * 10**8,
+    p_outer, p_pair = swapped(pooled, "sx", 1), paired(pooled, "sx")
+    vt, ow2, bb2 = call(k_weights, (S((C, 9 * 128), BF), S((C, 128), BF), S((1, C), F32)), *later[2:], flops=4 * 10**8)
+    wd, bd, smat = call(
+        k_dec_weights, (S((3 * C, 9 * C), BF), S((C, 128), F32), S((256, 9 * 128), BF)), *later[:2], flops=10**8
     )
     d = call(
         k_decode,
@@ -471,7 +470,7 @@
         scratch=[pltpu.VMEM((18, 9, C + 16, 128), BF), pltpu.VMEM((18, 3 * C + 8, 128), F32)],
         flops=4 * 10**8,
     )
-    message = call(k_message, S((NSY, 8, 128), F32), p_inner, pooled, p_outer, vt)
+    message = call(k_message, S((NSY, 8, 128), F32), p_pair, pooled, p_outer)
     everyone = lax.all_to_all(message, "sy", 0, 0, tiled=True)
     partial = call(k_bottleneck, S((NSY, 24, 128), BF), everyone, vt, bb2, ow2)
     parts = lax.all_to_all(partial, "sy", 0, 0, tiled=True)

time: 58.5 us -> 56.1 us (0.959)
  blocking collectives: 18.8 us -> 9.2 us
  waiting for transfers between devices: 8.77 us -> 12.4 us
  starting transfers between devices: 20 us -> 22.9 us
  Pallas kernels: 10.4 us -> 11.1 us
    all_to_all x1 -> x0, blocking collectives: 18.8 us -> none  [per_device(): everyone = lax.all_to_all(message, 'sy', 0, 0, tiled=True)]
    all_to_all x0 -> x1, starting transfers between devices: none -> 11.4 us  [per_device(): everyone = lax.all_to_all(message, 'sy', 0, 0, tiled=True)]
    all_gather x0 -> x2, blocking collectives: none -> 9.2 us  [paired(): return lax.all_gather(v, axis, axis_index_groups=pairs)]
    ppermute x6 -> x4, starting transfers between devices: 16.5 us -> 7.99 us  [swapped(): lax.ppermute(v, axis, [(i, i + 1) for i in low] + [(i + 1, i) for i in low])]
    all_to_all x0 -> x1, waiting for transfers between devices: none -> 7.26 us  [per_device(): everyone = lax.all_to_all(message, 'sy', 0, 0, tiled=True)]
    ppermute x6 -> x4, waiting for transfers between devices: 3.44 us -> 0.02 us  [swapped(): lax.ppermute(v, axis, [(i, i + 1) for i in low] + [(i + 1, i) for i in low])]
    pallas_call x10 -> x11, Pallas kernels: 10.4 us -> 11.1 us  [call(): pl.pallas_call(kernel, out_shape=outs, in_specs=[pl.BlockSpec(memory_spac...]
  transfers between devices with their start and end apart: 7 -> 6, of which waited for: 3 -> 2; matrix products, arithmetic and copies ran while one was open for 0% -> 0% of each run, Pallas kernels for 9% -> 10%
where the time goes in v5:
time: 56.1 us; the launch traced here: 55.7 us
  starting transfers between devices  22.9 us (41%)
  waiting for transfers between devices  12.4 us (22%)
  Pallas kernels  11.1 us (20%)
  blocking collectives  9.2 us (16%)
    all_to_all x1, starting transfers between devices, per_device(): everyone = lax.all_to_all(message, 'sy', 0, 0, tiled=True)  11.4 us
    pallas_call x11, Pallas kernels, call(): pl.pallas_call(kernel, out_shape=outs, in_specs=[pl.BlockSpec(memory_spac...  11.1 us
    all_gather x2, blocking collectives, paired(): return lax.all_gather(v, axis, axis_index_groups=pairs)  9.2 us
    ppermute x4, starting transfers between devices, swapped(): lax.ppermute(v, axis, [(i, i + 1) for i in low] + [(i + 1, i) for i in low])  7.99 us
    all_to_all x1, waiting for transfers between devices, per_device(): everyone = lax.all_to_all(message, 'sy', 0, 0, tiled=True)  7.26 us
    all_to_all x1, waiting for transfers between devices, per_device(): parts = lax.all_to_all(partial, 'sy', 0, 0, tiled=True)  5.15 us
    all_to_all x1, starting transfers between devices, per_device(): parts = lax.all_to_all(partial, 'sy', 0, 0, tiled=True)  3.51 us
  transfers between devices with their start and end apart: 6, of which 2 were waited for; matrix products, arithmetic and copies ran while one was open for 0% of the time, Pallas kernels for 10%

profile of v5, /device:TPU:224, one launch (start us, length us, event | category | flops | bytes accessed | tf_op | source)
XLA Modules:
  0.0 55.7 jit_solution(8202997538450013979)
XLA Ops:
  0.0 1.2 %shard_map.91 = (bf16[18,64,128]{2,1,0:T(8,128)(2,1)S(1)}, bf16[2,64,128]{2,1,0:T(8,128)(2,1)S(1)}, bf16[2,64,128]{2,1,0:T(8,128)(2,1)S(1)}, bf16[27,64,64]{2,1,0:T(8,128)(2,1)S(1)}, f32[1,64]{1,0:T(1,128)S(1)}) custom-call(bf16[64,16,128]{2,1,0:T(8,128)(2,1)} %x_ref.1, bf16[27,64,64]{2,1,0:T(8,128)(2,1)} %bitcast.12, f32[1,64]{1,0:T(1,128)} %bitcast.13), custom_call_target="tpu_custom_call" | custom-call | flops 1000000 | bytes 100000 | tf_op jit(solution)/shard_map/pallas_call | solution.py:18
  1.2 1.9 %collective-permute-start = (bf16[2,64,128]{2,1,0:T(8,128)(2,1)S(1)}, bf16[2,64,128]{2,1,0:T(8,128)(2,1)S(1)}, u32[]{:S(2)}, u32[]{:S(2)}) collective-permute-start(bf16[2,64,128]{2,1,0:T(8,128)(2,1)S(1)} %get-tuple-element.35), channel_id=1, source_target_pairs={{16,32},{48,64},{80,96},{112,128},{144,160},{176,192},{208,224},{2... | collective-permute-start | bytes 98312 | tf_op jit(solution)/shard_map/ppermute | solution.py:410
  3.1 4.7 %all-gather = bf16[4,64,128]{2,1,0:T(8,128)(2,1)S(1)} all-gather(bf16[2,64,128]{2,1,0:T(8,128)(2,1)S(1)} %get-tuple-element.34), channel_id=2, replica_groups={{0,16},{32,48},{64,80},{96,112},{128,144},{160,176},{192,208},{224,240}..., dimensions={0}, use_global_device_ids=true | all-gather | bytes 98304 | tf_op jit(solution)/shard_map/all_gather | solution.py:415
  7.9 0.0 collective-permute-done.outer_ref
  7.9 0.2 shard_map.92
  8.1 3.5 %collective-permute-start.1 = (bf16[5,64,128]{2,1,0:T(8,128)(2,1)S(1)}, bf16[5,64,128]{2,1,0:T(8,128)(2,1)S(1)}, u32[]{:S(2)}, u32[]{:S(2)}) collective-permute-start(bf16[5,64,128]{2,1,0:T(8,128)(2,1)S(1)} %get-tuple-element.41), channel_id=1, source_target_pairs={{0,1},{2,3},{4,5},{6,7},{8,9},{10,11},{12,13},{14,15},{1,0},{3,2},... | collective-permute-start | bytes 245768 | tf_op jit(solution)/shard_map/ppermute | solution.py:410
  11.6 0.7 %collective-permute-start.2 = (bf16[5,64,128]{2,1,0:T(8,128)(2,1)S(1)}, bf16[5,64,128]{2,1,0:T(8,128)(2,1)S(1)}, u32[]{:S(2)}, u32[]{:S(2)}) collective-permute-start(bf16[5,64,128]{2,1,0:T(8,128)(2,1)S(1)} %get-tuple-element.42), channel_id=1, source_target_pairs={{1,2},{3,4},{5,6},{7,8},{9,10},{11,12},{13,14},{2,1},{4,3},{6,5},{... | collective-permute-start | bytes 245768 | tf_op jit(solution)/shard_map/ppermute | solution.py:410
  12.3 0.2 shard_map.93
  12.4 2.2 %shard_map.94 = (f32[20,200,128]{2,1,0:T(8,128)S(1)}, bf16[27,64,64]{2,1,0:T(8,128)(2,1)S(1)}, f32[1,64]{1,0:T(1,128)S(1)}, bf16[864,512]{1,0:T(8,128)(2,1)S(1)}...) custom-call(bf16[18,64,128]{2,1,0:T(8,128)(2,1)S(1)} %get-tuple-element.33.ft_ref, ...), custom_call_target="tpu_custom_call" | custom-call | flops 400000000 | bytes 100000 | tf_op jit(solution)/shard_map/pallas_call | solution.py:18
  14.7 0.0 collective-permute-done.1.inner_ref
  14.7 1.2 %shard_map.95 = (bf16[18,64,128]{2,1,0:T(8,128)(2,1)S(1)}, f32[8,128]{1,0:T(8,128)S(1)}) custom-call(f32[20,200,128]{2,1,0:T(8,128)S(1)} %get-tuple-element.40.g_ref, bf16[5,64,128]{2,1,0:T(8,128)(2,1)S(1)} %collective-permute-done.1.inner_ref, bf16[5,64,128]{2,1,0:T(8,128)(2,1)S(1)} %collective-permute-done.2.outer_ref, ...), custom_call_target="tpu_custom_call" | custom-call | flops 1000000 | bytes 100000 | tf_op jit(solution)/shard_map/pallas_call | solution.py:18
  15.8 1.9 %collective-permute-start.3 = (f32[8,128]{1,0:T(8,128)S(1)}, f32[8,128]{1,0:T(8,128)S(1)}, u32[]{:S(2)}, u32[]{:S(2)}) collective-permute-start(f32[8,128]{1,0:T(8,128)S(1)} %get-tuple-element.45.own_ref), channel_id=1, source_target_pairs={{16,32},{48,64},{80,96},{112,128},{144,160},{176,192},{208,224},{2... | collective-permute-start | bytes 12296 | tf_op jit(solution)/shard_map/ppermute | solution.py:410
  17.8 4.5 %all-gather.1 = f32[16,128]{1,0:T(8,128)S(1)} all-gather(f32[8,128]{1,0:T(8,128)S(1)} %get-tuple-element.45.own_ref), channel_id=3, replica_groups={{0,16},{32,48},{64,80},{96,112},{128,144},{160,176},{192,208},{224,240}..., dimensions={0}, use_global_device_ids=true | all-gather | bytes 12288 | tf_op jit(solution)/shard_map/all_gather | solution.py:415
  22.2 0.0 collective-permute-done.3.outer_ref
  22.2 0.6 %shard_map.96 = f32[16,8,128]{2,1,0:T(8,128)} custom-call(f32[2,8,128]{2,1,0:T(8,128)S(1)} %bitcast.9, f32[8,128]{1,0:T(8,128)S(1)} %get-tuple-element.45.own_ref, f32[8,128]{1,0:T(8,128)S(1)} %collective-permute-done.3.outer_ref), custom_call_target="tpu_custom_call" | custom-call | flops 1000000 | bytes 100000 | tf_op jit(solution)/shard_map/pallas_call | solution.py:18
  22.9 11.4 %all-to-all-start = ((f32[16,8,128]{2,1,0:T(8,128)}), f32[16,8,128]{2,1,0:T(8,128)S(1)}, u32[]{:S(2)}, u32[]{:S(2)}) async-start(f32[16,8,128]{2,1,0:T(8,128)} %shard_map.96), calls=%async_computation | async-start | bytes 131072 | tf_op jit(solution)/shard_map/all_to_all | solution.py:474
  34.3 0.4 shard_map.97
  34.7 7.3 %all-to-all-done.p_ref = f32[16,8,128]{2,1,0:T(8,128)S(1)} async-done(((f32[16,8,128]{2,1,0:T(8,128)}), f32[16,8,128]{2,1,0:T(8,128)S(1)}, u32[]{:S(2)}, u32[]{:S(2)}) %all-to-all-start) | async-done | bytes 65568 | tf_op jit(solution)/shard_map/all_to_all | solution.py:474
  41.9 1.0 %shard_map.98 = bf16[16,24,128]{2,1,0:T(8,128)(2,1)} custom-call(f32[16,8,128]{2,1,0:T(8,128)S(1)} %all-to-all-done.p_ref, bf16[64,1152]{1,0:T(8,128)(2,1)S(1)} %get-tuple-element.50.vt_ref, f32[1,64]{1,0:T(1,128)S(1)} %get-tuple-element.51.bb_ref, bf16[64,128]{1,0:T(8,128)(2,1)S(1)} %get-tuple-element.52.ow_ref), custom_call_target="tpu_custom_call" | custom-call | flops 1000000 | bytes 100000 | tf_op jit(solution)/shard_map/pallas_call | solution.py:18
  42.9 3.5 %all-to-all-start.1 = ((bf16[16,24,128]{2,1,0:T(8,128)(2,1)}), bf16[16,24,128]{2,1,0:T(8,128)(2,1)S(1)}, u32[]{:S(2)}, u32[]{:S(2)}) async-start(bf16[16,24,128]{2,1,0:T(8,128)(2,1)} %shard_map.98), calls=%async_computation.1 | async-start | bytes 196608 | tf_op jit(solution)/shard_map/all_to_all | solution.py:476
  46.4 0.2 shard_map.99
  46.6 2.4 %shard_map.100.d_ref = f32[16,64,128]{2,1,0:T(8,128)S(1)} custom-call(bf16[5,64,128]{2,1,0:T(8,128)(2,1)S(1)} %get-tuple-element.57.fl_ref, bf16[5,64,128]{2,1,0:T(8,128)(2,1)S(1)} %get-tuple-element.58.fr_ref, bf16[5,64,128]{2,1,0:T(8,128)(2,1)S(1)} %collective-permute-done.1.inner_ref, bf16[5,64,128]{2,1,0:T(8,128)(2,1)S(1)} %collective-permute-done.2.outer_ref, ...), custom_call_target="tpu_custom_call" | custom-call | flops 400000000 | bytes 100000 | tf_op jit(solution)/shard_map/pallas_call | solution.py:18
  49.0 5.1 %all-to-all-done.1.parts_ref = bf16[16,24,128]{2,1,0:T(8,128)(2,1)S(1)} async-done(((bf16[16,24,128]{2,1,0:T(8,128)(2,1)}), bf16[16,24,128]{2,1,0:T(8,128)(2,1)S(1)}, u32[]{:S(2)}, u32[]{:S(2)}) %all-to-all-start.1) | async-done | bytes 98336 | tf_op jit(solution)/shard_map/all_to_all | solution.py:476
  54.1 1.6 %shard_map.101 = bf16[64,16,128]{2,1,0:T(8,128)(2,1)} custom-call(bf16[16,24,128]{2,1,0:T(8,128)(2,1)S(1)} %all-to-all-done.1.parts_ref, bf16[256,1152]{1,0:T(8,128)(2,1)S(1)} %get-tuple-element.55.s_ref, bf16[192,576]{1,0:T(8,128)(2,1)S(1)} %get-tuple-element.56.w_ref, f32[16,64,128]{2,1,0:T(8,128)S(1)} %shard_map.100.d_ref), custom_call_target="tpu_custom_call" | custom-call | flops 1000000 | bytes 100000 | tf_op jit(solution)/shard_map/pallas_call | solution.py:18
  (1 shorter events, 0.0 us)
Async XLA Ops:
  1.2 6.7 %collective-permute-start = (bf16[2,64,128]{2,1,0:T(8,128)(2,1)S(1)}, bf16[2,64,128]{2,1,0:T(8,128)(2,1)S(1)}, u32[]{:S(2)}, u32[]{:S(2)}) collective-permute-start(bf16[2,64,128]{2,1,0:T(8,128)(2,1)S(1)} %get-tuple-element.35), channel_id=1, source_target_pairs={{16,32},{48,64},{80,96},{112,128},{144,160},{176,192},{208,224},{2... | collective-permute-start | bytes 98312 | tf_op jit(solution)/shard_map/ppermute | solution.py:410
  8.1 6.6 %collective-permute-start.1 = (bf16[5,64,128]{2,1,0:T(8,128)(2,1)S(1)}, bf16[5,64,128]{2,1,0:T(8,128)(2,1)S(1)}, u32[]{:S(2)}, u32[]{:S(2)}) collective-permute-start(bf16[5,64,128]{2,1,0:T(8,128)(2,1)S(1)} %get-tuple-element.41), channel_id=1, source_target_pairs={{0,1},{2,3},{4,5},{6,7},{8,9},{10,11},{12,13},{14,15},{1,0},{3,2},... | collective-permute-start | bytes 245768 | tf_op jit(solution)/shard_map/ppermute | solution.py:410
  11.6 3.1 %collective-permute-start.2 = (bf16[5,64,128]{2,1,0:T(8,128)(2,1)S(1)}, bf16[5,64,128]{2,1,0:T(8,128)(2,1)S(1)}, u32[]{:S(2)}, u32[]{:S(2)}) collective-permute-start(bf16[5,64,128]{2,1,0:T(8,128)(2,1)S(1)} %get-tuple-element.42), channel_id=1, source_target_pairs={{1,2},{3,4},{5,6},{7,8},{9,10},{11,12},{13,14},{2,1},{4,3},{6,5},{... | collective-permute-start | bytes 245768 | tf_op jit(solution)/shard_map/ppermute | solution.py:410
  15.8 6.4 %collective-permute-start.3 = (f32[8,128]{1,0:T(8,128)S(1)}, f32[8,128]{1,0:T(8,128)S(1)}, u32[]{:S(2)}, u32[]{:S(2)}) collective-permute-start(f32[8,128]{1,0:T(8,128)S(1)} %get-tuple-element.45.own_ref), channel_id=1, source_target_pairs={{16,32},{48,64},{80,96},{112,128},{144,160},{176,192},{208,224},{2... | collective-permute-start | bytes 12296 | tf_op jit(solution)/shard_map/ppermute | solution.py:410
  22.9 19.0 %all-to-all-start = ((f32[16,8,128]{2,1,0:T(8,128)}), f32[16,8,128]{2,1,0:T(8,128)S(1)}, u32[]{:S(2)}, u32[]{:S(2)}) async-start(f32[16,8,128]{2,1,0:T(8,128)} %shard_map.96), calls=%async_computation | async-start | bytes 131072 | tf_op jit(solution)/shard_map/all_to_all | solution.py:474
  42.9 11.2 %all-to-all-start.1 = ((bf16[16,24,128]{2,1,0:T(8,128)(2,1)}), bf16[16,24,128]{2,1,0:T(8,128)(2,1)S(1)}, u32[]{:S(2)}, u32[]{:S(2)}) async-start(bf16[16,24,128]{2,1,0:T(8,128)(2,1)} %shard_map.98), calls=%async_computation.1 | async-start | bytes 196608 | tf_op jit(solution)/shard_map/all_to_all | solution.py:476

commit v6 on v5

--- a/solution.py
+++ b/solution.py
@@ -11,6 +11,7 @@
 C = 64
 NSX = 32
 NSY = 16
+STRIDE = 17
 
 
 def call(kernel, outs, *ins, scratch=(), flops=1000000, limit=16, hbm=(), out_space=pltpu.VMEM):
@@ -62,10 +63,11 @@
     copies = fetches((x_ref, ew_hbm, eb_hbm), (held, ew_ref, eb_ref), sem)
     even = even_of("sx")
     copies[0].wait()
-    buf[...] = held[...].reshape(C * 16, 128).astype(F32)
+    for c in range(C):
+        buf[pl.ds(STRIDE * c, 16), :] = held[c].astype(F32)
 
     def row(x):
-        return buf[pl.ds(x, C, stride=16), :]
+        return buf[pl.ds(x, C, stride=STRIDE), :]
 
     for k in range(2):
         low, high = row(k), row(14 + k)
@@ -145,24 +147,27 @@
     bb2_ref[...] = jnp.concatenate([bb[...], bb[...]], axis=1)
 
 
-def k_dec_weights(dw, db, wd_ref, bd_ref, s_ref):
-    arranged(dw, wd_ref, range(9))
-    bd_ref[...] = column(db)
+def k_dec_weights(dw_hbm, db_hbm, wd_ref, bd_ref, s_ref, dw, db, sem):
+    copies = fetches((dw_hbm, db_hbm), (dw, db), sem)
     j = lax.axis_index("sy")
-    row = lax.broadcasted_iota(jnp.int32, (32, 128), 0)
-    lane = lax.broadcasted_iota(jnp.int32, (32, 128), 1)
+    row = lax.broadcasted_iota(jnp.int32, (16, 128), 0)
+    lane = lax.broadcasted_iota(jnp.int32, (16, 128), 1)
     y, z = jnp.right_shift(lane, 4), jnp.bitwise_and(lane, 15)
-    cell_y = j - 1 + jnp.right_shift(row, 3)
-    zero = jnp.zeros((96, 128), BF)
+    cell_y = j - 1 + jnp.right_shift(row, 2)
+    zero = jnp.zeros((112, 128), BF)
     for b in range(3):
         wy = interp_weight(8 * j + y + (b - 1), cell_y, 8 * NSY, NSY)
-        wy = jnp.where(row < 24, wy, 0.0)
+        wy = jnp.where(row < 12, wy, 0.0)
         for c in range(3):
             for zo in range(2):
                 wz = interp_weight(z + (c - 1), 1 - zo, 16, 2)
                 at = pl.ds(128 * (3 * b + c), 128)
-                s_ref[pl.ds(128 * zo, 32), at] = (wy * wz).astype(BF)
-                s_ref[pl.ds(128 * zo + 32, 96), at] = zero
+                s_ref[pl.ds(128 * zo, 16), at] = (wy * wz).astype(BF)
+                s_ref[pl.ds(128 * zo + 16, 112), at] = zero
+    for copy in copies:
+        copy.wait()
+    arranged(dw, wd_ref, range(9))
+    bd_ref[...] = column(db)
 
 
 def taps_of(v, z):
@@ -228,7 +233,7 @@
 
 
 def k_interior(ft_ref, x_ref, w_ref, *refs):
-    sources, g_ref, targets, xm, sem = refs[:6], refs[6], refs[7:13], refs[13], refs[14]
+    sources, g_ref, targets, xm, sem = refs[:4], refs[4], refs[5:9], refs[9], refs[10]
     copies = fetches(sources, targets, sem)
     lane = lanes_of(C)
     z = jnp.bitwise_and(lane, 15)
@@ -272,14 +277,13 @@
         if 1 <= r <= 16:
             cell = (r - 1) // 8
             best[cell] = v if best[cell] is None else jnp.maximum(best[cell], v)
-    for cell in range(2):
-        m = best[cell].astype(BF).astype(F32)
-        for shift in (64, 32, 16, -1, -2, -4):
-            m = jnp.maximum(m, roll(m, shift))
-        best[cell] = m
-    first = lane == 0
-    both = [jnp.where(first, best[0], roll(best[1], 1)), jnp.where(first, roll(best[0], -8), roll(best[1], -7))]
-    pool_ref[...] = jnp.transpose(jnp.concatenate(both, axis=0))[:8]
+    halves = [jnp.maximum(m, roll(m, 64)) for m in best]
+    m = jnp.where(lane < 64, halves[0], halves[1])
+    for shift in (-32, -16, -1, -2, -4):
+        m = jnp.maximum(m, roll(m, shift))
+    m = jnp.transpose(m.astype(BF).astype(F32))
+    rows = [jnp.concatenate([m[64 * x : 64 * x + 1], m[64 * x + 8 : 64 * x + 9]], axis=1) for x in range(2)]
+    pool_ref[...] = jnp.concatenate(rows + [jnp.zeros((6, 128), F32)], axis=0)
 
 
 def k_decode(
@@ -327,12 +331,13 @@
     inner, outer = jnp.where(even, pair_ref[1, 0:2], pair_ref[0, 0:2]), outer_ref[0:2]
     left, right = jnp.where(even, outer, inner), jnp.where(even, inner, outer)
     message = jnp.concatenate([left, own_ref[0:2], right, jnp.zeros((2, 128), F32)], axis=0)
+    message = message.astype(BF)
     for i in range(NSY):
         out_ref[i] = message
 
 
 def k_bottleneck(p_ref, vt_ref, bb_ref, ow_ref, out_ref):
-    p = p_ref[...]
+    p = p_ref[...].astype(F32)
     pieces = []
     none = jnp.zeros((1, 8, 128), F32)
     for a in range(3):
@@ -347,24 +352,23 @@
             pieces.append(v.reshape(128, 128).astype(BF))
     h = dot_nt(jnp.concatenate(pieces, axis=1), vt_ref[...])
     h = jnp.maximum(h + bb_ref[...], 0.0).astype(BF)
-    low = dot(h, ow_ref[...]).astype(BF).astype(F32)
-    zero = jnp.zeros((8, 128), F32)
+    low = dot(h, ow_ref[...])
+    zero = jnp.zeros((4, 128), F32)
+    rows = [zero] + [low[8 * i : 8 * i + 4] for i in range(NSY)] + [zero, zero]
     for i in range(NSY):
-        before = low[8 * (i - 1) : 8 * i] if i else zero
-        after = low[8 * (i + 1) : 8 * (i + 2)] if i < NSY - 1 else zero
-        out_ref[i] = jnp.concatenate([before, low[8 * i : 8 * i + 8], after], axis=0).astype(BF)
+        out_ref[i] = jnp.concatenate(rows[i : i + 3] + [zero], axis=0).astype(BF)
 
 
 def k_final(parts_ref, s_ref, w_ref, d_ref, out_ref, xt, q_ref, buf, done, sem):
     total = parts_ref[0].astype(F32)
     for i in range(1, NSY):
         total = total + parts_ref[i].astype(F32)
-    total = jnp.concatenate([total, jnp.zeros((104, 128), F32)], axis=0)
+    total = jnp.concatenate([total, jnp.zeros((112, 128), F32)], axis=0)
     lt = jnp.transpose(total)
     lane = lanes_of(C)
     left = []
     for cell in range(4):
-        here = jnp.bitwise_and(lane, 7) == cell
+        here = jnp.bitwise_and(lane, 3) == cell
         left.append(jnp.concatenate([jnp.where(here, lt[:C], 0.0), jnp.where(here, lt[C:], 0.0)], axis=1).astype(BF))
     t = dot(jnp.concatenate(left, axis=0), s_ref[...])
     for cell in range(4):
@@ -394,9 +398,10 @@
                 at = pl.ds(C * a + rows * part, rows)
                 v = v + w_low * q_ref[cell, at, :]
                 v = v + w_high * q_ref[cell + 1, at, :]
-            buf[part, pl.ds(x, rows, stride=16), :] = v
+            buf[part, pl.ds(x, rows, stride=STRIDE), :] = v
         at = pl.ds(rows * part, rows)
-        done[at] = buf[part].reshape(rows, 16, 128).astype(BF)
+        for o in range(rows):
+            done[rows * part + o] = buf[part, pl.ds(STRIDE * o, 16), :].astype(BF)
         copy = pltpu.make_async_copy(done.at[at], out_ref.at[at], sem.at[part])
         copy.start()
         copies.append(copy)
@@ -417,19 +422,13 @@
 
 def per_device(features, enc_weight, enc_bias, proj_weight, bottle_weight, bottle_bias, out_weight, dec_weight, dec_bias):
     first = (features, enc_weight.reshape(27, C, C), enc_bias.reshape(1, C))
-    later = (
-        dec_weight.reshape(27, C, C),
-        dec_bias.reshape(1, C),
-        bottle_weight.reshape(27 * 32, 512),
-        proj_weight,
-        out_weight,
-        bottle_bias.reshape(1, 32),
-    )
+    deep = (bottle_weight.reshape(27 * 32, 512), proj_weight, out_weight, bottle_bias.reshape(1, 32))
+    last = (dec_weight.reshape(27, C, C), dec_bias.reshape(1, C))
     ft, inner, outer, ew, eb = call(
         k_features,
         (S((18, C, 128), BF), S((2, C, 128), BF), S((2, C, 128), BF)) + tuple(S(v.shape, v.dtype) for v in first[1:]),
         *first,
-        scratch=[pltpu.VMEM((C, 16, 128), BF), pltpu.VMEM((C * 16, 128), F32), pltpu.SemaphoreType.DMA((3,))],
+        scratch=[pltpu.VMEM((C, 16, 128), BF), pltpu.VMEM((C * STRIDE, 128), F32), pltpu.SemaphoreType.DMA((3,))],
         hbm=range(3),
     )
     outer, pair = swapped(outer, "sx", 1), paired(inner, "sx")
@@ -438,22 +437,27 @@
     )
     xh, fl, fr, inner, outer = call(k_faces, (S((4, C, 128), BF),) + (S((5, C, 128), BF),) * 4, pair, outer, ft)
     outer, inner = swapped(outer, "sy", 1), swapped(inner, "sy", 0)
-    product, *later = call(
+    product, *deep = call(
         k_interior,
-        (S((20, 3 * C + 8, 128), F32),) + tuple(S(v.shape, v.dtype) for v in later),
+        (S((20, 3 * C + 8, 128), F32),) + tuple(S(v.shape, v.dtype) for v in deep),
         ft,
         xh,
         we,
-        *later,
-        scratch=[pltpu.VMEM((20, 9, C + 16, 128), BF), pltpu.SemaphoreType.DMA((6,))],
+        *deep,
+        scratch=[pltpu.VMEM((20, 9, C + 16, 128), BF), pltpu.SemaphoreType.DMA((4,))],
         flops=4 * 10**8,
-        hbm=range(3, 9),
+        hbm=range(3, 7),
     )
     em, pooled = call(k_encode, (S((18, C, 128), BF), S((8, 128), F32)), product, inner, outer, wedge, be)
     p_outer, p_pair = swapped(pooled, "sx", 1), paired(pooled, "sx")
-    vt, ow2, bb2 = call(k_weights, (S((C, 9 * 128), BF), S((C, 128), BF), S((1, C), F32)), *later[2:], flops=4 * 10**8)
+    vt, ow2, bb2 = call(k_weights, (S((C, 9 * 128), BF), S((C, 128), BF), S((1, C), F32)), *deep, flops=4 * 10**8)
     wd, bd, smat = call(
-        k_dec_weights, (S((3 * C, 9 * C), BF), S((C, 128), F32), S((256, 9 * 128), BF)), *later[:2], flops=10**8
+        k_dec_weights,
+        (S((3 * C, 9 * C), BF), S((C, 128), F32), S((256, 9 * 128), BF)),
+        *last,
+        scratch=[pltpu.VMEM(v.shape, v.dtype) for v in last] + [pltpu.SemaphoreType.DMA((2,))],
+        flops=10**8,
+        hbm=(0, 1),
     )
     d = call(
         k_decode,
@@ -470,9 +474,9 @@
         scratch=[pltpu.VMEM((18, 9, C + 16, 128), BF), pltpu.VMEM((18, 3 * C + 8, 128), F32)],
         flops=4 * 10**8,
     )
-    message = call(k_message, S((NSY, 8, 128), F32), p_pair, pooled, p_outer)
+    message = call(k_message, S((NSY, 8, 128), BF), p_pair, pooled, p_outer)
     everyone = lax.all_to_all(message, "sy", 0, 0, tiled=True)
-    partial = call(k_bottleneck, S((NSY, 24, 128), BF), everyone, vt, bb2, ow2)
+    partial = call(k_bottleneck, S((NSY, 16, 128), BF), everyone, vt, bb2, ow2)
     parts = lax.all_to_all(partial, "sy", 0, 0, tiled=True)
     return call(
         k_final,
@@ -484,7 +488,7 @@
         scratch=[
             pltpu.VMEM((4, 9, C + 16, 128), BF),
             pltpu.VMEM((4, 3 * C + 8, 128), F32),
-            pltpu.VMEM((4, 256, 128), F32),
+            pltpu.VMEM((4, 16 * STRIDE, 128), F32),
             pltpu.VMEM((C, 16, 128), BF),
             pltpu.SemaphoreType.DMA((4,)),
         ],

time: 56.1 us -> 55.8 us (level)
  the two profiles are of different devices: /device:TPU:224 before, /device:TPU:96 now
where the time goes in v6:
time: 55.8 us; the launch traced here: 55.5 us
  starting transfers between devices  22.9 us (41%)
  Pallas kernels  11.9 us (21%)
  waiting for transfers between devices  11.3 us (20%)
  blocking collectives  9.15 us (16%)
    pallas_call x11, Pallas kernels, call(): pl.pallas_call(kernel, out_shape=outs, in_specs=[pl.BlockSpec(memory_spac...  11.9 us
    all_to_all x1, starting transfers between devices, per_device(): everyone = lax.all_to_all(message, 'sy', 0, 0, tiled=True)  11.4 us
    all_gather x2, blocking collectives, paired(): return lax.all_gather(v, axis, axis_index_groups=pairs)  9.15 us
    ppermute x4, starting transfers between devices, swapped(): lax.ppermute(v, axis, [(i, i + 1) for i in low] + [(i + 1, i) for i in low])  8.02 us
    all_to_all x1, waiting for transfers between devices, per_device(): everyone = lax.all_to_all(message, 'sy', 0, 0, tiled=True)  7.22 us
    all_to_all x1, waiting for transfers between devices, per_device(): parts = lax.all_to_all(partial, 'sy', 0, 0, tiled=True)  4.03 us
    all_to_all x1, starting transfers between devices, per_device(): parts = lax.all_to_all(partial, 'sy', 0, 0, tiled=True)  3.5 us
  transfers between devices with their start and end apart: 6, of which 3 were waited for; matrix products, arithmetic and copies ran while one was open for 0% of the time, Pallas kernels for 11%

profile of v6, /device:TPU:96, one launch (start us, length us, event | category | flops | bytes accessed | tf_op | source)
XLA Modules:
  0.0 55.5 jit_solution(4479922535677979574)
XLA Ops:
  0.0 1.1 %shard_map.91 = (bf16[18,64,128]{2,1,0:T(8,128)(2,1)S(1)}, bf16[2,64,128]{2,1,0:T(8,128)(2,1)S(1)}, bf16[2,64,128]{2,1,0:T(8,128)(2,1)S(1)}, bf16[27,64,64]{2,1,0:T(8,128)(2,1)S(1)}, f32[1,64]{1,0:T(1,128)S(1)}) custom-call(bf16[64,16,128]{2,1,0:T(8,128)(2,1)} %x_ref.1, bf16[27,64,64]{2,1,0:T(8,128)(2,1)} %bitcast.11, f32[1,64]{1,0:T(1,128)} %bitcast.13), custom_call_target="tpu_custom_call" | custom-call | flops 1000000 | bytes 100000 | tf_op jit(solution)/shard_map/pallas_call | solution.py:19
  1.1 1.9 %collective-permute-start = (bf16[2,64,128]{2,1,0:T(8,128)(2,1)S(1)}, bf16[2,64,128]{2,1,0:T(8,128)(2,1)S(1)}, u32[]{:S(2)}, u32[]{:S(2)}) collective-permute-start(bf16[2,64,128]{2,1,0:T(8,128)(2,1)S(1)} %get-tuple-element.33), channel_id=1, source_target_pairs={{16,32},{48,64},{80,96},{112,128},{144,160},{176,192},{208,224},{2... | collective-permute-start | bytes 98312 | tf_op jit(solution)/shard_map/ppermute | solution.py:415
  3.1 4.7 %all-gather = bf16[4,64,128]{2,1,0:T(8,128)(2,1)S(1)} all-gather(bf16[2,64,128]{2,1,0:T(8,128)(2,1)S(1)} %get-tuple-element.32), channel_id=2, replica_groups={{0,16},{32,48},{64,80},{96,112},{128,144},{160,176},{192,208},{224,240}..., dimensions={0}, use_global_device_ids=true | all-gather | bytes 98304 | tf_op jit(solution)/shard_map/all_gather | solution.py:420
  7.8 0.0 collective-permute-done.outer_ref
  7.8 0.2 shard_map.92
  8.0 3.5 %collective-permute-start.1 = (bf16[5,64,128]{2,1,0:T(8,128)(2,1)S(1)}, bf16[5,64,128]{2,1,0:T(8,128)(2,1)S(1)}, u32[]{:S(2)}, u32[]{:S(2)}) collective-permute-start(bf16[5,64,128]{2,1,0:T(8,128)(2,1)S(1)} %get-tuple-element.39), channel_id=1, source_target_pairs={{0,1},{2,3},{4,5},{6,7},{8,9},{10,11},{12,13},{14,15},{1,0},{3,2},... | collective-permute-start | bytes 245768 | tf_op jit(solution)/shard_map/ppermute | solution.py:415
  11.5 0.7 %collective-permute-start.2 = (bf16[5,64,128]{2,1,0:T(8,128)(2,1)S(1)}, bf16[5,64,128]{2,1,0:T(8,128)(2,1)S(1)}, u32[]{:S(2)}, u32[]{:S(2)}) collective-permute-start(bf16[5,64,128]{2,1,0:T(8,128)(2,1)S(1)} %get-tuple-element.40), channel_id=1, source_target_pairs={{1,2},{3,4},{5,6},{7,8},{9,10},{11,12},{13,14},{2,1},{4,3},{6,5},{... | collective-permute-start | bytes 245768 | tf_op jit(solution)/shard_map/ppermute | solution.py:415
  12.2 0.2 shard_map.93
  12.4 2.2 %shard_map.94 = (f32[20,200,128]{2,1,0:T(8,128)S(1)}, bf16[864,512]{1,0:T(8,128)(2,1)S(1)}, bf16[64,512]{1,0:T(8,128)(2,1)S(1)}, bf16[32,64]{1,0:T(8,128)(2,1)S(1)}, f32[1,32]{1,0:T(1,128)S(1)}) custom-call(bf16[18,64,128]{2,1,0:T(8,128)(2,1)S(1)} %get-tuple-element.31.ft_ref, bf16[4,64,128]{2,1,0:T(8,128)(2,1)S(1)} %get-tuple-element.34.x_ref, ...), custom_call_target="tpu_custom_call" | custom-call | flops 400000000 | bytes 100000 | tf_op jit(solution)/shard_map/pallas_call | solution.py:19
  14.5 0.1 collective-permute-done.1.inner_ref
  14.6 0.0 collective-permute-done.2.outer_ref
  14.6 1.2 %shard_map.95 = (bf16[18,64,128]{2,1,0:T(8,128)(2,1)S(1)}, f32[8,128]{1,0:T(8,128)S(1)}) custom-call(f32[20,200,128]{2,1,0:T(8,128)S(1)} %get-tuple-element.38.g_ref, bf16[5,64,128]{2,1,0:T(8,128)(2,1)S(1)} %collective-permute-done.1.inner_ref, bf16[5,64,128]{2,1,0:T(8,128)(2,1)S(1)} %collective-permute-done.2.outer_ref, ...), custom_call_target="tpu_custom_call" | custom-call | flops 1000000 | bytes 100000 | tf_op jit(solution)/shard_map/pallas_call | solution.py:19
  15.8 1.9 %collective-permute-start.3 = (f32[8,128]{1,0:T(8,128)S(1)}, f32[8,128]{1,0:T(8,128)S(1)}, u32[]{:S(2)}, u32[]{:S(2)}) collective-permute-start(f32[8,128]{1,0:T(8,128)S(1)} %get-tuple-element.43.own_ref), channel_id=1, source_target_pairs={{16,32},{48,64},{80,96},{112,128},{144,160},{176,192},{208,224},{2... | collective-permute-start | bytes 12296 | tf_op jit(solution)/shard_map/ppermute | solution.py:415
  17.7 4.4 %all-gather.1 = f32[16,128]{1,0:T(8,128)S(1)} all-gather(f32[8,128]{1,0:T(8,128)S(1)} %get-tuple-element.43.own_ref), channel_id=3, replica_groups={{0,16},{32,48},{64,80},{96,112},{128,144},{160,176},{192,208},{224,240}..., dimensions={0}, use_global_device_ids=true | all-gather | bytes 12288 | tf_op jit(solution)/shard_map/all_gather | solution.py:420
  22.2 0.6 %shard_map.96 = bf16[16,8,128]{2,1,0:T(8,128)(2,1)} custom-call(f32[2,8,128]{2,1,0:T(8,128)S(1)} %bitcast.9, f32[8,128]{1,0:T(8,128)S(1)} %get-tuple-element.43.own_ref, f32[8,128]{1,0:T(8,128)S(1)} %collective-permute-done.3.outer_ref), custom_call_target="tpu_custom_call" | custom-call | flops 1000000 | bytes 100000 | tf_op jit(solution)/shard_map/pallas_call | solution.py:19
  22.8 11.4 %all-to-all-start = ((bf16[16,8,128]{2,1,0:T(8,128)(2,1)}), bf16[16,8,128]{2,1,0:T(8,128)(2,1)S(1)}, u32[]{:S(2)}, u32[]{:S(2)}) async-start(bf16[16,8,128]{2,1,0:T(8,128)(2,1)} %shard_map.96), calls=%async_computation | async-start | bytes 65536 | tf_op jit(solution)/shard_map/all_to_all | solution.py:478
  34.2 0.4 shard_map.97
  34.6 7.2 %all-to-all-done.p_ref = bf16[16,8,128]{2,1,0:T(8,128)(2,1)S(1)} async-done(((bf16[16,8,128]{2,1,0:T(8,128)(2,1)}), bf16[16,8,128]{2,1,0:T(8,128)(2,1)S(1)}, u32[]{:S(2)}, u32[]{:S(2)}) %all-to-all-start) | async-done | bytes 32800 | tf_op jit(solution)/shard_map/all_to_all | solution.py:478
  41.8 1.0 %shard_map.98 = bf16[16,16,128]{2,1,0:T(8,128)(2,1)} custom-call(bf16[16,8,128]{2,1,0:T(8,128)(2,1)S(1)} %all-to-all-done.p_ref, bf16[64,1152]{1,0:T(8,128)(2,1)S(1)} %get-tuple-element.48.vt_ref, f32[1,64]{1,0:T(1,128)S(1)} %get-tuple-element.49.bb_ref, bf16[64,128]{1,0:T(8,128)(2,1)S(1)} %get-tuple-element.50.ow_ref), custom_call_target="tpu_custom_call" | custom-call | flops 1000000 | bytes 100000 | tf_op jit(solution)/shard_map/pallas_call | solution.py:19
  42.8 3.5 %all-to-all-start.1 = ((bf16[16,16,128]{2,1,0:T(8,128)(2,1)}), bf16[16,16,128]{2,1,0:T(8,128)(2,1)S(1)}, u32[]{:S(2)}, u32[]{:S(2)}) async-start(bf16[16,16,128]{2,1,0:T(8,128)(2,1)} %shard_map.98), calls=%async_computation.1 | async-start | bytes 131072 | tf_op jit(solution)/shard_map/all_to_all | solution.py:480
  46.3 1.2 %shard_map.99 = (bf16[192,576]{1,0:T(8,128)(2,1)S(1)}, f32[64,128]{1,0:T(8,128)S(1)}, bf16[256,1152]{1,0:T(8,128)(2,1)S(1)}) custom-call(bf16[27,64,64]{2,1,0:T(8,128)(2,1)} %bitcast.12, f32[1,64]{1,0:T(1,128)} %bitcast.15), custom_call_target="tpu_custom_call" | custom-call | flops 100000000 | bytes 100000 | tf_op jit(solution)/shard_map/pallas_call | solution.py:19
  47.5 2.4 %shard_map.100.d_ref = f32[16,64,128]{2,1,0:T(8,128)S(1)} custom-call(bf16[5,64,128]{2,1,0:T(8,128)(2,1)S(1)} %get-tuple-element.53.fl_ref, bf16[5,64,128]{2,1,0:T(8,128)(2,1)S(1)} %get-tuple-element.54.fr_ref, bf16[5,64,128]{2,1,0:T(8,128)(2,1)S(1)} %collective-permute-done.1.inner_ref, bf16[5,64,128]{2,1,0:T(8,128)(2,1)S(1)} %collective-permute-done.2.outer_ref, ...), custom_call_target="tpu_custom_call" | custom-call | flops 400000000 | bytes 100000 | tf_op jit(solution)/shard_map/pallas_call | solution.py:19
  49.9 4.0 %all-to-all-done.1.parts_ref = bf16[16,16,128]{2,1,0:T(8,128)(2,1)S(1)} async-done(((bf16[16,16,128]{2,1,0:T(8,128)(2,1)}), bf16[16,16,128]{2,1,0:T(8,128)(2,1)S(1)}, u32[]{:S(2)}, u32[]{:S(2)}) %all-to-all-start.1) | async-done | bytes 65568 | tf_op jit(solution)/shard_map/all_to_all | solution.py:480
  53.9 1.5 %shard_map.101 = bf16[64,16,128]{2,1,0:T(8,128)(2,1)} custom-call(bf16[16,16,128]{2,1,0:T(8,128)(2,1)S(1)} %all-to-all-done.1.parts_ref, bf16[256,1152]{1,0:T(8,128)(2,1)S(1)} %get-tuple-element.51.s_ref, bf16[192,576]{1,0:T(8,128)(2,1)S(1)} %get-tuple-element.52.w_ref, f32[16,64,128]{2,1,0:T(8,128)S(1)} %shard_map.100.d_ref), custom_call_target="tpu_custom_call" | custom-call | flops 1000000 | bytes 100000 | tf_op jit(solution)/shard_map/pallas_call | solution.py:19
  (1 shorter events, 0.0 us)
Async XLA Ops:
  1.1 6.7 %collective-permute-start = (bf16[2,64,128]{2,1,0:T(8,128)(2,1)S(1)}, bf16[2,64,128]{2,1,0:T(8,128)(2,1)S(1)}, u32[]{:S(2)}, u32[]{:S(2)}) collective-permute-start(bf16[2,64,128]{2,1,0:T(8,128)(2,1)S(1)} %get-tuple-element.33), channel_id=1, source_target_pairs={{16,32},{48,64},{80,96},{112,128},{144,160},{176,192},{208,224},{2... | collective-permute-start | bytes 98312 | tf_op jit(solution)/shard_map/ppermute | solution.py:415
  8.0 6.6 %collective-permute-start.1 = (bf16[5,64,128]{2,1,0:T(8,128)(2,1)S(1)}, bf16[5,64,128]{2,1,0:T(8,128)(2,1)S(1)}, u32[]{:S(2)}, u32[]{:S(2)}) collective-permute-start(bf16[5,64,128]{2,1,0:T(8,128)(2,1)S(1)} %get-tuple-element.39), channel_id=1, source_target_pairs={{0,1},{2,3},{4,5},{6,7},{8,9},{10,11},{12,13},{14,15},{1,0},{3,2},... | collective-permute-start | bytes 245768 | tf_op jit(solution)/shard_map/ppermute | solution.py:415
  11.5 3.1 %collective-permute-start.2 = (bf16[5,64,128]{2,1,0:T(8,128)(2,1)S(1)}, bf16[5,64,128]{2,1,0:T(8,128)(2,1)S(1)}, u32[]{:S(2)}, u32[]{:S(2)}) collective-permute-start(bf16[5,64,128]{2,1,0:T(8,128)(2,1)S(1)} %get-tuple-element.40), channel_id=1, source_target_pairs={{1,2},{3,4},{5,6},{7,8},{9,10},{11,12},{13,14},{2,1},{4,3},{6,5},{... | collective-permute-start | bytes 245768 | tf_op jit(solution)/shard_map/ppermute | solution.py:415
  15.8 6.4 %collective-permute-start.3 = (f32[8,128]{1,0:T(8,128)S(1)}, f32[8,128]{1,0:T(8,128)S(1)}, u32[]{:S(2)}, u32[]{:S(2)}) collective-permute-start(f32[8,128]{1,0:T(8,128)S(1)} %get-tuple-element.43.own_ref), channel_id=1, source_target_pairs={{16,32},{48,64},{80,96},{112,128},{144,160},{176,192},{208,224},{2... | collective-permute-start | bytes 12296 | tf_op jit(solution)/shard_map/ppermute | solution.py:415
  22.8 19.0 %all-to-all-start = ((bf16[16,8,128]{2,1,0:T(8,128)(2,1)}), bf16[16,8,128]{2,1,0:T(8,128)(2,1)S(1)}, u32[]{:S(2)}, u32[]{:S(2)}) async-start(bf16[16,8,128]{2,1,0:T(8,128)(2,1)} %shard_map.96), calls=%async_computation | async-start | bytes 65536 | tf_op jit(solution)/shard_map/all_to_all | solution.py:478
  42.8 11.1 %all-to-all-start.1 = ((bf16[16,16,128]{2,1,0:T(8,128)(2,1)}), bf16[16,16,128]{2,1,0:T(8,128)(2,1)S(1)}, u32[]{:S(2)}, u32[]{:S(2)}) async-start(bf16[16,16,128]{2,1,0:T(8,128)(2,1)} %shard_map.98), calls=%async_computation.1 | async-start | bytes 131072 | tf_op jit(solution)/shard_map/all_to_all | solution.py:480

commit v7 on v6

--- a/solution.py
+++ b/solution.py
@@ -89,7 +89,7 @@
     for g in range(5):
         left = None
         for q in range(4):
-            r = 4 * g + q
+            r = 5 * q + g
             v = x_ref[r] if r < 2 else ft_ref[r] if r < 18 else x_ref[r - 16]
             v = v.astype(F32)
             a, b = roll(v, 32 * q), roll(v, 32 * q - 96)
@@ -207,11 +207,11 @@
     return g_ref[r, pl.ds(0, C), :] + g_ref[r + 1, pl.ds(C, C), :] + g_ref[r + 2, pl.ds(2 * C, C), :]
 
 
-def summed_packed(packed, g, lane):
+def summed_packed(packed, g):
     v = packed[g][:C]
     for a in (1, 2):
-        this, after = packed[g][a * C : a * C + C], packed[min(g + 1, 4)][a * C : a * C + C]
-        v = v + roll(jnp.where(lane < 32 * a, after, this), -32 * a)
+        tap = packed[(g + a) % 5][a * C : a * C + C]
+        v = v + (tap if g + a < 5 else roll(tap, -32))
     return v
 
 
@@ -263,11 +263,10 @@
     packed = packed_products(w_ref[...], blocks)
     bias = bias_ref[...]
     best = [None, None]
+    at_edge = [summed_packed(packed, g) for g in range(5)]
     for r in range(18):
-        if r % 4 == 0:
-            at_edge = summed_packed(packed, r // 4, lane)
         v = summed(g_ref, r) + bias
-        v = v + jnp.where(edge, roll(at_edge, -(32 * (r % 4) + 16)), 0.0)
+        v = v + jnp.where(edge, roll(at_edge[r % 5], -(32 * (r // 5) + 16)), 0.0)
         v = jnp.maximum(v, 0.0)
         if r == 0:
             v = jnp.where(s == 0, 0.0, v)
@@ -307,16 +306,16 @@
     outside = (even & (j == NSY - 1)) | (~even & (j == 0))
     halo = []
     for g in range(5):
-        v = summed_packed(packed, g, lane) + be_ref[...]
+        v = summed_packed(packed, g) + be_ref[...]
         v = jnp.where(outside, 0.0, jnp.maximum(v, 0.0))
         if g == 0:
             v = jnp.where((lane < 32) & (s == 0), 0.0, v)
-        if g == 4:
-            v = jnp.where((lane >= 64) | ((lane >= 32) & (s == NSX - 1)), 0.0, v)
+        if g == 2:
+            v = jnp.where((lane >= 96) & (s == NSX - 1), 0.0, v)
         halo.append(v.astype(BF))
     for r in range(18):
         v = em_ref[r]
-        beside = roll(halo[r // 4], -(32 * (r % 4) + 16))
+        beside = roll(halo[r % 5], -(32 * (r // 5) + 16))
         put_taps(
             [jnp.where(lane < 16, beside, roll(v, 16)), v, jnp.where(lane >= 112, beside, roll(v, -16))], xm, r, z
         )

time: 55.8 us -> 55.8 us (level)
  no operation moved by 1% of the time
where the time goes in v7:
time: 55.8 us; the launch traced here: 55.4 us
  starting transfers between devices  22.9 us (41%)
  Pallas kernels  11.9 us (21%)
  waiting for transfers between devices  11.3 us (20%)
  blocking collectives  9.16 us (16%)
    pallas_call x11, Pallas kernels, call(): pl.pallas_call(kernel, out_shape=outs, in_specs=[pl.BlockSpec(memory_spac...  11.9 us
    all_to_all x1, starting transfers between devices, per_device(): everyone = lax.all_to_all(message, 'sy', 0, 0, tiled=True)  11.4 us
    all_gather x2, blocking collectives, paired(): return lax.all_gather(v, axis, axis_index_groups=pairs)  9.16 us
    ppermute x4, starting transfers between devices, swapped(): lax.ppermute(v, axis, [(i, i + 1) for i in low] + [(i + 1, i) for i in low])  8.02 us
    all_to_all x1, waiting for transfers between devices, per_device(): everyone = lax.all_to_all(message, 'sy', 0, 0, tiled=True)  7.23 us
    all_to_all x1, waiting for transfers between devices, per_device(): parts = lax.all_to_all(partial, 'sy', 0, 0, tiled=True)  4.02 us
    all_to_all x1, starting transfers between devices, per_device(): parts = lax.all_to_all(partial, 'sy', 0, 0, tiled=True)  3.5 us
  transfers between devices with their start and end apart: 6, of which 3 were waited for; matrix products, arithmetic and copies ran while one was open for 0% of the time, Pallas kernels for 11%

profile of v7, /device:TPU:96, one launch (start us, length us, event | category | flops | bytes accessed | tf_op | source)
XLA Modules:
  0.0 55.4 jit_solution(2820380836539087202)
XLA Ops:
  0.0 1.1 %shard_map.91 = (bf16[18,64,128]{2,1,0:T(8,128)(2,1)S(1)}, bf16[2,64,128]{2,1,0:T(8,128)(2,1)S(1)}, bf16[2,64,128]{2,1,0:T(8,128)(2,1)S(1)}, bf16[27,64,64]{2,1,0:T(8,128)(2,1)S(1)}, f32[1,64]{1,0:T(1,128)S(1)}) custom-call(bf16[64,16,128]{2,1,0:T(8,128)(2,1)} %x_ref.1, bf16[27,64,64]{2,1,0:T(8,128)(2,1)} %bitcast.11, f32[1,64]{1,0:T(1,128)} %bitcast.13), custom_call_target="tpu_custom_call" | custom-call | flops 1000000 | bytes 100000 | tf_op jit(solution)/shard_map/pallas_call | solution.py:19
  1.1 1.9 %collective-permute-start = (bf16[2,64,128]{2,1,0:T(8,128)(2,1)S(1)}, bf16[2,64,128]{2,1,0:T(8,128)(2,1)S(1)}, u32[]{:S(2)}, u32[]{:S(2)}) collective-permute-start(bf16[2,64,128]{2,1,0:T(8,128)(2,1)S(1)} %get-tuple-element.33), channel_id=1, source_target_pairs={{16,32},{48,64},{80,96},{112,128},{144,160},{176,192},{208,224},{2... | collective-permute-start | bytes 98312 | tf_op jit(solution)/shard_map/ppermute | solution.py:414
  3.1 4.7 %all-gather = bf16[4,64,128]{2,1,0:T(8,128)(2,1)S(1)} all-gather(bf16[2,64,128]{2,1,0:T(8,128)(2,1)S(1)} %get-tuple-element.32), channel_id=2, replica_groups={{0,16},{32,48},{64,80},{96,112},{128,144},{160,176},{192,208},{224,240}..., dimensions={0}, use_global_device_ids=true | all-gather | bytes 98304 | tf_op jit(solution)/shard_map/all_gather | solution.py:419
  7.8 0.0 collective-permute-done.outer_ref
  7.8 0.2 shard_map.92
  8.0 3.5 %collective-permute-start.1 = (bf16[5,64,128]{2,1,0:T(8,128)(2,1)S(1)}, bf16[5,64,128]{2,1,0:T(8,128)(2,1)S(1)}, u32[]{:S(2)}, u32[]{:S(2)}) collective-permute-start(bf16[5,64,128]{2,1,0:T(8,128)(2,1)S(1)} %get-tuple-element.39), channel_id=1, source_target_pairs={{0,1},{2,3},{4,5},{6,7},{8,9},{10,11},{12,13},{14,15},{1,0},{3,2},... | collective-permute-start | bytes 245768 | tf_op jit(solution)/shard_map/ppermute | solution.py:414
  11.5 0.7 %collective-permute-start.2 = (bf16[5,64,128]{2,1,0:T(8,128)(2,1)S(1)}, bf16[5,64,128]{2,1,0:T(8,128)(2,1)S(1)}, u32[]{:S(2)}, u32[]{:S(2)}) collective-permute-start(bf16[5,64,128]{2,1,0:T(8,128)(2,1)S(1)} %get-tuple-element.40), channel_id=1, source_target_pairs={{1,2},{3,4},{5,6},{7,8},{9,10},{11,12},{13,14},{2,1},{4,3},{6,5},{... | collective-permute-start | bytes 245768 | tf_op jit(solution)/shard_map/ppermute | solution.py:414
  12.2 0.2 shard_map.93
  12.4 2.2 %shard_map.94 = (f32[20,200,128]{2,1,0:T(8,128)S(1)}, bf16[864,512]{1,0:T(8,128)(2,1)S(1)}, bf16[64,512]{1,0:T(8,128)(2,1)S(1)}, bf16[32,64]{1,0:T(8,128)(2,1)S(1)}, f32[1,32]{1,0:T(1,128)S(1)}) custom-call(bf16[18,64,128]{2,1,0:T(8,128)(2,1)S(1)} %get-tuple-element.31.ft_ref, bf16[4,64,128]{2,1,0:T(8,128)(2,1)S(1)} %get-tuple-element.34.x_ref, ...), custom_call_target="tpu_custom_call" | custom-call | flops 400000000 | bytes 100000 | tf_op jit(solution)/shard_map/pallas_call | solution.py:19
  14.5 0.1 collective-permute-done.1.inner_ref
  14.6 0.0 collective-permute-done.2.outer_ref
  14.6 1.1 %shard_map.95 = (bf16[18,64,128]{2,1,0:T(8,128)(2,1)S(1)}, f32[8,128]{1,0:T(8,128)S(1)}) custom-call(f32[20,200,128]{2,1,0:T(8,128)S(1)} %get-tuple-element.38.g_ref, bf16[5,64,128]{2,1,0:T(8,128)(2,1)S(1)} %collective-permute-done.1.inner_ref, bf16[5,64,128]{2,1,0:T(8,128)(2,1)S(1)} %collective-permute-done.2.outer_ref, ...), custom_call_target="tpu_custom_call" | custom-call | flops 1000000 | bytes 100000 | tf_op jit(solution)/shard_map/pallas_call | solution.py:19
  15.7 1.9 %collective-permute-start.3 = (f32[8,128]{1,0:T(8,128)S(1)}, f32[8,128]{1,0:T(8,128)S(1)}, u32[]{:S(2)}, u32[]{:S(2)}) collective-permute-start(f32[8,128]{1,0:T(8,128)S(1)} %get-tuple-element.43.own_ref), channel_id=1, source_target_pairs={{16,32},{48,64},{80,96},{112,128},{144,160},{176,192},{208,224},{2... | collective-permute-start | bytes 12296 | tf_op jit(solution)/shard_map/ppermute | solution.py:414
  17.7 4.4 %all-gather.1 = f32[16,128]{1,0:T(8,128)S(1)} all-gather(f32[8,128]{1,0:T(8,128)S(1)} %get-tuple-element.43.own_ref), channel_id=3, replica_groups={{0,16},{32,48},{64,80},{96,112},{128,144},{160,176},{192,208},{224,240}..., dimensions={0}, use_global_device_ids=true | all-gather | bytes 12288 | tf_op jit(solution)/shard_map/all_gather | solution.py:419
  22.1 0.6 %shard_map.96 = bf16[16,8,128]{2,1,0:T(8,128)(2,1)} custom-call(f32[2,8,128]{2,1,0:T(8,128)S(1)} %bitcast.9, f32[8,128]{1,0:T(8,128)S(1)} %get-tuple-element.43.own_ref, f32[8,128]{1,0:T(8,128)S(1)} %collective-permute-done.3.outer_ref), custom_call_target="tpu_custom_call" | custom-call | flops 1000000 | bytes 100000 | tf_op jit(solution)/shard_map/pallas_call | solution.py:19
  22.7 11.4 %all-to-all-start = ((bf16[16,8,128]{2,1,0:T(8,128)(2,1)}), bf16[16,8,128]{2,1,0:T(8,128)(2,1)S(1)}, u32[]{:S(2)}, u32[]{:S(2)}) async-start(bf16[16,8,128]{2,1,0:T(8,128)(2,1)} %shard_map.96), calls=%async_computation | async-start | bytes 65536 | tf_op jit(solution)/shard_map/all_to_all | solution.py:477
  34.1 0.4 shard_map.97
  34.5 7.2 %all-to-all-done.p_ref = bf16[16,8,128]{2,1,0:T(8,128)(2,1)S(1)} async-done(((bf16[16,8,128]{2,1,0:T(8,128)(2,1)}), bf16[16,8,128]{2,1,0:T(8,128)(2,1)S(1)}, u32[]{:S(2)}, u32[]{:S(2)}) %all-to-all-start) | async-done | bytes 32800 | tf_op jit(solution)/shard_map/all_to_all | solution.py:477
  41.8 1.0 %shard_map.98 = bf16[16,16,128]{2,1,0:T(8,128)(2,1)} custom-call(bf16[16,8,128]{2,1,0:T(8,128)(2,1)S(1)} %all-to-all-done.p_ref, bf16[64,1152]{1,0:T(8,128)(2,1)S(1)} %get-tuple-element.48.vt_ref, f32[1,64]{1,0:T(1,128)S(1)} %get-tuple-element.49.bb_ref, bf16[64,128]{1,0:T(8,128)(2,1)S(1)} %get-tuple-element.50.ow_ref), custom_call_target="tpu_custom_call" | custom-call | flops 1000000 | bytes 100000 | tf_op jit(solution)/shard_map/pallas_call | solution.py:19
  42.8 3.5 %all-to-all-start.1 = ((bf16[16,16,128]{2,1,0:T(8,128)(2,1)}), bf16[16,16,128]{2,1,0:T(8,128)(2,1)S(1)}, u32[]{:S(2)}, u32[]{:S(2)}) async-start(bf16[16,16,128]{2,1,0:T(8,128)(2,1)} %shard_map.98), calls=%async_computation.1 | async-start | bytes 131072 | tf_op jit(solution)/shard_map/all_to_all | solution.py:479
  46.3 1.2 %shard_map.99 = (bf16[192,576]{1,0:T(8,128)(2,1)S(1)}, f32[64,128]{1,0:T(8,128)S(1)}, bf16[256,1152]{1,0:T(8,128)(2,1)S(1)}) custom-call(bf16[27,64,64]{2,1,0:T(8,128)(2,1)} %bitcast.12, f32[1,64]{1,0:T(1,128)} %bitcast.15), custom_call_target="tpu_custom_call" | custom-call | flops 100000000 | bytes 100000 | tf_op jit(solution)/shard_map/pallas_call | solution.py:19
  47.5 2.4 %shard_map.100.d_ref = f32[16,64,128]{2,1,0:T(8,128)S(1)} custom-call(bf16[5,64,128]{2,1,0:T(8,128)(2,1)S(1)} %get-tuple-element.53.fl_ref, bf16[5,64,128]{2,1,0:T(8,128)(2,1)S(1)} %get-tuple-element.54.fr_ref, bf16[5,64,128]{2,1,0:T(8,128)(2,1)S(1)} %collective-permute-done.1.inner_ref, bf16[5,64,128]{2,1,0:T(8,128)(2,1)S(1)} %collective-permute-done.2.outer_ref, ...), custom_call_target="tpu_custom_call" | custom-call | flops 400000000 | bytes 100000 | tf_op jit(solution)/shard_map/pallas_call | solution.py:19
  49.8 4.0 %all-to-all-done.1.parts_ref = bf16[16,16,128]{2,1,0:T(8,128)(2,1)S(1)} async-done(((bf16[16,16,128]{2,1,0:T(8,128)(2,1)}), bf16[16,16,128]{2,1,0:T(8,128)(2,1)S(1)}, u32[]{:S(2)}, u32[]{:S(2)}) %all-to-all-start.1) | async-done | bytes 65568 | tf_op jit(solution)/shard_map/all_to_all | solution.py:479
  53.9 1.5 %shard_map.101 = bf16[64,16,128]{2,1,0:T(8,128)(2,1)} custom-call(bf16[16,16,128]{2,1,0:T(8,128)(2,1)S(1)} %all-to-all-done.1.parts_ref, bf16[256,1152]{1,0:T(8,128)(2,1)S(1)} %get-tuple-element.51.s_ref, bf16[192,576]{1,0:T(8,128)(2,1)S(1)} %get-tuple-element.52.w_ref, f32[16,64,128]{2,1,0:T(8,128)S(1)} %shard_map.100.d_ref), custom_call_target="tpu_custom_call" | custom-call | flops 1000000 | bytes 100000 | tf_op jit(solution)/shard_map/pallas_call | solution.py:19
  (1 shorter events, 0.0 us)
Async XLA Ops:
  1.1 6.7 %collective-permute-start = (bf16[2,64,128]{2,1,0:T(8,128)(2,1)S(1)}, bf16[2,64,128]{2,1,0:T(8,128)(2,1)S(1)}, u32[]{:S(2)}, u32[]{:S(2)}) collective-permute-start(bf16[2,64,128]{2,1,0:T(8,128)(2,1)S(1)} %get-tuple-element.33), channel_id=1, source_target_pairs={{16,32},{48,64},{80,96},{112,128},{144,160},{176,192},{208,224},{2... | collective-permute-start | bytes 98312 | tf_op jit(solution)/shard_map/ppermute | solution.py:414
  8.0 6.6 %collective-permute-start.1 = (bf16[5,64,128]{2,1,0:T(8,128)(2,1)S(1)}, bf16[5,64,128]{2,1,0:T(8,128)(2,1)S(1)}, u32[]{:S(2)}, u32[]{:S(2)}) collective-permute-start(bf16[5,64,128]{2,1,0:T(8,128)(2,1)S(1)} %get-tuple-element.39), channel_id=1, source_target_pairs={{0,1},{2,3},{4,5},{6,7},{8,9},{10,11},{12,13},{14,15},{1,0},{3,2},... | collective-permute-start | bytes 245768 | tf_op jit(solution)/shard_map/ppermute | solution.py:414
  11.5 3.1 %collective-permute-start.2 = (bf16[5,64,128]{2,1,0:T(8,128)(2,1)S(1)}, bf16[5,64,128]{2,1,0:T(8,128)(2,1)S(1)}, u32[]{:S(2)}, u32[]{:S(2)}) collective-permute-start(bf16[5,64,128]{2,1,0:T(8,128)(2,1)S(1)} %get-tuple-element.40), channel_id=1, source_target_pairs={{1,2},{3,4},{5,6},{7,8},{9,10},{11,12},{13,14},{2,1},{4,3},{6,5},{... | collective-permute-start | bytes 245768 | tf_op jit(solution)/shard_map/ppermute | solution.py:414
  15.7 6.4 %collective-permute-start.3 = (f32[8,128]{1,0:T(8,128)S(1)}, f32[8,128]{1,0:T(8,128)S(1)}, u32[]{:S(2)}, u32[]{:S(2)}) collective-permute-start(f32[8,128]{1,0:T(8,128)S(1)} %get-tuple-element.43.own_ref), channel_id=1, source_target_pairs={{16,32},{48,64},{80,96},{112,128},{144,160},{176,192},{208,224},{2... | collective-permute-start | bytes 12296 | tf_op jit(solution)/shard_map/ppermute | solution.py:414
  22.7 19.0 %all-to-all-start = ((bf16[16,8,128]{2,1,0:T(8,128)(2,1)}), bf16[16,8,128]{2,1,0:T(8,128)(2,1)S(1)}, u32[]{:S(2)}, u32[]{:S(2)}) async-start(bf16[16,8,128]{2,1,0:T(8,128)(2,1)} %shard_map.96), calls=%async_computation | async-start | bytes 65536 | tf_op jit(solution)/shard_map/all_to_all | solution.py:477
  42.8 11.1 %all-to-all-start.1 = ((bf16[16,16,128]{2,1,0:T(8,128)(2,1)}), bf16[16,16,128]{2,1,0:T(8,128)(2,1)S(1)}, u32[]{:S(2)}, u32[]{:S(2)}) async-start(bf16[16,16,128]{2,1,0:T(8,128)(2,1)} %shard_map.98), calls=%async_computation.1 | async-start | bytes 131072 | tf_op jit(solution)/shard_map/all_to_all | solution.py:479

commit v8 on v7

--- a/solution.py
+++ b/solution.py
@@ -233,7 +233,7 @@
 
 
 def k_interior(ft_ref, x_ref, w_ref, *refs):
-    sources, g_ref, targets, xm, sem = refs[:4], refs[4], refs[5:9], refs[9], refs[10]
+    sources, g_ref, targets, xm, sem = refs[:3], refs[3], refs[4:7], refs[7], refs[8]
     copies = fetches(sources, targets, sem)
     lane = lanes_of(C)
     z = jnp.bitwise_and(lane, 15)
@@ -421,7 +421,7 @@
 
 def per_device(features, enc_weight, enc_bias, proj_weight, bottle_weight, bottle_bias, out_weight, dec_weight, dec_bias):
     first = (features, enc_weight.reshape(27, C, C), enc_bias.reshape(1, C))
-    deep = (bottle_weight.reshape(27 * 32, 512), proj_weight, out_weight, bottle_bias.reshape(1, 32))
+    deep = (proj_weight, out_weight, bottle_bias.reshape(1, 32))
     last = (dec_weight.reshape(27, C, C), dec_bias.reshape(1, C))
     ft, inner, outer, ew, eb = call(
         k_features,
@@ -443,13 +443,19 @@
         xh,
         we,
         *deep,
-        scratch=[pltpu.VMEM((20, 9, C + 16, 128), BF), pltpu.SemaphoreType.DMA((4,))],
+        scratch=[pltpu.VMEM((20, 9, C + 16, 128), BF), pltpu.SemaphoreType.DMA((3,))],
         flops=4 * 10**8,
-        hbm=range(3, 7),
+        hbm=range(3, 6),
     )
     em, pooled = call(k_encode, (S((18, C, 128), BF), S((8, 128), F32)), product, inner, outer, wedge, be)
     p_outer, p_pair = swapped(pooled, "sx", 1), paired(pooled, "sx")
-    vt, ow2, bb2 = call(k_weights, (S((C, 9 * 128), BF), S((C, 128), BF), S((1, C), F32)), *deep, flops=4 * 10**8)
+    vt, ow2, bb2 = call(
+        k_weights,
+        (S((C, 9 * 128), BF), S((C, 128), BF), S((1, C), F32)),
+        bottle_weight.reshape(27 * 32, 512),
+        *deep,
+        flops=4 * 10**8,
+    )
     wd, bd, smat = call(
         k_dec_weights,
         (S((3 * C, 9 * C), BF), S((C, 128), F32), S((256, 9 * 128), BF)),

time: 55.8 us -> 55.8 us (level)
  no operation moved by 1% of the time
where the time goes in v8:
time: 55.8 us; the launch traced here: 55.4 us
  starting transfers between devices  23.1 us (41%)
  Pallas kernels  11.7 us (21%)
  waiting for transfers between devices  11.5 us (21%)
  blocking collectives  9.03 us (16%)
    pallas_call x11, Pallas kernels, call(): pl.pallas_call(kernel, out_shape=outs, in_specs=[pl.BlockSpec(memory_spac...  11.7 us
    all_to_all x1, starting transfers between devices, per_device(): everyone = lax.all_to_all(message, 'sy', 0, 0, tiled=True)  11.5 us
    all_gather x2, blocking collectives, paired(): return lax.all_gather(v, axis, axis_index_groups=pairs)  9.03 us
    ppermute x4, starting transfers between devices, swapped(): lax.ppermute(v, axis, [(i, i + 1) for i in low] + [(i + 1, i) for i in low])  8.02 us
    all_to_all x1, waiting for transfers between devices, per_device(): everyone = lax.all_to_all(message, 'sy', 0, 0, tiled=True)  7.22 us
    all_to_all x1, waiting for transfers between devices, per_device(): parts = lax.all_to_all(partial, 'sy', 0, 0, tiled=True)  4.02 us
    all_to_all x1, starting transfers between devices, per_device(): parts = lax.all_to_all(partial, 'sy', 0, 0, tiled=True)  3.5 us
  transfers between devices with their start and end apart: 6, of which 3 were waited for; matrix products, arithmetic and copies ran while one was open for 0% of the time, Pallas kernels for 11%

profile of v8, /device:TPU:96, one launch (start us, length us, event | category | flops | bytes accessed | tf_op | source)
XLA Modules:
  0.0 55.4 jit_solution(4062036811166433371)
XLA Ops:
  0.0 1.1 %shard_map.91 = (bf16[18,64,128]{2,1,0:T(8,128)(2,1)S(1)}, bf16[2,64,128]{2,1,0:T(8,128)(2,1)S(1)}, bf16[2,64,128]{2,1,0:T(8,128)(2,1)S(1)}, bf16[27,64,64]{2,1,0:T(8,128)(2,1)S(1)}, f32[1,64]{1,0:T(1,128)S(1)}) custom-call(bf16[64,16,128]{2,1,0:T(8,128)(2,1)} %x_ref.1, bf16[27,64,64]{2,1,0:T(8,128)(2,1)} %bitcast.11, f32[1,64]{1,0:T(1,128)} %bitcast.13), custom_call_target="tpu_custom_call" | custom-call | flops 1000000 | bytes 100000 | tf_op jit(solution)/shard_map/pallas_call | solution.py:19
  1.1 1.9 %collective-permute-start = (bf16[2,64,128]{2,1,0:T(8,128)(2,1)S(1)}, bf16[2,64,128]{2,1,0:T(8,128)(2,1)S(1)}, u32[]{:S(2)}, u32[]{:S(2)}) collective-permute-start(bf16[2,64,128]{2,1,0:T(8,128)(2,1)S(1)} %get-tuple-element.32), channel_id=1, source_target_pairs={{16,32},{48,64},{80,96},{112,128},{144,160},{176,192},{208,224},{2... | collective-permute-start | bytes 98312 | tf_op jit(solution)/shard_map/ppermute | solution.py:414
  3.1 4.7 %all-gather = bf16[4,64,128]{2,1,0:T(8,128)(2,1)S(1)} all-gather(bf16[2,64,128]{2,1,0:T(8,128)(2,1)S(1)} %get-tuple-element.31), channel_id=2, replica_groups={{0,16},{32,48},{64,80},{96,112},{128,144},{160,176},{192,208},{224,240}..., dimensions={0}, use_global_device_ids=true | all-gather | bytes 98304 | tf_op jit(solution)/shard_map/all_gather | solution.py:419
  7.8 0.0 collective-permute-done.outer_ref
  7.8 0.2 shard_map.92
  8.0 3.5 %collective-permute-start.1 = (bf16[5,64,128]{2,1,0:T(8,128)(2,1)S(1)}, bf16[5,64,128]{2,1,0:T(8,128)(2,1)S(1)}, u32[]{:S(2)}, u32[]{:S(2)}) collective-permute-start(bf16[5,64,128]{2,1,0:T(8,128)(2,1)S(1)} %get-tuple-element.38), channel_id=1, source_target_pairs={{0,1},{2,3},{4,5},{6,7},{8,9},{10,11},{12,13},{14,15},{1,0},{3,2},... | collective-permute-start | bytes 245768 | tf_op jit(solution)/shard_map/ppermute | solution.py:414
  11.5 0.7 %collective-permute-start.2 = (bf16[5,64,128]{2,1,0:T(8,128)(2,1)S(1)}, bf16[5,64,128]{2,1,0:T(8,128)(2,1)S(1)}, u32[]{:S(2)}, u32[]{:S(2)}) collective-permute-start(bf16[5,64,128]{2,1,0:T(8,128)(2,1)S(1)} %get-tuple-element.39), channel_id=1, source_target_pairs={{1,2},{3,4},{5,6},{7,8},{9,10},{11,12},{13,14},{2,1},{4,3},{6,5},{... | collective-permute-start | bytes 245768 | tf_op jit(solution)/shard_map/ppermute | solution.py:414
  12.2 0.2 shard_map.93
  12.4 0.0 copy-start
  12.4 2.0 %shard_map.94 = (f32[20,200,128]{2,1,0:T(8,128)S(1)}, bf16[64,512]{1,0:T(8,128)(2,1)S(1)}, bf16[32,64]{1,0:T(8,128)(2,1)S(1)}, f32[1,32]{1,0:T(1,128)S(1)}) custom-call(bf16[18,64,128]{2,1,0:T(8,128)(2,1)S(1)} %get-tuple-element.30.ft_ref, bf16[4,64,128]{2,1,0:T(8,128)(2,1)S(1)} %get-tuple-element.33.x_ref, ...), custom_call_target="tpu_custom_call" | custom-call | flops 400000000 | bytes 100000 | tf_op jit(solution)/shard_map/pallas_call | solution.py:19
  14.4 0.2 collective-permute-done.1.inner_ref
  14.6 1.1 %shard_map.95 = (bf16[18,64,128]{2,1,0:T(8,128)(2,1)S(1)}, f32[8,128]{1,0:T(8,128)S(1)}) custom-call(f32[20,200,128]{2,1,0:T(8,128)S(1)} %get-tuple-element.37.g_ref, bf16[5,64,128]{2,1,0:T(8,128)(2,1)S(1)} %collective-permute-done.1.inner_ref, bf16[5,64,128]{2,1,0:T(8,128)(2,1)S(1)} %collective-permute-done.2.outer_ref, ...), custom_call_target="tpu_custom_call" | custom-call | flops 1000000 | bytes 100000 | tf_op jit(solution)/shard_map/pallas_call | solution.py:19
  15.7 1.9 %collective-permute-start.3 = (f32[8,128]{1,0:T(8,128)S(1)}, f32[8,128]{1,0:T(8,128)S(1)}, u32[]{:S(2)}, u32[]{:S(2)}) collective-permute-start(f32[8,128]{1,0:T(8,128)S(1)} %get-tuple-element.42.own_ref), channel_id=1, source_target_pairs={{16,32},{48,64},{80,96},{112,128},{144,160},{176,192},{208,224},{2... | collective-permute-start | bytes 12296 | tf_op jit(solution)/shard_map/ppermute | solution.py:414
  17.7 4.3 %all-gather.1 = f32[16,128]{1,0:T(8,128)S(1)} all-gather(f32[8,128]{1,0:T(8,128)S(1)} %get-tuple-element.42.own_ref), channel_id=3, replica_groups={{0,16},{32,48},{64,80},{96,112},{128,144},{160,176},{192,208},{224,240}..., dimensions={0}, use_global_device_ids=true | all-gather | bytes 12288 | tf_op jit(solution)/shard_map/all_gather | solution.py:419
  22.0 0.6 %shard_map.96 = bf16[16,8,128]{2,1,0:T(8,128)(2,1)} custom-call(f32[2,8,128]{2,1,0:T(8,128)S(1)} %bitcast.9, f32[8,128]{1,0:T(8,128)S(1)} %get-tuple-element.42.own_ref, f32[8,128]{1,0:T(8,128)S(1)} %collective-permute-done.3.outer_ref), custom_call_target="tpu_custom_call" | custom-call | flops 1000000 | bytes 100000 | tf_op jit(solution)/shard_map/pallas_call | solution.py:19
  22.6 11.5 %all-to-all-start = ((bf16[16,8,128]{2,1,0:T(8,128)(2,1)}), bf16[16,8,128]{2,1,0:T(8,128)(2,1)S(1)}, u32[]{:S(2)}, u32[]{:S(2)}) async-start(bf16[16,8,128]{2,1,0:T(8,128)(2,1)} %shard_map.96), calls=%async_computation | async-start | bytes 65536 | tf_op jit(solution)/shard_map/all_to_all | solution.py:483
  34.2 0.4 shard_map.97
  34.5 7.2 %all-to-all-done.p_ref = bf16[16,8,128]{2,1,0:T(8,128)(2,1)S(1)} async-done(((bf16[16,8,128]{2,1,0:T(8,128)(2,1)}), bf16[16,8,128]{2,1,0:T(8,128)(2,1)S(1)}, u32[]{:S(2)}, u32[]{:S(2)}) %all-to-all-start) | async-done | bytes 32800 | tf_op jit(solution)/shard_map/all_to_all | solution.py:483
  41.8 1.0 %shard_map.98 = bf16[16,16,128]{2,1,0:T(8,128)(2,1)} custom-call(bf16[16,8,128]{2,1,0:T(8,128)(2,1)S(1)} %all-to-all-done.p_ref, bf16[64,1152]{1,0:T(8,128)(2,1)S(1)} %get-tuple-element.46.vt_ref, f32[1,64]{1,0:T(1,128)S(1)} %get-tuple-element.47.bb_ref, bf16[64,128]{1,0:T(8,128)(2,1)S(1)} %get-tuple-element.48.ow_ref), custom_call_target="tpu_custom_call" | custom-call | flops 1000000 | bytes 100000 | tf_op jit(solution)/shard_map/pallas_call | solution.py:19
  42.8 3.5 %all-to-all-start.1 = ((bf16[16,16,128]{2,1,0:T(8,128)(2,1)}), bf16[16,16,128]{2,1,0:T(8,128)(2,1)S(1)}, u32[]{:S(2)}, u32[]{:S(2)}) async-start(bf16[16,16,128]{2,1,0:T(8,128)(2,1)} %shard_map.98), calls=%async_computation.1 | async-start | bytes 131072 | tf_op jit(solution)/shard_map/all_to_all | solution.py:485
  46.3 1.2 %shard_map.99 = (bf16[192,576]{1,0:T(8,128)(2,1)S(1)}, f32[64,128]{1,0:T(8,128)S(1)}, bf16[256,1152]{1,0:T(8,128)(2,1)S(1)}) custom-call(bf16[27,64,64]{2,1,0:T(8,128)(2,1)} %bitcast.12, f32[1,64]{1,0:T(1,128)} %bitcast.14), custom_call_target="tpu_custom_call" | custom-call | flops 100000000 | bytes 100000 | tf_op jit(solution)/shard_map/pallas_call | solution.py:19
  47.5 2.4 %shard_map.100.d_ref = f32[16,64,128]{2,1,0:T(8,128)S(1)} custom-call(bf16[5,64,128]{2,1,0:T(8,128)(2,1)S(1)} %get-tuple-element.51.fl_ref, bf16[5,64,128]{2,1,0:T(8,128)(2,1)S(1)} %get-tuple-element.52.fr_ref, bf16[5,64,128]{2,1,0:T(8,128)(2,1)S(1)} %collective-permute-done.1.inner_ref, bf16[5,64,128]{2,1,0:T(8,128)(2,1)S(1)} %collective-permute-done.2.outer_ref, ...), custom_call_target="tpu_custom_call" | custom-call | flops 400000000 | bytes 100000 | tf_op jit(solution)/shard_map/pallas_call | solution.py:19
  49.8 4.0 %all-to-all-done.1.parts_ref = bf16[16,16,128]{2,1,0:T(8,128)(2,1)S(1)} async-done(((bf16[16,16,128]{2,1,0:T(8,128)(2,1)}), bf16[16,16,128]{2,1,0:T(8,128)(2,1)S(1)}, u32[]{:S(2)}, u32[]{:S(2)}) %all-to-all-start.1) | async-done | bytes 65568 | tf_op jit(solution)/shard_map/all_to_all | solution.py:485
  53.9 1.5 %shard_map.101 = bf16[64,16,128]{2,1,0:T(8,128)(2,1)} custom-call(bf16[16,16,128]{2,1,0:T(8,128)(2,1)S(1)} %all-to-all-done.1.parts_ref, bf16[256,1152]{1,0:T(8,128)(2,1)S(1)} %get-tuple-element.49.s_ref, bf16[192,576]{1,0:T(8,128)(2,1)S(1)} %get-tuple-element.50.w_ref, f32[16,64,128]{2,1,0:T(8,128)S(1)} %shard_map.100.d_ref), custom_call_target="tpu_custom_call" | custom-call | flops 1000000 | bytes 100000 | tf_op jit(solution)/shard_map/pallas_call | solution.py:19
  (3 shorter events, 0.0 us)
Async XLA Ops:
  1.1 6.7 %collective-permute-start = (bf16[2,64,128]{2,1,0:T(8,128)(2,1)S(1)}, bf16[2,64,128]{2,1,0:T(8,128)(2,1)S(1)}, u32[]{:S(2)}, u32[]{:S(2)}) collective-permute-start(bf16[2,64,128]{2,1,0:T(8,128)(2,1)S(1)} %get-tuple-element.32), channel_id=1, source_target_pairs={{16,32},{48,64},{80,96},{112,128},{144,160},{176,192},{208,224},{2... | collective-permute-start | bytes 98312 | tf_op jit(solution)/shard_map/ppermute | solution.py:414
  8.0 6.6 %collective-permute-start.1 = (bf16[5,64,128]{2,1,0:T(8,128)(2,1)S(1)}, bf16[5,64,128]{2,1,0:T(8,128)(2,1)S(1)}, u32[]{:S(2)}, u32[]{:S(2)}) collective-permute-start(bf16[5,64,128]{2,1,0:T(8,128)(2,1)S(1)} %get-tuple-element.38), channel_id=1, source_target_pairs={{0,1},{2,3},{4,5},{6,7},{8,9},{10,11},{12,13},{14,15},{1,0},{3,2},... | collective-permute-start | bytes 245768 | tf_op jit(solution)/shard_map/ppermute | solution.py:414
  11.5 3.1 %collective-permute-start.2 = (bf16[5,64,128]{2,1,0:T(8,128)(2,1)S(1)}, bf16[5,64,128]{2,1,0:T(8,128)(2,1)S(1)}, u32[]{:S(2)}, u32[]{:S(2)}) collective-permute-start(bf16[5,64,128]{2,1,0:T(8,128)(2,1)S(1)} %get-tuple-element.39), channel_id=1, source_target_pairs={{1,2},{3,4},{5,6},{7,8},{9,10},{11,12},{13,14},{2,1},{4,3},{6,5},{... | collective-permute-start | bytes 245768 | tf_op jit(solution)/shard_map/ppermute | solution.py:414
  12.4 21.8 %copy-start = (bf16[3,3,3,32,512]{4,3,2,1,0:T(8,128)(2,1)S(1)}, bf16[3,3,3,32,512]{4,3,2,1,0:T(8,128)(2,1)}, u32[]{:S(2)}) copy-start(bf16[3,3,3,32,512]{4,3,2,1,0:T(8,128)(2,1)} %param.13) | copy-start | bytes 2654212
  15.7 6.3 %collective-permute-start.3 = (f32[8,128]{1,0:T(8,128)S(1)}, f32[8,128]{1,0:T(8,128)S(1)}, u32[]{:S(2)}, u32[]{:S(2)}) collective-permute-start(f32[8,128]{1,0:T(8,128)S(1)} %get-tuple-element.42.own_ref), channel_id=1, source_target_pairs={{16,32},{48,64},{80,96},{112,128},{144,160},{176,192},{208,224},{2... | collective-permute-start | bytes 12296 | tf_op jit(solution)/shard_map/ppermute | solution.py:414
  22.6 19.2 %all-to-all-start = ((bf16[16,8,128]{2,1,0:T(8,128)(2,1)}), bf16[16,8,128]{2,1,0:T(8,128)(2,1)S(1)}, u32[]{:S(2)}, u32[]{:S(2)}) async-start(bf16[16,8,128]{2,1,0:T(8,128)(2,1)} %shard_map.96), calls=%async_computation | async-start | bytes 65536 | tf_op jit(solution)/shard_map/all_to_all | solution.py:483
  42.8 11.1 %all-to-all-start.1 = ((bf16[16,16,128]{2,1,0:T(8,128)(2,1)}), bf16[16,16,128]{2,1,0:T(8,128)(2,1)S(1)}, u32[]{:S(2)}, u32[]{:S(2)}) async-start(bf16[16,16,128]{2,1,0:T(8,128)(2,1)} %shard_map.98), calls=%async_computation.1 | async-start | bytes 131072 | tf_op jit(solution)/shard_map/all_to_all | solution.py:485

commit v9 on v8

--- a/solution.py
+++ b/solution.py
@@ -59,8 +59,10 @@
     return copies
 
 
-def k_features(x_ref, ew_hbm, eb_hbm, ft_ref, inner_ref, outer_ref, ew_ref, eb_ref, held, buf, sem):
-    copies = fetches((x_ref, ew_hbm, eb_hbm), (held, ew_ref, eb_ref), sem)
+def k_features(*refs):
+    x_ref, sources, (ft_ref, inner_ref, outer_ref), targets = refs[0], refs[1:6], refs[6:9], refs[9:14]
+    held, buf, sem = refs[14:]
+    copies = fetches((x_ref, *sources), (held, *targets), sem)
     even = even_of("sx")
     copies[0].wait()
     for c in range(C):
@@ -232,9 +234,7 @@
     return jnp.where(even_y, outer, inner), jnp.where(even_y, inner, outer)
 
 
-def k_interior(ft_ref, x_ref, w_ref, *refs):
-    sources, g_ref, targets, xm, sem = refs[:3], refs[3], refs[4:7], refs[7], refs[8]
-    copies = fetches(sources, targets, sem)
+def k_interior(ft_ref, x_ref, w_ref, g_ref, xm):
     lane = lanes_of(C)
     z = jnp.bitwise_and(lane, 15)
     for r in range(20):
@@ -244,8 +244,6 @@
             [jnp.where(lane < 16, zero, roll(v, 16)), v, jnp.where(lane >= 112, zero, roll(v, -16))], xm, r, z
         )
     products(w_ref, xm, 0, 20, into(g_ref))
-    for copy in copies:
-        copy.wait()
 
 
 def k_encode(g_ref, inner_ref, outer_ref, w_ref, bias_ref, em_ref, pool_ref):
@@ -420,15 +418,21 @@
 
 
 def per_device(features, enc_weight, enc_bias, proj_weight, bottle_weight, bottle_bias, out_weight, dec_weight, dec_bias):
-    first = (features, enc_weight.reshape(27, C, C), enc_bias.reshape(1, C))
-    deep = (proj_weight, out_weight, bottle_bias.reshape(1, 32))
+    first = (
+        features,
+        enc_weight.reshape(27, C, C),
+        enc_bias.reshape(1, C),
+        proj_weight,
+        out_weight,
+        bottle_bias.reshape(1, 32),
+    )
     last = (dec_weight.reshape(27, C, C), dec_bias.reshape(1, C))
-    ft, inner, outer, ew, eb = call(
+    ft, inner, outer, ew, eb, *deep = call(
         k_features,
         (S((18, C, 128), BF), S((2, C, 128), BF), S((2, C, 128), BF)) + tuple(S(v.shape, v.dtype) for v in first[1:]),
         *first,
-        scratch=[pltpu.VMEM((C, 16, 128), BF), pltpu.VMEM((C * STRIDE, 128), F32), pltpu.SemaphoreType.DMA((3,))],
-        hbm=range(3),
+        scratch=[pltpu.VMEM((C, 16, 128), BF), pltpu.VMEM((C * STRIDE, 128), F32), pltpu.SemaphoreType.DMA((6,))],
+        hbm=range(6),
     )
     outer, pair = swapped(outer, "sx", 1), paired(inner, "sx")
     we, wedge, be = call(
@@ -436,16 +440,14 @@
     )
     xh, fl, fr, inner, outer = call(k_faces, (S((4, C, 128), BF),) + (S((5, C, 128), BF),) * 4, pair, outer, ft)
     outer, inner = swapped(outer, "sy", 1), swapped(inner, "sy", 0)
-    product, *deep = call(
+    product = call(
         k_interior,
-        (S((20, 3 * C + 8, 128), F32),) + tuple(S(v.shape, v.dtype) for v in deep),
+        S((20, 3 * C + 8, 128), F32),
         ft,
         xh,
         we,
-        *deep,
-        scratch=[pltpu.VMEM((20, 9, C + 16, 128), BF), pltpu.SemaphoreType.DMA((3,))],
+        scratch=[pltpu.VMEM((20, 9, C + 16, 128), BF)],
         flops=4 * 10**8,
-        hbm=range(3, 6),
     )
     em, pooled = call(k_encode, (S((18, C, 128), BF), S((8, 128), F32)), product, inner, outer, wedge, be)
     p_outer, p_pair = swapped(pooled, "sx", 1), paired(pooled, "sx")

time: 55.8 us -> 55.8 us (level)
  transfers between devices with their start and end apart: 6 -> 6, of which waited for: 3 -> 3; matrix products, arithmetic and copies ran while one was open for 0% -> 0% of each run, Pallas kernels for 11% -> 10%
where the time goes in v9:
time: 55.8 us; the launch traced here: 55.4 us
  starting transfers between devices  23.1 us (41%)
  waiting for transfers between devices  11.8 us (21%)
  Pallas kernels  11.4 us (20%)
  blocking collectives  8.95 us (16%)
    all_to_all x1, starting transfers between devices, per_device(): everyone = lax.all_to_all(message, 'sy', 0, 0, tiled=True)  11.6 us
    pallas_call x11, Pallas kernels, call(): pl.pallas_call(kernel, out_shape=outs, in_specs=[pl.BlockSpec(memory_spac...  11.4 us
    all_gather x2, blocking collectives, paired(): return lax.all_gather(v, axis, axis_index_groups=pairs)  8.95 us
    ppermute x4, starting transfers between devices, swapped(): lax.ppermute(v, axis, [(i, i + 1) for i in low] + [(i + 1, i) for i in low])  8.02 us
    all_to_all x1, waiting for transfers between devices, per_device(): everyone = lax.all_to_all(message, 'sy', 0, 0, tiled=True)  7.22 us
    all_to_all x1, waiting for transfers between devices, per_device(): parts = lax.all_to_all(partial, 'sy', 0, 0, tiled=True)  4.02 us
    all_to_all x1, starting transfers between devices, per_device(): parts = lax.all_to_all(partial, 'sy', 0, 0, tiled=True)  3.5 us
  transfers between devices with their start and end apart: 6, of which 3 were waited for; matrix products, arithmetic and copies ran while one was open for 0% of the time, Pallas kernels for 10%

profile of v9, /device:TPU:96, one launch (start us, length us, event | category | flops | bytes accessed | tf_op | source)
XLA Modules:
  0.0 55.4 jit_solution(13184027828332260007)
XLA Ops:
  0.0 1.2 %shard_map.91 = (bf16[18,64,128]{2,1,0:T(8,128)(2,1)S(1)}, bf16[2,64,128]{2,1,0:T(8,128)(2,1)S(1)}, bf16[2,64,128]{2,1,0:T(8,128)(2,1)S(1)}, bf16[27,64,64]{2,1,...) custom-call(bf16[64,16,128]{2,1,0:T(8,128)(2,1)} %refs_0_.1, ...), custom_call_target="tpu_custom_call" | custom-call | flops 1000000 | bytes 100000 | tf_op jit(solution)/shard_map/pallas_call | solution.py:19
  1.2 1.9 %collective-permute-start = (bf16[2,64,128]{2,1,0:T(8,128)(2,1)S(1)}, bf16[2,64,128]{2,1,0:T(8,128)(2,1)S(1)}, u32[]{:S(2)}, u32[]{:S(2)}) collective-permute-start(bf16[2,64,128]{2,1,0:T(8,128)(2,1)S(1)} %get-tuple-element.31), channel_id=1, source_target_pairs={{16,32},{48,64},{80,96},{112,128},{144,160},{176,192},{208,224},{2... | collective-permute-start | bytes 98312 | tf_op jit(solution)/shard_map/ppermute | solution.py:412
  3.1 4.7 %all-gather = bf16[4,64,128]{2,1,0:T(8,128)(2,1)S(1)} all-gather(bf16[2,64,128]{2,1,0:T(8,128)(2,1)S(1)} %get-tuple-element.30), channel_id=2, replica_groups={{0,16},{32,48},{64,80},{96,112},{128,144},{160,176},{192,208},{224,240}..., dimensions={0}, use_global_device_ids=true | all-gather | bytes 98304 | tf_op jit(solution)/shard_map/all_gather | solution.py:417
  7.8 0.0 collective-permute-done.outer_ref
  7.8 0.2 shard_map.92
  8.0 3.5 %collective-permute-start.1 = (bf16[5,64,128]{2,1,0:T(8,128)(2,1)S(1)}, bf16[5,64,128]{2,1,0:T(8,128)(2,1)S(1)}, u32[]{:S(2)}, u32[]{:S(2)}) collective-permute-start(bf16[5,64,128]{2,1,0:T(8,128)(2,1)S(1)} %get-tuple-element.36), channel_id=1, source_target_pairs={{0,1},{2,3},{4,5},{6,7},{8,9},{10,11},{12,13},{14,15},{1,0},{3,2},... | collective-permute-start | bytes 245768 | tf_op jit(solution)/shard_map/ppermute | solution.py:412
  11.5 0.7 %collective-permute-start.2 = (bf16[5,64,128]{2,1,0:T(8,128)(2,1)S(1)}, bf16[5,64,128]{2,1,0:T(8,128)(2,1)S(1)}, u32[]{:S(2)}, u32[]{:S(2)}) collective-permute-start(bf16[5,64,128]{2,1,0:T(8,128)(2,1)S(1)} %get-tuple-element.37), channel_id=1, source_target_pairs={{1,2},{3,4},{5,6},{7,8},{9,10},{11,12},{13,14},{2,1},{4,3},{6,5},{... | collective-permute-start | bytes 245768 | tf_op jit(solution)/shard_map/ppermute | solution.py:412
  12.2 0.2 shard_map.93
  12.4 0.0 copy-start
  12.4 1.6 %shard_map.94.g_ref = f32[20,200,128]{2,1,0:T(8,128)S(1)} custom-call(bf16[18,64,128]{2,1,0:T(8,128)(2,1)S(1)} %get-tuple-element.29.ft_ref, bf16[4,64,128]{2,1,0:T(8,128)(2,1)S(1)} %get-tuple-element.32.x_ref, bf16[192,576]{1,0:T(8,128)(2,1)S(1)} %get-tuple-element.35.w_ref.we_ref), custom_call_target="tpu_custom_call" | custom-call | flops 400000000 | bytes 100000 | tf_op jit(solution)/shard_map/pallas_call | solution.py:19
  14.0 0.6 %collective-permute-done.1.inner_ref = bf16[5,64,128]{2,1,0:T(8,128)(2,1)S(1)} collective-permute-done((bf16[5,64,128]{2,1,0:T(8,128)(2,1)S(1)}, bf16[5,64,128]{2,1,0:T(8,128)(2,1)S(1)}, u32[]{:S(2)}, u32[]{:S(2)}) %collective-permute-start.1) | collective-permute-done | bytes 81952 | tf_op jit(solution)/shard_map/ppermute | solution.py:412
  14.6 1.1 %shard_map.95 = (bf16[18,64,128]{2,1,0:T(8,128)(2,1)S(1)}, f32[8,128]{1,0:T(8,128)S(1)}) custom-call(f32[20,200,128]{2,1,0:T(8,128)S(1)} %shard_map.94.g_ref, bf16[5,64,128]{2,1,0:T(8,128)(2,1)S(1)} %collective-permute-done.1.inner_ref, bf16[5,64,128]{2,1,0:T(8,128)(2,1)S(1)} %collective-permute-done.2.outer_ref, ...), custom_call_target="tpu_custom_call" | custom-call | flops 1000000 | bytes 100000 | tf_op jit(solution)/shard_map/pallas_call | solution.py:19
  15.7 1.9 %collective-permute-start.3 = (f32[8,128]{1,0:T(8,128)S(1)}, f32[8,128]{1,0:T(8,128)S(1)}, u32[]{:S(2)}, u32[]{:S(2)}) collective-permute-start(f32[8,128]{1,0:T(8,128)S(1)} %get-tuple-element.40.own_ref), channel_id=1, source_target_pairs={{16,32},{48,64},{80,96},{112,128},{144,160},{176,192},{208,224},{2... | collective-permute-start | bytes 12296 | tf_op jit(solution)/shard_map/ppermute | solution.py:412
  17.7 4.2 %all-gather.1 = f32[16,128]{1,0:T(8,128)S(1)} all-gather(f32[8,128]{1,0:T(8,128)S(1)} %get-tuple-element.40.own_ref), channel_id=3, replica_groups={{0,16},{32,48},{64,80},{96,112},{128,144},{160,176},{192,208},{224,240}..., dimensions={0}, use_global_device_ids=true | all-gather | bytes 12288 | tf_op jit(solution)/shard_map/all_gather | solution.py:417
  21.9 0.6 %shard_map.96 = bf16[16,8,128]{2,1,0:T(8,128)(2,1)} custom-call(f32[2,8,128]{2,1,0:T(8,128)S(1)} %bitcast.9, f32[8,128]{1,0:T(8,128)S(1)} %get-tuple-element.40.own_ref, f32[8,128]{1,0:T(8,128)S(1)} %collective-permute-done.3.outer_ref), custom_call_target="tpu_custom_call" | custom-call | flops 1000000 | bytes 100000 | tf_op jit(solution)/shard_map/pallas_call | solution.py:19
  22.6 11.6 %all-to-all-start = ((bf16[16,8,128]{2,1,0:T(8,128)(2,1)}), bf16[16,8,128]{2,1,0:T(8,128)(2,1)S(1)}, u32[]{:S(2)}, u32[]{:S(2)}) async-start(bf16[16,8,128]{2,1,0:T(8,128)(2,1)} %shard_map.96), calls=%async_computation | async-start | bytes 65536 | tf_op jit(solution)/shard_map/all_to_all | solution.py:485
  34.2 0.4 shard_map.97
  34.6 7.2 %all-to-all-done.p_ref = bf16[16,8,128]{2,1,0:T(8,128)(2,1)S(1)} async-done(((bf16[16,8,128]{2,1,0:T(8,128)(2,1)}), bf16[16,8,128]{2,1,0:T(8,128)(2,1)S(1)}, u32[]{:S(2)}, u32[]{:S(2)}) %all-to-all-start) | async-done | bytes 32800 | tf_op jit(solution)/shard_map/all_to_all | solution.py:485
  41.8 1.0 %shard_map.98 = bf16[16,16,128]{2,1,0:T(8,128)(2,1)} custom-call(bf16[16,8,128]{2,1,0:T(8,128)(2,1)S(1)} %all-to-all-done.p_ref, bf16[64,1152]{1,0:T(8,128)(2,1)S(1)} %get-tuple-element.44.vt_ref, f32[1,64]{1,0:T(1,128)S(1)} %get-tuple-element.45.bb_ref, bf16[64,128]{1,0:T(8,128)(2,1)S(1)} %get-tuple-element.46.ow_ref), custom_call_target="tpu_custom_call" | custom-call | flops 1000000 | bytes 100000 | tf_op jit(solution)/shard_map/pallas_call | solution.py:19
  42.8 3.5 %all-to-all-start.1 = ((bf16[16,16,128]{2,1,0:T(8,128)(2,1)}), bf16[16,16,128]{2,1,0:T(8,128)(2,1)S(1)}, u32[]{:S(2)}, u32[]{:S(2)}) async-start(bf16[16,16,128]{2,1,0:T(8,128)(2,1)} %shard_map.98), calls=%async_computation.1 | async-start | bytes 131072 | tf_op jit(solution)/shard_map/all_to_all | solution.py:487
  46.3 1.2 %shard_map.99 = (bf16[192,576]{1,0:T(8,128)(2,1)S(1)}, f32[64,128]{1,0:T(8,128)S(1)}, bf16[256,1152]{1,0:T(8,128)(2,1)S(1)}) custom-call(bf16[27,64,64]{2,1,0:T(8,128)(2,1)} %bitcast.12, f32[1,64]{1,0:T(1,128)} %bitcast.15), custom_call_target="tpu_custom_call" | custom-call | flops 100000000 | bytes 100000 | tf_op jit(solution)/shard_map/pallas_call | solution.py:19
  47.5 2.4 %shard_map.100.d_ref = f32[16,64,128]{2,1,0:T(8,128)S(1)} custom-call(bf16[5,64,128]{2,1,0:T(8,128)(2,1)S(1)} %get-tuple-element.49.fl_ref, bf16[5,64,128]{2,1,0:T(8,128)(2,1)S(1)} %get-tuple-element.50.fr_ref, bf16[5,64,128]{2,1,0:T(8,128)(2,1)S(1)} %collective-permute-done.1.inner_ref, bf16[5,64,128]{2,1,0:T(8,128)(2,1)S(1)} %collective-permute-done.2.outer_ref, ...), custom_call_target="tpu_custom_call" | custom-call | flops 400000000 | bytes 100000 | tf_op jit(solution)/shard_map/pallas_call | solution.py:19
  49.9 4.0 %all-to-all-done.1.parts_ref = bf16[16,16,128]{2,1,0:T(8,128)(2,1)S(1)} async-done(((bf16[16,16,128]{2,1,0:T(8,128)(2,1)}), bf16[16,16,128]{2,1,0:T(8,128)(2,1)S(1)}, u32[]{:S(2)}, u32[]{:S(2)}) %all-to-all-start.1) | async-done | bytes 65568 | tf_op jit(solution)/shard_map/all_to_all | solution.py:487
  53.9 1.5 %shard_map.101 = bf16[64,16,128]{2,1,0:T(8,128)(2,1)} custom-call(bf16[16,16,128]{2,1,0:T(8,128)(2,1)S(1)} %all-to-all-done.1.parts_ref, bf16[256,1152]{1,0:T(8,128)(2,1)S(1)} %get-tuple-element.47.s_ref, bf16[192,576]{1,0:T(8,128)(2,1)S(1)} %get-tuple-element.48.w_ref, f32[16,64,128]{2,1,0:T(8,128)S(1)} %shard_map.100.d_ref), custom_call_target="tpu_custom_call" | custom-call | flops 1000000 | bytes 100000 | tf_op jit(solution)/shard_map/pallas_call | solution.py:19
  (3 shorter events, 0.0 us)
Async XLA Ops:
  1.2 6.7 %collective-permute-start = (bf16[2,64,128]{2,1,0:T(8,128)(2,1)S(1)}, bf16[2,64,128]{2,1,0:T(8,128)(2,1)S(1)}, u32[]{:S(2)}, u32[]{:S(2)}) collective-permute-start(bf16[2,64,128]{2,1,0:T(8,128)(2,1)S(1)} %get-tuple-element.31), channel_id=1, source_target_pairs={{16,32},{48,64},{80,96},{112,128},{144,160},{176,192},{208,224},{2... | collective-permute-start | bytes 98312 | tf_op jit(solution)/shard_map/ppermute | solution.py:412
  8.0 6.6 %collective-permute-start.1 = (bf16[5,64,128]{2,1,0:T(8,128)(2,1)S(1)}, bf16[5,64,128]{2,1,0:T(8,128)(2,1)S(1)}, u32[]{:S(2)}, u32[]{:S(2)}) collective-permute-start(bf16[5,64,128]{2,1,0:T(8,128)(2,1)S(1)} %get-tuple-element.36), channel_id=1, source_target_pairs={{0,1},{2,3},{4,5},{6,7},{8,9},{10,11},{12,13},{14,15},{1,0},{3,2},... | collective-permute-start | bytes 245768 | tf_op jit(solution)/shard_map/ppermute | solution.py:412
  11.5 3.1 %collective-permute-start.2 = (bf16[5,64,128]{2,1,0:T(8,128)(2,1)S(1)}, bf16[5,64,128]{2,1,0:T(8,128)(2,1)S(1)}, u32[]{:S(2)}, u32[]{:S(2)}) collective-permute-start(bf16[5,64,128]{2,1,0:T(8,128)(2,1)S(1)} %get-tuple-element.37), channel_id=1, source_target_pairs={{1,2},{3,4},{5,6},{7,8},{9,10},{11,12},{13,14},{2,1},{4,3},{6,5},{... | collective-permute-start | bytes 245768 | tf_op jit(solution)/shard_map/ppermute | solution.py:412
  12.4 21.8 %copy-start = (bf16[3,3,3,32,512]{4,3,2,1,0:T(8,128)(2,1)S(1)}, bf16[3,3,3,32,512]{4,3,2,1,0:T(8,128)(2,1)}, u32[]{:S(2)}) copy-start(bf16[3,3,3,32,512]{4,3,2,1,0:T(8,128)(2,1)} %param.13) | copy-start | bytes 2654212
  15.7 6.2 %collective-permute-start.3 = (f32[8,128]{1,0:T(8,128)S(1)}, f32[8,128]{1,0:T(8,128)S(1)}, u32[]{:S(2)}, u32[]{:S(2)}) collective-permute-start(f32[8,128]{1,0:T(8,128)S(1)} %get-tuple-element.40.own_ref), channel_id=1, source_target_pairs={{16,32},{48,64},{80,96},{112,128},{144,160},{176,192},{208,224},{2... | collective-permute-start | bytes 12296 | tf_op jit(solution)/shard_map/ppermute | solution.py:412
  22.6 19.2 %all-to-all-start = ((bf16[16,8,128]{2,1,0:T(8,128)(2,1)}), bf16[16,8,128]{2,1,0:T(8,128)(2,1)S(1)}, u32[]{:S(2)}, u32[]{:S(2)}) async-start(bf16[16,8,128]{2,1,0:T(8,128)(2,1)} %shard_map.96), calls=%async_computation | async-start | bytes 65536 | tf_op jit(solution)/shard_map/all_to_all | solution.py:485
  42.8 11.1 %all-to-all-start.1 = ((bf16[16,16,128]{2,1,0:T(8,128)(2,1)}), bf16[16,16,128]{2,1,0:T(8,128)(2,1)S(1)}, u32[]{:S(2)}, u32[]{:S(2)}) async-start(bf16[16,16,128]{2,1,0:T(8,128)(2,1)} %shard_map.98), calls=%async_computation.1 | async-start | bytes 131072 | tf_op jit(solution)/shard_map/all_to_all | solution.py:487
